TPU v7x, 8 devices: a whole 2x2x1 slice. The times are simulated.
8 devices in a mesh: dp: 1 (over z), yz: 2 (over y), x: 4 (over x, core).
Axes of the slice: x: 2, y: 2, z: 1, core: 2. Of those that a mesh axis runs over, the one named last changes fastest.
Arguments:
- x_in: bfloat16 [128, 6144], P('dp', ('x', 'yz'))
- ln_gain: bfloat16 [6144], P(('x', 'yz'))
- w_qkv: bfloat16 [6144, 6400], P('x', 'yz')
- w_gate: bfloat16 [6144, 24576], P('x', 'yz')
- w_up: bfloat16 [6144, 24576], P('x', 'yz')
- w_attn_out: bfloat16 [6144, 6144], P('yz', 'x')
- w_mlp_out: bfloat16 [24576, 6144], P('yz', 'x')
- k_cache: bfloat16 [128, 4096, 128], P(('dp', 'x', 'yz'))
- v_cache: bfloat16 [128, 4096, 128], P(('dp', 'x', 'yz'))
- ctx_len: int32 [128], P(('dp', 'x', 'yz'))
Outputs:
- output 1: bfloat16 [128, 6144], P('dp', ('x', 'yz'))
- output 2: bfloat16 [128, 4096, 128], P(('dp', 'x', 'yz'))
- output 3: bfloat16 [128, 4096, 128], P(('dp', 'x', 'yz'))
All inputs are finite; a program needn't handle non-finite values.
Results may differ from a plain program's by a relative error of at most 0.00713931.
Values are sent between devices in bfloat16 or wider.
A program may use at most 1 GiB of HBM per device.

v0:
```python
import jax
import jax.numpy as jnp
from jax import lax
from jax.sharding import PartitionSpec as P


def apply_rope(vecs, positions):
    half_dim = vecs.shape[-1] // 2
    inv_freq = 10000.0 ** (-jnp.arange(half_dim, dtype=jnp.float32) / half_dim)
    angles = positions.astype(jnp.float32)[..., None] * inv_freq
    cos_t = jnp.cos(angles)
    sin_t = jnp.sin(angles)
    first_half = vecs[..., :half_dim]
    second_half = vecs[..., half_dim:]
    return jnp.concatenate([first_half * cos_t - second_half * sin_t, second_half * cos_t + first_half * sin_t], axis=-1)


def attend_local(q_rot, k_all, v_all, ctx_len):
    head_dim = q_rot.shape[-1]
    positions = jnp.arange(k_all.shape[1])
    scores = jnp.einsum("bhd,btd->bht", q_rot, k_all, preferred_element_type=jnp.float32) * head_dim ** -0.5
    visible = (positions[None, :] <= ctx_len[:, None])[:, None, :]
    scores = jnp.where(visible, scores, -1e30)
    attn_probs = jax.nn.softmax(scores, axis=-1).astype(jnp.bfloat16)
    return jnp.einsum("bht,btd->bhd", attn_probs, v_all, preferred_element_type=jnp.float32).astype(jnp.bfloat16)


def solution(mesh):
    x_size = mesh.shape["x"]
    yz_size = mesh.shape["yz"]
    both_axes = ("x", "yz")
    row_spec = P("dp", both_axes)
    in_w_spec = P("x", "yz")
    out_w_spec = P("yz", "x")
    cache_spec = P(("dp", "x", "yz"), None, None)
    len_spec = P(("dp", "x", "yz"))

    def local_layer(x_loc, gain_loc, wqkv_loc, wgate_loc, wup_loc, wao_loc, wmo_loc, kc_loc, vc_loc, len_loc):
        d_model = x_loc.shape[1] * x_size * yz_size
        head_dim = kc_loc.shape[2]
        dev_rows = kc_loc.shape[0]
        attn_cols = wao_loc.shape[0] * yz_size
        num_heads = attn_cols // head_dim
        x_f32 = x_loc.astype(jnp.float32)
        row_stats = jnp.stack([jnp.sum(x_f32, axis=1), jnp.sum(x_f32 * x_f32, axis=1)], axis=1)
        row_stats = lax.psum(row_stats, both_axes)
        row_mean = row_stats[:, 0:1] / d_model
        row_var = row_stats[:, 1:2] / d_model - row_mean * row_mean
        normed = ((x_f32 - row_mean) * lax.rsqrt(row_var + 1e-6) * gain_loc.astype(jnp.float32)).astype(jnp.bfloat16)
        normed_rows = lax.all_gather(normed, "yz", axis=1, tiled=True)
        qkv_part = jnp.dot(normed_rows, wqkv_loc, preferred_element_type=jnp.float32)
        gate_part = jnp.dot(normed_rows, wgate_loc, preferred_element_type=jnp.float32)
        up_part = jnp.dot(normed_rows, wup_loc, preferred_element_type=jnp.float32)
        qkv_rows = lax.psum_scatter(qkv_part, "x", scatter_dimension=0, tiled=True).astype(jnp.bfloat16)
        gate_rows = lax.psum_scatter(gate_part, "x", scatter_dimension=0, tiled=True).astype(jnp.bfloat16)
        up_rows = lax.psum_scatter(up_part, "x", scatter_dimension=0, tiled=True).astype(jnp.bfloat16)
        mlp_rows = (jax.nn.silu(gate_rows.astype(jnp.float32)) * up_rows.astype(jnp.float32)).astype(jnp.bfloat16)
        qkv_dev = lax.all_to_all(qkv_rows, "yz", 0, 1, tiled=True)
        q_heads = qkv_dev[:, :attn_cols].reshape(dev_rows, num_heads, head_dim)
        k_new = qkv_dev[:, attn_cols:attn_cols + head_dim]
        v_new = qkv_dev[:, attn_cols + head_dim:]
        q_rot = apply_rope(q_heads.astype(jnp.float32), len_loc[:, None]).astype(jnp.bfloat16)
        k_rot = apply_rope(k_new.astype(jnp.float32), len_loc).astype(jnp.bfloat16)
        new_slot = (jnp.arange(kc_loc.shape[1])[None, :] == len_loc[:, None])[:, :, None]
        k_all = jnp.where(new_slot, k_rot[:, None, :], kc_loc)
        v_all = jnp.where(new_slot, v_new[:, None, :], vc_loc)
        attn_dev = attend_local(q_rot, k_all, v_all, len_loc).reshape(dev_rows, attn_cols)
        attn_rows = lax.all_to_all(attn_dev, "yz", 1, 0, tiled=True)
        attn_full = lax.all_gather(attn_rows, "x", axis=0, tiled=True)
        mlp_full = lax.all_gather(mlp_rows, "x", axis=0, tiled=True)
        z_part = jnp.dot(attn_full, wao_loc, preferred_element_type=jnp.float32) + jnp.dot(mlp_full, wmo_loc, preferred_element_type=jnp.float32)
        z_loc = lax.psum_scatter(z_part, "yz", scatter_dimension=1, tiled=True)
        y_loc = (x_f32 + z_loc).astype(jnp.bfloat16)
        return y_loc, k_all, v_all

    in_specs = (row_spec, P(both_axes), in_w_spec, in_w_spec, in_w_spec, out_w_spec, out_w_spec, cache_spec, cache_spec, len_spec)
    out_specs = (row_spec, cache_spec, cache_spec)
    return jax.shard_map(local_layer, mesh=mesh, in_specs=in_specs, out_specs=out_specs, check_vma=False)
```

profile of v0, /device:TPU:0, one launch (start us, length us, event | category | flops | bytes accessed | tf_op | source)
XLA Modules:
  0.0 273.3 jit_solution(11108905730566903433)
XLA Ops:
  7.2 0.0 reduce-scatter.5.cloned.1.call-start
  7.2 0.7 convert_element_type.57
  7.9 1.1 convert_reduce_fusion
  9.0 25.1 %psum.7 = f32[128,2]{0,1:T(2,128)S(1)} all-reduce(f32[128,2]{0,1:T(2,128)S(1)} %pad_maximum_fusion.1), channel_id=1, replica_groups=mesh['dp'=1,'yz'=2,'x'=4] {'x','yz'}, use_global_device_ids=true, to_apply=%region_2.0 | all-reduce | flops 256 | bytes 2048 | tf_op jit(solution)/shard_map/psum | solution.py:46
  34.1 1.1 fusion.15
  35.2 6.6 %all_gather.9 = bf16[128,1536]{1,0:T(8,128)(2,1)S(1)} all-gather(bf16[128,768]{1,0:T(8,128)(2,1)S(1)} %fusion.15), channel_id=1, replica_groups=mesh['dp'=1,'yz'=2,'x'=4] {'yz'}, dimensions={1}, use_global_device_ids=true | all-gather | bytes 589824 | tf_op jit(solution)/shard_map/all_gather | solution.py:50
  41.7 6.5 %fusion.26 = f32[128,3200]{1,0:T(8,128)} fusion(bf16[128,1536]{1,0:T(8,128)(2,1)S(1)} %all_gather.9, bf16[1536,3200]{1,0:T(8,128)(2,1)} %param.12), kind=kOutput, calls=%fused_computation.53 | convolution fusion | flops 1258291200 | bytes 11862016 | tf_op jit(solution)/shard_map/dot_general | solution.py:51
  48.2 0.0 reduce-scatter.5.cloned.1.call-update
  48.2 0.0 reduce-scatter.9.cloned.1.call-start
  48.3 17.2 %fusion.29 = f32[128,12288]{1,0:T(8,128)} fusion(bf16[128,1536]{1,0:T(8,128)(2,1)S(1)} %all_gather.9, bf16[1536,12288]{1,0:T(8,128)(2,1)} %param.14), kind=kOutput, calls=%fused_computation.56 | convolution fusion | flops 4831838208 | bytes 44433408 | tf_op jit(solution)/shard_map/dot_general | solution.py:53
  65.5 0.0 reduce-scatter.9.cloned.1.call-update
  65.5 0.0 copy-start.1
  65.5 0.0 reduce-scatter.7.cloned.1.call-start
  65.6 17.2 %fusion.28 = f32[128,12288]{1,0:T(8,128)} fusion(bf16[128,1536]{1,0:T(8,128)(2,1)S(1)} %all_gather.9, bf16[1536,12288]{1,0:T(8,128)(2,1)} %param.13), kind=kOutput, calls=%fused_computation.55 | convolution fusion | flops 4831838208 | bytes 44433408 | tf_op jit(solution)/shard_map/dot_general | solution.py:52
  82.7 0.0 reduce-scatter.7.cloned.1.call-update
  82.7 0.0 copy-done.1
  82.8 0.1 iota_compare_fusion.1
  82.9 0.0 reduce-scatter.5.cloned.1.call-done
  82.9 1.7 convert_element_type.59
  84.6 3.4 %all-to-all-start = ((bf16[2,16,3200]{2,1,0:T(8,128)(2,1)}), bf16[2,16,3200]{2,1,0:T(8,128)(2,1)S(1)}, u32[]{:S(2)}, u32[]{:S(2)}) async-start(bf16[2,16,3200]{2,1,0:T(8,128)(2,1)} %bitcast.4), calls=%async_computation.1 | async-start | bytes 409600 | tf_op jit(solution)/shard_map/all_to_all | solution.py:58
  88.1 0.0 all-gather.2.cloned.1.call-start
  88.1 4.6 %all-to-all-done = bf16[2,16,3200]{2,1,0:T(8,128)(2,1)S(1)} async-done(((bf16[2,16,3200]{2,1,0:T(8,128)(2,1)}), bf16[2,16,3200]{2,1,0:T(8,128)(2,1)S(1)}, u32[]{:S(2)}, u32[]{:S(2)}) %all-to-all-start) | async-done | bytes 204832 | tf_op jit(solution)/shard_map/all_to_all | solution.py:58
  92.8 0.1 copy.18
  92.9 0.1 multiply_cosine_fusion
  93.0 0.1 pad_maximum_fusion
  93.1 0.2 subtract_convert_fusion
  93.3 23.3 %broadcast_select_fusion.1 = (bf16[16,4096,128]{2,1,0:T(8,128)(2,1)}, bf16[16,4096,128]{2,1,0:T(8,128)(2,1)}) fusion(bf16[16,4096,128]{2,1,0:T(8,128)(2,1)} %param.17, pred[16,4096]{1,0:T(8,128)(4,1)S(1)} %get-tuple-element.20, bf16[16,128]{1,0:T(8,128)(2,1)S(1)} %pad_maximum_fusion, bf16[16,4096,128]{2,1,0:T(8,128)(2,1)} %param.18, ...), kind=kLoop, calls=%fused_computation.2 | loop fusion | flops 16777216 | bytes 67182592 | tf_op jit(solution)/shard_map/jit(_where)/select_n | solution.py:65
  116.6 12.1 %fusion.17 = f32[16,48,4096]{2,1,0:T(8,128)} fusion(bf16[16,4096,128]{2,1,0:T(8,128)(2,1)} %get-tuple-element.9, bf16[16,48,64]{2,1,0:T(8,128)(2,1)S(1)} %get-tuple-element.6, bf16[16,48,64]{2,1,0:T(8,128)(2,1)S(1)} %get-tuple-element.5), kind=kOutput, calls=%fused_computation.34 | convolution fusion | flops 805699584 | bytes 29556736 | tf_op jit(solution)/shard_map/bhd,btd->bht/dot_general | solution.py:21
  128.7 0.0 reduce-scatter.9.cloned.1.call-done
  128.7 50.8 %reduce-scatter.7.cloned.1.call-done = f32[32,12288]{1,0:T(8,128)} async-done(((f32[128,12288]{1,0:T(8,128)}), f32[32,12288]{1,0:T(8,128)}) %reduce-scatter.7.cloned.1.call-update) | async-done | bytes 1572880 | tf_op jit(solution)/shard_map/reduce_scatter | solution.py:55
  179.6 3.2 %fusion.10 = bf16[32,12288]{1,0:T(8,128)(2,1)} fusion(f32[32,12288]{1,0:T(8,128)} %reduce-scatter.9.cloned.1.call-done, f32[32,12288]{1,0:T(8,128)} %reduce-scatter.7.cloned.1.call-done), kind=kLoop, calls=%fused_computation.18 | loop fusion | flops 3932160 | bytes 3932160 | tf_op jit(solution)/shard_map/convert_element_type | solution.py:57
  182.7 0.0 all-gather.2.cloned.1.call-update
  182.8 0.2 reduce-scatter.11.cloned.1.call-start
  183.0 16.2 %fusion.25 = (f32[16,48]{1,0:T(8,128)S(1)}, f32[16,48,4096]{2,1,0:T(8,128)}) fusion(f32[16,48,4096]{2,1,0:T(8,128)} %fusion.17, pred[16,4096]{1,0:T(8,128)(4,1)S(1)} %get-tuple-element.19), kind=kOutput, calls=%fused_computation.52 | output fusion | flops 18878464 | bytes 25234432 | tf_op jit(solution)/shard_map/sub | solution.py:24
  199.2 12.2 %fusion.11 = bf16[16,48,128]{2,1,0:T(8,128)(2,1)S(1)} fusion(bf16[16,4096,128]{2,1,0:T(8,128)(2,1)} %get-tuple-element.10, f32[16,48,4096]{2,1,0:T(8,128)} %get-tuple-element.22, f32[16,48]{1,0:T(8,128)S(1)} %get-tuple-element.21), kind=kOutput, calls=%fused_computation.19 | convolution fusion | flops 811696128 | bytes 29559808 | tf_op jit(solution)/shard_map/bht,btd->bhd/dot_general | solution.py:25
  211.3 0.1 all_to_all.32
  211.4 7.4 %all_to_all.38 = bf16[16,2,3072]{2,0,1:T(8,128)(2,1)S(1)} all-to-all(bf16[16,2,3072]{2,0,1:T(8,128)(2,1)S(1)} %copy.16), channel_id=1, replica_groups=mesh['dp'=1,'yz'=2,'x'=4] {'yz'}, dimensions={1} | all-to-all | bytes 393216 | tf_op jit(solution)/shard_map/all_to_all | solution.py:68
  218.8 11.2 %all_gather.10 = bf16[128,3072]{1,0:T(8,128)(2,1)S(1)} all-gather(bf16[32,3072]{1,0:T(8,128)(2,1)S(1)} %bitcast.32), channel_id=1, replica_groups=mesh['dp'=1,'yz'=2,'x'=4] {'x'}, dimensions={0}, use_global_device_ids=true | all-gather | bytes 983040 | tf_op jit(solution)/shard_map/all_gather | solution.py:69
  230.0 5.1 %fusion.27 = f32[128,1536]{1,0:T(8,128)S(1)} fusion(bf16[128,3072]{1,0:T(8,128)(2,1)S(1)} %all_gather.10, bf16[3072,1536]{1,0:T(8,128)(2,1)} %param.15), kind=kOutput, calls=%fused_computation.54 | convolution fusion | flops 1207959552 | bytes 11010048 | tf_op jit(solution)/shard_map/dot_general | solution.py:71
  235.1 0.0 copy-start
  235.1 0.0 all-gather.2.cloned.1.call-done
  235.1 16.2 %convolution_add_fusion = f32[128,1536]{1,0:T(8,128)} fusion(f32[128,1536]{1,0:T(8,128)S(1)} %fusion.27, bf16[128,12288]{1,0:T(8,128)(2,1)} %all-gather.2.cloned.1.call-done, bf16[12288,1536]{1,0:T(8,128)(2,1)} %param.16), kind=kOutput, calls=%fused_computation.11 | convolution fusion | flops 4832034816 | bytes 42467328 | tf_op jit(solution)/shard_map/dot_general | solution.py:71
  251.3 0.0 reduce-scatter.11.cloned.1.call-update
  251.4 13.7 %reduce-scatter.11.cloned.1.call-done = f32[128,768]{1,0:T(8,128)} async-done(((f32[128,1536]{1,0:T(8,128)}), f32[128,768]{1,0:T(8,128)}) %reduce-scatter.11.cloned.1.call-update) | async-done | bytes 393232 | tf_op jit(solution)/shard_map/reduce_scatter | solution.py:72
  265.1 0.0 copy-done
  265.1 1.7 fusion.16
  (8 shorter events, 0.1 us)
Async XLA Ops:
  7.2 75.8 %reduce-scatter.5.cloned.1.call-start = ((), (), s32[]{:S(2)}) async-start(), calls=%async_computation.6 | async-start | bytes 2048000 | tf_op jit(solution)/shard_map/reduce_scatter | solution.py:54
  48.2 80.5 %reduce-scatter.9.cloned.1.call-start = ((), (), s32[]{:S(2)}) async-start(), calls=%async_computation.8 | async-start | bytes 7864320 | tf_op jit(solution)/shard_map/reduce_scatter | solution.py:56
  65.5 17.3 %copy-start.1 = (s32[16]{0:T(128)S(1)}, s32[16]{0:T(128)}, u32[]{:S(2)}) copy-start(s32[16]{0:T(128)} %param.19) | copy-start | bytes 196
  65.5 114.0 %reduce-scatter.7.cloned.1.call-start = ((), (), s32[]{:S(2)}) async-start(), calls=%async_computation.7 | async-start | bytes 7864320 | tf_op jit(solution)/shard_map/reduce_scatter | solution.py:55
  84.6 8.1 %all-to-all-start = ((bf16[2,16,3200]{2,1,0:T(8,128)(2,1)}), bf16[2,16,3200]{2,1,0:T(8,128)(2,1)S(1)}, u32[]{:S(2)}, u32[]{:S(2)}) async-start(bf16[2,16,3200]{2,1,0:T(8,128)(2,1)} %bitcast.4), calls=%async_computation.1 | async-start | bytes 409600 | tf_op jit(solution)/shard_map/all_to_all | solution.py:58
  88.1 147.0 %all-gather.2.cloned.1.call-start = ((), (), s32[]{:S(2)}) async-start(), calls=%async_computation.9 | async-start | bytes 3932160 | tf_op jit(solution)/shard_map/all_gather | solution.py:70
  182.8 82.3 %reduce-scatter.11.cloned.1.call-start = ((), (), s32[]{:S(2)}) async-start(), calls=%async_computation.10 | async-start | bytes 1179648 | tf_op jit(solution)/shard_map/reduce_scatter | solution.py:72
  235.1 30.0 %copy-start = (bf16[128,768]{1,0:T(8,128)(2,1)S(1)}, bf16[128,768]{1,0:T(8,128)(2,1)}, u32[]{:S(2)}) copy-start(bf16[128,768]{1,0:T(8,128)(2,1)} %param.10) | copy-start | bytes 589828
Sparse Core Ops, SparseCore 0:
  48.4 23.4 reduce-scatter.4
  74.4 51.3 reduce-scatter.8
  128.2 51.3 reduce-scatter.6
  182.9 25.4 all-gather.1
  251.5 13.5 reduce-scatter.10
where the time goes:
time: 274 us; the launch traced here: 273 us
  matrix products  86.4 us (32%)
  waiting for transfers between devices  69.3 us (25%)
  blocking collectives  50.2 us (18%)
  other arithmetic  49.5 us (18%)
  between operations  13.9 us (5%)
  starting transfers between devices  3.82 us (1%)
    reduce_scatter x1, waiting for transfers between devices, local_layer(): lax.psum_scatter(gate_part, 'x', scatter_dimension=0, tiled=True)  50.8 us
    psum x1, blocking collectives, local_layer(): row_stats = lax.psum(row_stats, both_axes)  25.1 us
    select_n x1, other arithmetic, local_layer(): k_all = jnp.where(new_slot, k_rot[:, None, :], kc_loc)  23.3 us
    dot_general x1, matrix products, local_layer(): up_part = jnp.dot(normed_rows, wup_loc, preferred_element_type=jnp.float32)  17.2 us
    dot_general x1, matrix products, local_layer(): jnp.dot(normed_rows, wgate_loc, preferred_element_type=jnp.float32)  17.2 us
    dot_general x1, matrix products, local_layer(): jnp.dot(mlp_full, wmo_loc, preferred_element_type=jnp.float32)  16.2 us
    sub x1, other arithmetic, attend_local(): attn_probs = jax.nn.softmax(scores, axis=-1).astype(jnp.bfloat16)  16.2 us
    reduce_scatter x1, waiting for transfers between devices, local_layer(): z_loc = lax.psum_scatter(z_part, 'yz', scatter_dimension=1, tiled=True)  13.7 us
  transfers between devices with their start and end apart: 6, of which 3 were waited for; matrix products, arithmetic and copies ran while one was open for 39% of the time, Pallas kernels for 0%

commit v1 on v0

v1 whole, which is shorter than its diff:
```python
import functools

import jax
import jax.numpy as jnp
from jax import lax
from jax.experimental import pallas as pl
from jax.experimental.pallas import tpu as pltpu
from jax.sharding import PartitionSpec as P

MESH = pl.DeviceIdType.MESH
F32 = jnp.float32
BF16 = jnp.bfloat16
VMEM_LIMIT = 66_900_000

C = 768
CQ = 640
SLOTS = 3
N1 = 4
N2 = 9


def remote(src, dst, send_sem, recv_sem, device):
    return pltpu.make_async_remote_copy(
        src_ref=src, dst_ref=dst, send_sem=send_sem, recv_sem=recv_sem, device_id=device, device_id_type=MESH
    )


def places():
    xi = lax.axis_index("x")
    yi = lax.axis_index("yz")
    sib = xi + 1 - 2 * (xi % 2)
    xn = (xi + 2) % 4
    return xi, yi, sib, xn, (sib + 2) % 4, 1 - yi


def activation(total):
    gate = total[:, :C].astype(BF16).astype(F32)
    up = total[:, C:].astype(BF16).astype(F32)
    return (jax.nn.silu(gate) * up).astype(BF16)


def front_kernel(
    d_model, x_ref, g_ref, wq_hbm, wg_hbm, wu_hbm,
    qkv_hbm, a_hbm, perm_hbm, send_hbm, own_hbm,
    stat, xbuf, gbuf, h, wq, wg, wu, pq, rq, xq, qs, qd, p, r, xr, a,
    wq_sem, wg_sem, wu_sem, st_s, st_r, xg_s, xg_r,
    dq_s, dq_r, xq_s, xq_r, yq_s, yq_r, d_s, d_r, x_s, x_r, out_sem, own_sem, q_sem, a_sem,
):
    xi, yi, sib, xn, sibn, yn = places()
    me = yi * 4 + xi
    rows, width = x_ref.shape
    num_q = wq_hbm.shape[1] // CQ
    num_c = wg_hbm.shape[1] // C
    sib_dev, xn_dev, yn_dev = {"x": sib}, {"x": xn}, {"yz": yn}

    def wq_copy(c):
        return pltpu.make_async_copy(wq_hbm.at[:, pl.ds(c * CQ, CQ)], wq.at[c], wq_sem.at[c])

    def w_copies(i, slot):
        start = pl.multiple_of(i * C, C)
        return (
            pltpu.make_async_copy(wg_hbm.at[:, pl.ds(start, C)], wg.at[slot], wg_sem.at[slot]),
            pltpu.make_async_copy(wu_hbm.at[:, pl.ds(start, C)], wu.at[slot], wu_sem.at[slot]),
        )

    for c in range(num_q):
        wq_copy(c).start()
    for i in range(SLOTS):
        for copy in w_copies(i, i):
            copy.start()

    barrier = pltpu.get_barrier_semaphore()
    offsets = [(dy, dx) for dy in range(2) for dx in range(4)][1:]
    for dy, dx in offsets:
        pl.semaphore_signal(barrier, inc=1, device_id={"yz": (yi + dy) % 2, "x": (xi + dx) % 4}, device_id_type=MESH)

    x_f32 = x_ref[...].astype(F32)
    lane = lax.broadcasted_iota(jnp.int32, (rows, rows), 1)
    sums = jnp.where(
        lane == 0,
        jnp.sum(x_f32, axis=1, keepdims=True),
        jnp.where(lane == 1, jnp.sum(x_f32 * x_f32, axis=1, keepdims=True), 0.0),
    )
    stat[me] = sums.T[0:8, :]
    gbuf[yi] = jnp.broadcast_to(g_ref[...].astype(F32), (8, width))
    xbuf[yi] = x_ref[...]
    pl.semaphore_wait(barrier, 7)

    def stat_copy(k, slot):
        dy, dx = offsets[k]
        dev = {"yz": (yi + dy) % 2, "x": (xi + dx) % 4}
        return remote(stat.at[slot], stat.at[slot], st_s.at[k], st_r.at[k], dev)

    def x_copy(slot):
        return remote(x_ref, xbuf.at[slot], xg_s.at[0], xg_r.at[0], yn_dev)

    def g_copy(slot):
        return remote(gbuf.at[slot], gbuf.at[slot], xg_s.at[1], xg_r.at[1], yn_dev)

    for k in range(7):
        stat_copy(k, me).start()
    g_copy(yi).start()
    x_copy(yi).start()
    for k, (dy, dx) in enumerate(offsets):
        stat_copy(k, ((yi + 2 - dy) % 2) * 4 + (xi + 4 - dx) % 4).wait_recv()
    total = stat[0]
    for k in range(1, 8):
        total = total + stat[k]
    cols = jnp.concatenate([total, jnp.zeros((rows - 8, rows), F32)], axis=0).T
    mean = cols[:, 0:1] / d_model
    var = cols[:, 1:2] / d_model - mean * mean
    scale = lax.rsqrt(var + 1e-6)
    g_copy(yn).wait_recv()
    x_copy(yn).wait_recv()
    for b in range(2):
        part = (xbuf[b].astype(F32) - mean) * scale * gbuf[b][0:1, :]
        h[:, b * width:(b + 1) * width] = part.astype(BF16)

    def dq(c, k):
        src = sib if k == 0 else sibn
        return remote(pq.at[c, src], rq.at[c, k], dq_s.at[c, k], dq_r.at[c, k], sib_dev)

    def xq_copy(c):
        return remote(pq.at[c, xn], xq.at[c], xq_s.at[c], xq_r.at[c], xn_dev)

    def q_sum(c):
        dq(c, 1).wait_recv()
        dq(c, 1).wait_send()
        pq[c, xn] = pq[c, xn] + rq[c, 1]
        xq_copy(c).start()
        dq(c, 0).wait_recv()
        dq(c, 0).wait_send()
        pq[c, xi] = pq[c, xi] + rq[c, 0]

    @pl.loop(0, num_q)
    def _(c):
        wq_copy(c).wait()
        prod = jnp.dot(h[...], wq[c], preferred_element_type=F32)
        pq[c] = prod.reshape(4, rows // 4, CQ)
        dq(c, 1).start()
        dq(c, 0).start()

        @pl.when(c >= 1)
        def _():
            q_sum(c - 1)

    def d_copy(i, k):
        src = sib if k == 0 else sibn
        return remote(p.at[i, src], r.at[i, k], d_s.at[i, k], d_r.at[i, k], sib_dev)

    def x_send(i):
        return remote(p.at[i, xn], xr.at[i], x_s.at[i], x_r.at[i], xn_dev)

    def perm_copy(i):
        return pltpu.make_async_copy(p.at[i, xn], perm_hbm.at[i - N1], out_sem.at[i])

    def send_copy(i):
        return pltpu.make_async_copy(p.at[i, xn], send_hbm.at[i - N2], out_sem.at[i])

    def own_copy(i):
        return pltpu.make_async_copy(p.at[i, xi], own_hbm.at[i - N1], own_sem.at[i])

    def chip_sum(i):
        d_copy(i, 1).wait_recv()
        d_copy(i, 1).wait_send()
        p[i, xn] = p[i, xn] + r[i, 1]

        @pl.when(i < N1)
        def _():
            x_send(i).start()

        @pl.when((i >= N1) & (i < N2))
        def _():
            perm_copy(i).start()

        @pl.when(i >= N2)
        def _():
            send_copy(i).start()

        d_copy(i, 0).wait_recv()
        d_copy(i, 0).wait_send()
        p[i, xi] = p[i, xi] + r[i, 0]

        @pl.when(i >= N1)
        def _():
            own_copy(i).start()

    def product(i):
        slot = i % SLOTS
        g_w, u_w = w_copies(i, slot)
        g_w.wait()
        p[i, :, :, :C] = jnp.dot(h[...], wg[slot], preferred_element_type=F32).reshape(4, rows // 4, C)
        u_w.wait()
        p[i, :, :, C:] = jnp.dot(h[...], wu[slot], preferred_element_type=F32).reshape(4, rows // 4, C)
        d_copy(i, 1).start()
        d_copy(i, 0).start()

        @pl.when(i + SLOTS < num_c)
        def _():
            for copy in w_copies(i + SLOTS, slot):
                copy.start()

    product(0)
    q_sum(num_q - 1)

    def step(i):
        product(i)
        chip_sum(i - 1)

    half = num_c // 2 + 1
    pl.loop(1, half)(step)

    @pl.loop(0, num_q)
    def _(c):
        xq_copy(c).wait_recv()
        xq_copy(c).wait_send()
        value = (pq[c, xi] + xq[c]).astype(BF16)
        qs[:, :, pl.ds(pl.multiple_of(c * CQ, CQ), CQ)] = value.reshape(2, rows // 8, CQ)

    def yq_copy(k):
        return remote(qs.at[1 - k], qd.at[k], yq_s, yq_r, yn_dev)

    yq_copy(yi).start()
    qd[yi] = qs[yi]

    pl.loop(half, num_c)(step)
    chip_sum(num_c - 1)
    yq_copy(yn).wait_recv()
    q_out = pltpu.make_async_copy(qd, qkv_hbm, q_sem)
    q_out.start()

    @pl.loop(0, N1)
    def _(i):
        x_send(i).wait_recv()
        x_send(i).wait_send()
        act = activation(p[i, xi] + xr[i])
        a[:, :, pl.ds(pl.multiple_of(i * C, C), C)] = act.reshape(2, rows // 8, C)

    a_out = pltpu.make_async_copy(a, a_hbm, a_sem)
    a_out.start()
    for k in range(7):
        stat_copy(k, me).wait_send()
    g_copy(yi).wait_send()
    x_copy(yi).wait_send()
    yq_copy(yi).wait_send()

    @pl.loop(N1, N2)
    def _(i):
        perm_copy(i).wait()
        own_copy(i).wait()

    @pl.loop(N2, num_c)
    def _(i):
        send_copy(i).wait()
        own_copy(i).wait()

    q_out.wait()
    a_out.wait()


def front(x_loc, gain_loc, wqkv, wgate, wup, d_model):
    rows, width = x_loc.shape
    depth, q_cols = wqkv.shape
    num_q, num_c = q_cols // CQ, wgate.shape[1] // C
    quarter = rows // 4
    dma = pltpu.SemaphoreType.DMA
    any_spec = pl.BlockSpec(memory_space=pl.ANY)
    vmem_spec = pl.BlockSpec(memory_space=pltpu.VMEM)
    return pl.pallas_call(
        functools.partial(front_kernel, d_model),
        name="front",
        out_shape=(
            jax.ShapeDtypeStruct((2, rows // 8, q_cols), BF16),
            jax.ShapeDtypeStruct((2, rows // 8, N1 * C), BF16),
            jax.ShapeDtypeStruct((N2 - N1, quarter, 2 * C), F32),
            jax.ShapeDtypeStruct((num_c - N2, quarter, 2 * C), F32),
            jax.ShapeDtypeStruct((num_c - N1, quarter, 2 * C), F32),
        ),
        in_specs=[vmem_spec, vmem_spec, any_spec, any_spec, any_spec],
        out_specs=(any_spec,) * 5,
        scratch_shapes=[
            pltpu.VMEM((8, 8, rows), F32),
            pltpu.VMEM((2, rows, width), BF16),
            pltpu.VMEM((2, 8, width), F32),
            pltpu.VMEM((rows, depth), BF16),
            pltpu.VMEM((num_q, depth, CQ), BF16),
            pltpu.VMEM((SLOTS, depth, C), BF16),
            pltpu.VMEM((SLOTS, depth, C), BF16),
            pltpu.VMEM((num_q, 4, quarter, CQ), F32),
            pltpu.VMEM((num_q, 2, quarter, CQ), F32),
            pltpu.VMEM((num_q, quarter, CQ), F32),
            pltpu.VMEM((2, rows // 8, q_cols), BF16),
            pltpu.VMEM((2, rows // 8, q_cols), BF16),
            pltpu.VMEM((num_c, 4, quarter, 2 * C), F32),
            pltpu.VMEM((num_c, 2, quarter, 2 * C), F32),
            pltpu.VMEM((N1, quarter, 2 * C), F32),
            pltpu.VMEM((2, rows // 8, N1 * C), BF16),
            dma((num_q,)), dma((SLOTS,)), dma((SLOTS,)), dma((7,)), dma((7,)), dma((2,)), dma((2,)),
            dma((num_q, 2)), dma((num_q, 2)), dma((num_q,)), dma((num_q,)), dma, dma,
            dma((num_c, 2)), dma((num_c, 2)), dma((N1,)), dma((N1,)), dma((num_c,)), dma((num_c,)), dma, dma,
        ],
        compiler_params=pltpu.CompilerParams(collective_id=0, has_side_effects=True, vmem_limit_bytes=VMEM_LIMIT),
        cost_estimate=pl.CostEstimate(
            flops=2 * rows * depth * (q_cols + 2 * wgate.shape[1]),
            bytes_accessed=2 * depth * (q_cols + 2 * wgate.shape[1]),
            transcendentals=0,
        ),
    )(x_loc, gain_loc, wqkv, wgate, wup)


def attend_kernel(len_ref, qkv_ref, cos_ref, sin_ref, k_ref, v_ref, ko_ref, vo_ref, o_ref):
    pos = len_ref[pl.program_id(0)]
    qkv = qkv_ref[0]
    heads, head_dim = qkv.shape[0] - 2, qkv.shape[1]
    wide = qkv.astype(F32)
    turned = (wide * cos_ref[0] + pltpu.roll(wide, head_dim // 2, 1) * sin_ref[0]).astype(BF16)
    query = turned[:heads]
    ko_ref[...] = k_ref[...]
    vo_ref[...] = v_ref[...]
    base = pl.multiple_of((pos // 16) * 16, 16)
    here = lax.broadcasted_iota(jnp.int32, (16, head_dim), 0) == pos - base
    for out, new in ((ko_ref, turned[heads:heads + 1]), (vo_ref, qkv[heads + 1:heads + 2])):
        tile = out[0, pl.ds(base, 16), :].astype(F32)
        out[0, pl.ds(base, 16), :] = jnp.where(here, new.astype(F32), tile).astype(BF16)
    scores = lax.dot_general(query, ko_ref[0], (((1,), (1,)), ((), ())), preferred_element_type=F32)
    scores = scores * head_dim ** -0.5
    at = lax.broadcasted_iota(jnp.int32, scores.shape, 1)
    scores = jnp.where(at <= pos, scores, -1e30)
    weight = jnp.exp(scores - jnp.max(scores, axis=1, keepdims=True))
    probs = (weight / jnp.sum(weight, axis=1, keepdims=True)).astype(BF16)
    o_ref[0] = jnp.dot(probs, vo_ref[0], preferred_element_type=F32).astype(BF16)


def attend(qkv, cos, sin, k_cache, v_cache, ctx_len):
    reqs, length, head_dim = k_cache.shape
    heads = qkv.shape[1] - 2
    cache_spec = pl.BlockSpec((1, length, head_dim), lambda i, lens: (i, 0, 0))
    table_spec = pl.BlockSpec((1, 1, head_dim), lambda i, lens: (i, 0, 0))
    return pl.pallas_call(
        attend_kernel,
        name="attend",
        grid_spec=pltpu.PrefetchScalarGridSpec(
            num_scalar_prefetch=1,
            grid=(reqs,),
            in_specs=[
                pl.BlockSpec((1, heads + 2, head_dim), lambda i, lens: (i, 0, 0)),
                table_spec, table_spec, cache_spec, cache_spec,
            ],
            out_specs=[cache_spec, cache_spec, pl.BlockSpec((1, heads, head_dim), lambda i, lens: (i, 0, 0))],
        ),
        out_shape=(
            jax.ShapeDtypeStruct(k_cache.shape, BF16),
            jax.ShapeDtypeStruct(v_cache.shape, BF16),
            jax.ShapeDtypeStruct((reqs, heads, head_dim), BF16),
        ),
        compiler_params=pltpu.CompilerParams(dimension_semantics=("arbitrary",)),
        cost_estimate=pl.CostEstimate(
            flops=64 * reqs * heads * length * head_dim,
            bytes_accessed=8 * reqs * length * head_dim,
            transcendentals=reqs * heads * length,
        ),
    )(ctx_len, qkv, cos, sin, k_cache, v_cache)


def back_kernel(
    x_ref, o_ref, a1_ref, own_hbm, perm_hbm, send_hbm, wao_hbm, wmo_hbm, y_ref,
    w, own, xr, act, z, zr,
    w_sem, own_sem, x_s, x_r, o_s, o_r, sib_s, sib_r, xn_s, xn_r, fwd_s, fwd_r, z_s, z_r,
):
    xi, yi, sib, xn, _, yn = places()
    sib_dev, xn_dev, yn_dev = {"x": sib}, {"x": xn}, {"yz": yn}
    rows = x_ref.shape[0]
    num_o, num_c = wao_hbm.shape[0] // C, wmo_hbm.shape[0] // C
    num_k = num_o + num_c
    o_cols = wao_hbm.shape[0]
    late = num_c - N1
    here = N2 - N1

    def w_copy(k):
        src = wao_hbm.at[pl.ds(k * C, C), :] if k < num_o else wmo_hbm.at[pl.ds((k - num_o) * C, C), :]
        return pltpu.make_async_copy(src, w.at[k], w_sem.at[k])

    def own_copy(i):
        return pltpu.make_async_copy(own_hbm.at[i], own.at[i], own_sem.at[i])

    def perm_copy(i):
        return pltpu.make_async_copy(perm_hbm.at[i], xr.at[i], x_r.at[i])

    def x_send(i):
        return remote(send_hbm.at[i - here], xr.at[i], x_s.at[i - here], x_r.at[i], xn_dev)

    barrier = pltpu.get_barrier_semaphore()
    for dev in (sib_dev, xn_dev, yn_dev):
        pl.semaphore_signal(barrier, inc=1, device_id=dev, device_id_type=MESH)
    for i in range(here):
        perm_copy(i).start()
        own_copy(i).start()
    for i in range(here, late):
        own_copy(i).start()
    for k in range(num_k):
        w_copy(k).start()
    z[...] = jnp.zeros_like(z)
    act[2 * xi + yi, :, :o_cols] = o_ref[yi]
    act[pl.ds(2 * xi, 2), :, o_cols:o_cols + N1 * C] = a1_ref[...]
    pl.semaphore_wait(barrier, 3)

    def o_copy(half, row):
        return remote(o_ref.at[half], act.at[2 * xi + row, :, 0:o_cols], o_s, o_r, yn_dev)

    def cols_of(e):
        if isinstance(e, int) and e == 0:
            return pl.ds(o_cols, N1 * C)
        if isinstance(e, int) and e == 1:
            return pl.ds(0, o_cols)
        return pl.ds(pl.multiple_of(o_cols + (N1 + e - 2) * C, C), C)

    def gather(e, owner, dev, send_sem, recv_sem):
        block = act.at[pl.ds(2 * owner, 2), :, cols_of(e)]
        return remote(block, block, send_sem.at[e], recv_sem.at[e], dev)

    def to_sib(e, owner):
        return gather(e, owner, sib_dev, sib_s, sib_r)

    def to_xn(e, owner):
        return gather(e, owner, xn_dev, xn_s, xn_r)

    def forward(e, owner):
        return gather(e, owner, sib_dev, fwd_s, fwd_r)

    def send_own(e):
        to_xn(e, xi).start()
        to_sib(e, xi).start()

    def pass_on(e):
        to_xn(e, xn).wait_recv()
        forward(e, xn).start()

    def arrived(e):
        to_sib(e, sib).wait_recv()
        forward(e, (sib + 2) % 4).wait_recv()

    def multiply(k, start):
        lhs = act[:, :, pl.ds(start, C)].reshape(rows, C)
        width = z.shape[2]
        for b in range(2):
            z[b] = z[b] + jnp.dot(lhs, w[k, :, b * width:(b + 1) * width], preferred_element_type=F32)

    def late_multiply(i):
        k = num_o + N1 + i
        pltpu.make_async_copy(wmo_hbm.at[pl.ds(0, C), :], w.at[k], w_sem.at[k]).wait()
        multiply(k, pl.multiple_of(k * C, C))

    def activate(i):
        own_copy(i).wait()
        value = activation(own[i] + xr[i])
        start = pl.multiple_of(o_cols + (N1 + i) * C, C)
        act[pl.ds(2 * xi, 2), :, pl.ds(start, C)] = value.reshape(2, rows // 8, C)

    ahead = 2
    o_copy(yn, yi).start()
    send_own(0)
    for i in range(here, min(here + ahead, late)):
        x_send(i).start()

    @pl.loop(0, here)
    def _(i):
        perm_copy(i).wait()
        activate(i)
        send_own(i + 2)

    o_copy(yi, yn).wait_recv()
    send_own(1)
    pass_on(0)
    pass_on(1)
    arrived(0)
    for k in range(num_o, num_o + N1):
        w_copy(k).wait()
        multiply(k, k * C)
    arrived(1)
    for k in range(num_o):
        w_copy(k).wait()
        multiply(k, k * C)

    @pl.loop(0, here)
    def _(i):
        pass_on(i + 2)

    @pl.loop(here, late)
    def _(i):
        x_send(i).wait_recv()
        activate(i)

        @pl.when(i + ahead < late)
        def _():
            x_send(i + ahead).start()

        send_own(i + 2)
        arrived(i - here + 2)
        late_multiply(i - here)

        @pl.when(i > here)
        def _():
            pass_on(i + 1)

    pass_on(late + 1)

    @pl.loop(late - here, late)
    def _(i):
        arrived(i + 2)
        late_multiply(i)

    z_copy = remote(z.at[yn], zr, z_s, z_r, yn_dev)
    z_copy.start()
    o_copy(yn, yi).wait_send()
    for e in range(2):
        to_xn(e, xi).wait_send()
        to_sib(e, xi).wait_send()
        forward(e, xn).wait_send()

    @pl.loop(2, late + 2)
    def _(e):
        to_xn(e, xi).wait_send()
        to_sib(e, xi).wait_send()
        forward(e, xn).wait_send()

    @pl.loop(here, late)
    def _(i):
        x_send(i).wait_send()

    z_copy.wait()
    y_ref[...] = (x_ref[...].astype(F32) + (z[yi] + zr[...])).astype(BF16)


def back(x_loc, o_halves, a1, own, perm, send, wao, wmo):
    rows, width = x_loc.shape
    num_o, num_c = wao.shape[0] // C, wmo.shape[0] // C
    num_k, late, groups = num_o + num_c, num_c - N1, 2 + num_c - N1
    quarter = rows // 4
    dma = pltpu.SemaphoreType.DMA
    any_spec = pl.BlockSpec(memory_space=pl.ANY)
    vmem_spec = pl.BlockSpec(memory_space=pltpu.VMEM)
    return pl.pallas_call(
        back_kernel,
        name="back",
        out_shape=jax.ShapeDtypeStruct((rows, width), BF16),
        in_specs=[vmem_spec] * 3 + [any_spec] * 5,
        out_specs=vmem_spec,
        scratch_shapes=[
            pltpu.VMEM((num_k, C, 2 * width), BF16),
            pltpu.VMEM((late, quarter, 2 * C), F32),
            pltpu.VMEM((late, quarter, 2 * C), F32),
            pltpu.VMEM((8, rows // 8, num_k * C), BF16),
            pltpu.VMEM((2, rows, width), F32),
            pltpu.VMEM((rows, width), F32),
            dma((num_k,)), dma((late,)), dma((num_c - N2,)), dma((late,)), dma, dma,
            dma((groups,)), dma((groups,)), dma((groups,)), dma((groups,)), dma((groups,)), dma((groups,)), dma, dma,
        ],
        compiler_params=pltpu.CompilerParams(collective_id=1, has_side_effects=True, vmem_limit_bytes=VMEM_LIMIT),
        cost_estimate=pl.CostEstimate(
            flops=4 * rows * num_k * C * width, bytes_accessed=4 * num_k * C * width, transcendentals=0
        ),
    )(x_loc, o_halves, a1, own, perm, send, wao, wmo)


def solution(mesh):
    x_size, yz_size = mesh.shape["x"], mesh.shape["yz"]
    both_axes = ("x", "yz")
    row_spec = P("dp", both_axes)
    in_w_spec = P("x", "yz")
    out_w_spec = P("yz", "x")
    cache_spec = P(("dp", "x", "yz"), None, None)
    len_spec = P(("dp", "x", "yz"))
    across = [(i, (i + 2) % 4) for i in range(4)]

    def local_layer(x_loc, gain_loc, wqkv_loc, wgate_loc, wup_loc, wao_loc, wmo_loc, kc_loc, vc_loc, len_loc):
        d_model = x_loc.shape[1] * x_size * yz_size
        reqs, _, head_dim = kc_loc.shape
        half = head_dim // 2
        inv_freq = 10000.0 ** (-jnp.arange(half, dtype=F32) / half)
        angles = len_loc.astype(F32)[:, None] * inv_freq
        cos, sin = jnp.cos(angles), jnp.sin(angles)
        cos = jnp.concatenate([cos, cos], axis=1)[:, None, :]
        sin = jnp.concatenate([-sin, sin], axis=1)[:, None, :]

        qkv, a1, perm, send, own = front(
            x_loc, gain_loc[None, :], wqkv_loc, wgate_loc, wup_loc, d_model
        )
        perm = lax.ppermute(perm, "x", across)
        qkv = jnp.concatenate([qkv[0], qkv[1]], axis=1).reshape(reqs, -1, head_dim)
        k_all, v_all, attn = attend(qkv, cos, sin, kc_loc, vc_loc, len_loc)
        o_halves = jnp.swapaxes(attn.reshape(reqs, 2, -1), 0, 1)
        y_loc = back(x_loc, o_halves, a1, own, perm, send, wao_loc, wmo_loc)
        return y_loc, k_all, v_all

    in_specs = (row_spec, P(both_axes), in_w_spec, in_w_spec, in_w_spec, out_w_spec, out_w_spec, cache_spec, cache_spec, len_spec)
    out_specs = (row_spec, cache_spec, cache_spec)
    return jax.shard_map(local_layer, mesh=mesh, in_specs=in_specs, out_specs=out_specs, check_vma=False)
```

time: 274 us -> 159 us (0.58)
  Pallas kernels: 0 us -> 149 us
  matrix products: 86.4 us -> 0 us
  waiting for transfers between devices: 69.3 us -> 0.01 us
  blocking collectives: 50.2 us -> 0 us
  other arithmetic: 49.5 us -> 1.59 us
  between operations: 13.9 us -> 0.69 us
  local copies, waits for them, and re-layouts: 0.19 us -> 5.65 us
    pallas_call x0 -> x3, Pallas kernels: none -> 149 us  [the longest x1 74.7 us: back(): pl.pallas_call(back_kernel, name='back', out_shape=jax.ShapeDtypeStruct((...]
    dot_general x7 -> x0, matrix products: 86.4 us -> none  [the longest x1 17.2 us: local_layer(): up_part = jnp.dot(normed_rows, wup_loc, preferred_element_type=jnp.float32)]
    reduce_scatter x4 -> x0, waiting for transfers between devices: 64.6 us -> none  [the longest x1 50.8 us: local_layer(): lax.psum_scatter(gate_part, 'x', scatter_dimension=0, tiled=True)]
    psum x1 -> x0, blocking collectives: 25.1 us -> none  [local_layer(): row_stats = lax.psum(row_stats, both_axes)]
    select_n x1 -> x0, other arithmetic: 23.3 us -> none  [local_layer(): k_all = jnp.where(new_slot, k_rot[:, None, :], kc_loc)]
    all_gather x2 -> x0, blocking collectives: 17.8 us -> none  [the longest x1 11.2 us: local_layer(): attn_full = lax.all_gather(attn_rows, 'x', axis=0, tiled=True)]
    sub x2 -> x0, other arithmetic: 16.2 us -> none  [the longest x1 16.2 us: attend_local(): attn_probs = jax.nn.softmax(scores, axis=-1).astype(jnp.bfloat16)]
    convert_element_type x7 -> x1, other arithmetic: 8.38 us -> 0.01 us  [local_layer(): angles = len_loc.astype(F32)[:, None] * inv_freq]
  transfers between devices with their start and end apart: 6 -> 1, of which waited for: 3 -> 0; matrix products, arithmetic and copies ran while one was open for 39% -> 3% of each run, Pallas kernels for 0% -> 20%
where the time goes in v1:
time: 159 us
  Pallas kernels  149 us (94%)
  local copies, waits for them, and re-layouts  5.65 us (4%)
  other arithmetic  1.59 us (1%)
    pallas_call x1, Pallas kernels, back(): pl.pallas_call(back_kernel, name='back', out_shape=jax.ShapeDtypeStruct((...  74.7 us
    pallas_call x1, Pallas kernels, front(): pl.pallas_call(functools.partial(front_kernel, d_model), name='front', ou...  43 us
    pallas_call x1, Pallas kernels, attend(): pl.pallas_call(attend_kernel, name='attend', grid_spec=pltpu.PrefetchScal...  31.6 us
  transfers between devices with their start and end apart: 1, of which 0 were waited for; matrix products, arithmetic and copies ran while one was open for 3% of the time, Pallas kernels for 20%

profile of v1, /device:TPU:0, one launch (start us, length us, event | category | flops | bytes accessed | tf_op | source)
XLA Modules:
  0.0 158.8 jit_solution(3091078824972652441)
XLA Ops:
  0.6 1.3 broadcast_in_dim.11.g_ref
  1.9 0.0 copy-start
  1.9 43.0 %front.1 = (bf16[2,16,3200]{2,1,0:T(8,128)(2,1)}, bf16[2,16,3072]{2,1,0:T(8,128)(2,1)}, f32[5,32,1536]{2,1,0:T(8,128)}, f32[7,32,1536]{2,1,0:T(8,128)}, f32[12,32,1536]{2,1,0:T(8,128)}) custom-call(bf16[128,768]{1,0:T(8,128)(2,1)} %x_ref.3, bf16[1,768]{1,0:T(2,128)(2,1)} %broadcast_in_dim.11.g_ref, bf16[1536,3200]{1,0:T(8,128)(2,1)} %wq_hbm.1, ...), custom_call_target="tpu_custom_call" | custom-call | flops 10921967616 | bytes 85327872 | tf_op jit(solution)/shard_map/front/pallas_call | solution.py:269
  44.9 1.5 collective-permute-start
  46.5 0.0 copy-done
  46.5 1.0 fusion.1
  47.4 0.1 concatenate.14
  47.5 0.1 concatenate.15
  47.6 0.1 fusion
  47.7 0.8 pad_maximum_fusion.qkv_ref
  48.5 0.7 pad_maximum_fusion.1
  49.2 31.6 %attend.1 = (bf16[16,4096,128]{2,1,0:T(8,128)(2,1)}, bf16[16,4096,128]{2,1,0:T(8,128)(2,1)}, bf16[16,48,128]{2,1,0:T(8,128)(2,1)}) custom-call(s32[16]{0:T(128)} %len_ref.1, bf16[16,50,128]{2,1,0:T(8,128)(2,1)} %pad_maximum_fusion.qkv_ref, f32[16,1,128]{2,1,0:T(1,128)} %bitcast.8, f32[16,1,128]{2,1,0:T(1,128)} %bitcast.9, bf16[16,4096,128]{2,1,0:T(8,128)(2,1)} %k_ref.1, ...), custom_call_target="tpu_custom_call" | custom-call | flops 25769803776 | bytes 67108864 | tf_op jit(solution)/shard_map/attend/pallas_call | solution.py:339
  80.8 1.0 reshape.21
  81.7 0.7 copy.17
  82.5 0.0 collective-permute-done.perm_hbm
  82.5 74.7 %back.1 = bf16[128,768]{1,0:T(8,128)(2,1)} custom-call(bf16[128,768]{1,0:T(8,128)(2,1)} %x_ref.3, bf16[2,16,3072]{2,1,0:T(8,128)(2,1)} %bitcast.7, bf16[2,16,3072]{2,1,0:T(8,128)(2,1)} %get-tuple-element.13.a1_ref, f32[12,32,1536]{2,1,0:T(8,128)} %get-tuple-element.14.own_hbm, f32[5,32,1536]{2,1,0:T(8,128)} %collective-permute-done.perm_hbm, ...), custom_call_target="tpu_custom_call" | custom-call | flops 6039797760 | bytes 47185920 | tf_op jit(solution)/shard_map/back/pallas_call | solution.py:542
  157.2 1.6 %copy.19 = bf16[128,768]{1,0:T(8,128)(2,1)} copy(bf16[128,768]{1,0:T(8,128)(2,1)} %back.1) | data formatting | bytes 393216
  (2 shorter events, 0.0 us)
Async XLA Ops:
  1.9 44.6 %copy-start = (s32[16]{0:T(128)S(1)}, s32[16]{0:T(128)}, u32[]{:S(2)}) copy-start(s32[16]{0:T(128)} %len_ref.1) | copy-start | bytes 196
  44.9 37.5 %collective-permute-start = (f32[5,32,1536]{2,1,0:T(8,128)}, f32[5,32,1536]{2,1,0:T(8,128)}, u32[]{:S(2)}, u32[]{:S(2)}) collective-permute-start(f32[5,32,1536]{2,1,0:T(8,128)} %get-tuple-element.15), channel_id=1, source_target_pairs={{0,2},{1,3},{2,0},{3,1},{4,6},{5,7},{6,4},{7,5}} | collective-permute-start | bytes 2949128 | tf_op jit(solution)/shard_map/ppermute | solution.py:588

commit v2 on v1

--- a/solution.py
+++ b/solution.py
@@ -16,7 +16,7 @@
 CQ = 640
 SLOTS = 3
 N1 = 4
-N2 = 9
+N2 = 12
 
 
 def remote(src, dst, send_sem, recv_sem, device):
@@ -82,7 +82,7 @@
         jnp.where(lane == 1, jnp.sum(x_f32 * x_f32, axis=1, keepdims=True), 0.0),
     )
     stat[me] = sums.T[0:8, :]
-    gbuf[yi] = jnp.broadcast_to(g_ref[...].astype(F32), (8, width))
+    gbuf[yi] = jnp.broadcast_to(g_ref[...].astype(F32)[None, :], (8, width))
     xbuf[yi] = x_ref[...]
     pl.semaphore_wait(barrier, 7)
 
@@ -583,7 +583,7 @@
         sin = jnp.concatenate([-sin, sin], axis=1)[:, None, :]
 
         qkv, a1, perm, send, own = front(
-            x_loc, gain_loc[None, :], wqkv_loc, wgate_loc, wup_loc, d_model
+            x_loc, gain_loc, wqkv_loc, wgate_loc, wup_loc, d_model
         )
         perm = lax.ppermute(perm, "x", across)
         qkv = jnp.concatenate([qkv[0], qkv[1]], axis=1).reshape(reqs, -1, head_dim)

time: 159 us -> 146 us (0.918)
  Pallas kernels: 149 us -> 137 us
    pallas_call x1, Pallas kernels: 74.7 us -> 62.3 us  [back(): pl.pallas_call(back_kernel, name='back', out_shape=jax.ShapeDtypeStruct((...]
  transfers between devices with their start and end apart: 1 -> 1, of which waited for: 0 -> 0; matrix products, arithmetic and copies ran while one was open for 3% -> 3% of each run, Pallas kernels for 20% -> 22%
where the time goes in v2:
time: 146 us; the launch traced here: 145 us
  Pallas kernels  137 us (94%)
  local copies, waits for them, and re-layouts  4.39 us (3%)
  other arithmetic  1.55 us (1%)
  starting transfers between devices  1.52 us (1%)
    pallas_call x1, Pallas kernels, back(): pl.pallas_call(back_kernel, name='back', out_shape=jax.ShapeDtypeStruct((...  62.3 us
    pallas_call x1, Pallas kernels, front(): pl.pallas_call(functools.partial(front_kernel, d_model), name='front', ou...  43 us
    pallas_call x1, Pallas kernels, attend(): pl.pallas_call(attend_kernel, name='attend', grid_spec=pltpu.PrefetchScal...  31.6 us
  transfers between devices with their start and end apart: 1, of which 0 were waited for; matrix products, arithmetic and copies ran while one was open for 3% of the time, Pallas kernels for 22%

profile of v2, /device:TPU:0, one launch (start us, length us, event | category | flops | bytes accessed | tf_op | source)
XLA Modules:
  0.0 145.1 jit_solution(1868761431156188120)
XLA Ops:
  0.6 0.0 copy-start
  0.6 43.0 %front.1 = (bf16[2,16,3200]{2,1,0:T(8,128)(2,1)}, bf16[2,16,3072]{2,1,0:T(8,128)(2,1)}, f32[8,32,1536]{2,1,0:T(8,128)}, f32[4,32,1536]{2,1,0:T(8,128)}, f32[12,32,1536]{2,1,0:T(8,128)}) custom-call(bf16[128,768]{1,0:T(8,128)(2,1)} %x_ref.3, bf16[768]{0:T(1024)(128)(2,1)} %g_ref.1, bf16[1536,3200]{1,0:T(8,128)(2,1)} %wq_hbm.1, bf16[1536,12288]{1,0:T(8,128)(2,1)} %wg_hbm.1, ...), custom_call_target="tpu_custom_call" | custom-call | flops 10921967616 | bytes 85327872 | tf_op jit(solution)/shard_map/front/pallas_call | solution.py:269
  43.7 1.5 %collective-permute-start = (f32[8,32,1536]{2,1,0:T(8,128)}, f32[8,32,1536]{2,1,0:T(8,128)}, u32[]{:S(2)}, u32[]{:S(2)}) collective-permute-start(f32[8,32,1536]{2,1,0:T(8,128)} %get-tuple-element.15), channel_id=1, source_target_pairs={{0,2},{1,3},{2,0},{3,1},{4,6},{5,7},{6,4},{7,5}} | collective-permute-start | bytes 4718600 | tf_op jit(solution)/shard_map/ppermute | solution.py:588
  45.2 0.0 copy-done
  45.2 1.0 fusion.1
  46.2 0.1 concatenate.14
  46.3 0.1 concatenate.15
  46.3 0.1 fusion
  46.4 0.7 pad_maximum_fusion.qkv_ref
  47.2 0.7 pad_maximum_fusion.1
  47.9 31.6 %attend.1 = (bf16[16,4096,128]{2,1,0:T(8,128)(2,1)}, bf16[16,4096,128]{2,1,0:T(8,128)(2,1)}, bf16[16,48,128]{2,1,0:T(8,128)(2,1)}) custom-call(s32[16]{0:T(128)} %len_ref.1, bf16[16,50,128]{2,1,0:T(8,128)(2,1)} %pad_maximum_fusion.qkv_ref, f32[16,1,128]{2,1,0:T(1,128)} %bitcast.8, f32[16,1,128]{2,1,0:T(1,128)} %bitcast.9, bf16[16,4096,128]{2,1,0:T(8,128)(2,1)} %k_ref.1, ...), custom_call_target="tpu_custom_call" | custom-call | flops 25769803776 | bytes 67108864 | tf_op jit(solution)/shard_map/attend/pallas_call | solution.py:339
  79.5 1.0 reshape.21
  80.5 0.7 copy.17
  81.2 0.0 collective-permute-done.perm_hbm
  81.2 62.3 %back.1 = bf16[128,768]{1,0:T(8,128)(2,1)} custom-call(bf16[128,768]{1,0:T(8,128)(2,1)} %x_ref.3, bf16[2,16,3072]{2,1,0:T(8,128)(2,1)} %bitcast.7, bf16[2,16,3072]{2,1,0:T(8,128)(2,1)} %get-tuple-element.13.a1_ref, f32[12,32,1536]{2,1,0:T(8,128)} %get-tuple-element.14.own_hbm, f32[8,32,1536]{2,1,0:T(8,128)} %collective-permute-done.perm_hbm, ...), custom_call_target="tpu_custom_call" | custom-call | flops 6039797760 | bytes 47185920 | tf_op jit(solution)/shard_map/back/pallas_call | solution.py:542
  143.5 1.6 %copy.19 = bf16[128,768]{1,0:T(8,128)(2,1)} copy(bf16[128,768]{1,0:T(8,128)(2,1)} %back.1) | data formatting | bytes 393216
  (2 shorter events, 0.0 us)
Async XLA Ops:
  0.6 44.6 %copy-start = (s32[16]{0:T(128)S(1)}, s32[16]{0:T(128)}, u32[]{:S(2)}) copy-start(s32[16]{0:T(128)} %len_ref.1) | copy-start | bytes 196
  43.7 37.5 %collective-permute-start = (f32[8,32,1536]{2,1,0:T(8,128)}, f32[8,32,1536]{2,1,0:T(8,128)}, u32[]{:S(2)}, u32[]{:S(2)}) collective-permute-start(f32[8,32,1536]{2,1,0:T(8,128)} %get-tuple-element.15), channel_id=1, source_target_pairs={{0,2},{1,3},{2,0},{3,1},{4,6},{5,7},{6,4},{7,5}} | collective-permute-start | bytes 4718600 | tf_op jit(solution)/shard_map/ppermute | solution.py:588

commit v3 on v2

--- a/solution.py
+++ b/solution.py
@@ -17,6 +17,7 @@
 SLOTS = 3
 N1 = 4
 N2 = 12
+PIECE = 3
 
 
 def remote(src, dst, send_sem, recv_sem, device):
@@ -369,12 +370,14 @@
 ):
     xi, yi, sib, xn, _, yn = places()
     sib_dev, xn_dev, yn_dev = {"x": sib}, {"x": xn}, {"yz": yn}
-    rows = x_ref.shape[0]
+    width = x_ref.shape[3]
+    half_rows = act.shape[1] * act.shape[2]
     num_o, num_c = wao_hbm.shape[0] // C, wmo_hbm.shape[0] // C
     num_k = num_o + num_c
     o_cols = wao_hbm.shape[0]
     late = num_c - N1
     here = N2 - N1
+    pieces = late // PIECE
 
     def w_copy(k):
         src = wao_hbm.at[pl.ds(k * C, C), :] if k < num_o else wmo_hbm.at[pl.ds((k - num_o) * C, C), :]
@@ -392,40 +395,38 @@
     barrier = pltpu.get_barrier_semaphore()
     for dev in (sib_dev, xn_dev, yn_dev):
         pl.semaphore_signal(barrier, inc=1, device_id=dev, device_id_type=MESH)
+    for i in range(late):
+        own_copy(i).start()
     for i in range(here):
         perm_copy(i).start()
-        own_copy(i).start()
-    for i in range(here, late):
-        own_copy(i).start()
     for k in range(num_k):
         w_copy(k).start()
-    z[...] = jnp.zeros_like(z)
-    act[2 * xi + yi, :, :o_cols] = o_ref[yi]
-    act[pl.ds(2 * xi, 2), :, o_cols:o_cols + N1 * C] = a1_ref[...]
+    act[yi, xi, :, :o_cols] = o_ref[yi]
+    act[:, xi, :, o_cols:o_cols + N1 * C] = a1_ref[...]
     pl.semaphore_wait(barrier, 3)
 
     def o_copy(half, row):
-        return remote(o_ref.at[half], act.at[2 * xi + row, :, 0:o_cols], o_s, o_r, yn_dev)
-
-    def cols_of(e):
-        if isinstance(e, int) and e == 0:
-            return pl.ds(o_cols, N1 * C)
-        if isinstance(e, int) and e == 1:
-            return pl.ds(0, o_cols)
-        return pl.ds(pl.multiple_of(o_cols + (N1 + e - 2) * C, C), C)
-
-    def gather(e, owner, dev, send_sem, recv_sem):
-        block = act.at[pl.ds(2 * owner, 2), :, cols_of(e)]
-        return remote(block, block, send_sem.at[e], recv_sem.at[e], dev)
+        return remote(o_ref.at[half], act.at[row, xi, :, 0:o_cols], o_s, o_r, yn_dev)
+
+    def block_of(e, owner):
+        if e == 0:
+            return act.at[:, owner, :, pl.ds(o_cols, N1 * C)]
+        if e == 1:
+            return act.at[:, owner, :, pl.ds(0, o_cols)]
+        half, n = divmod(e - 2, pieces)
+        return act.at[half, owner, :, pl.ds(o_cols + (N1 + n * PIECE) * C, PIECE * C)]
 
     def to_sib(e, owner):
-        return gather(e, owner, sib_dev, sib_s, sib_r)
+        block = block_of(e, owner)
+        return remote(block, block, sib_s.at[e], sib_r.at[e], sib_dev)
 
     def to_xn(e, owner):
-        return gather(e, owner, xn_dev, xn_s, xn_r)
+        block = block_of(e, owner)
+        return remote(block, block, xn_s.at[e], xn_r.at[e], xn_dev)
 
     def forward(e, owner):
-        return gather(e, owner, sib_dev, fwd_s, fwd_r)
+        block = block_of(e, owner)
+        return remote(block, block, fwd_s.at[e], fwd_r.at[e], sib_dev)
 
     def send_own(e):
         to_xn(e, xi).start()
@@ -438,128 +439,134 @@
     def arrived(e):
         to_sib(e, sib).wait_recv()
         forward(e, (sib + 2) % 4).wait_recv()
-
-    def multiply(k, start):
-        lhs = act[:, :, pl.ds(start, C)].reshape(rows, C)
-        width = z.shape[2]
-        for b in range(2):
-            z[b] = z[b] + jnp.dot(lhs, w[k, :, b * width:(b + 1) * width], preferred_element_type=F32)
-
-    def late_multiply(i):
-        k = num_o + N1 + i
-        pltpu.make_async_copy(wmo_hbm.at[pl.ds(0, C), :], w.at[k], w_sem.at[k]).wait()
-        multiply(k, pl.multiple_of(k * C, C))
 
     def activate(i):
         own_copy(i).wait()
         value = activation(own[i] + xr[i])
         start = pl.multiple_of(o_cols + (N1 + i) * C, C)
-        act[pl.ds(2 * xi, 2), :, pl.ds(start, C)] = value.reshape(2, rows // 8, C)
-
-    ahead = 2
+        act[:, xi, :, pl.ds(start, C)] = value.reshape(2, value.shape[0] // 2, C)
+
+    def w_wait(k):
+        pltpu.make_async_copy(wmo_hbm.at[pl.ds(0, C), :], w.at[k], w_sem.at[k]).wait()
+
+    def multiply(first, count):
+        @pl.loop(first, first + count)
+        def _(k):
+            w_wait(k)
+            lhs = act[:, :, :, pl.ds(pl.multiple_of(k * C, C), C)].reshape(2 * half_rows, C)
+            for b in range(2):
+                prod = jnp.dot(lhs, w[k, :, b * width:(b + 1) * width], preferred_element_type=F32)
+                z[b] = z[b] + prod.reshape(2, half_rows, width)
+
+    def multiply_half(half, n):
+        @pl.loop(num_o + N1 + n * PIECE, num_o + N1 + (n + 1) * PIECE)
+        def _(k):
+            if half == 0:
+                w_wait(k)
+            lhs = act[half, :, :, pl.ds(pl.multiple_of(k * C, C), C)].reshape(half_rows, C)
+            for b in range(2):
+                prod = jnp.dot(lhs, w[k, :, b * width:(b + 1) * width], preferred_element_type=F32)
+                z[b, half] = z[b, half] + prod
+
+    first = (late - here) // 2
+    for i in range(here, here + first):
+        x_send(i).start()
     o_copy(yn, yi).start()
-    send_own(0)
-    for i in range(here, min(here + ahead, late)):
-        x_send(i).start()
+    z[...] = jnp.zeros_like(z)
 
     @pl.loop(0, here)
     def _(i):
         perm_copy(i).wait()
         activate(i)
-        send_own(i + 2)
 
     o_copy(yi, yn).wait_recv()
     send_own(1)
-    pass_on(0)
-    pass_on(1)
-    arrived(0)
-    for k in range(num_o, num_o + N1):
-        w_copy(k).wait()
-        multiply(k, k * C)
-    arrived(1)
-    for k in range(num_o):
-        w_copy(k).wait()
-        multiply(k, k * C)
-
-    @pl.loop(0, here)
-    def _(i):
-        pass_on(i + 2)
-
-    @pl.loop(here, late)
+    send_own(0)
+    for i in range(here + first, late):
+        x_send(i).start()
+    ready = here // PIECE
+    for n in range(ready):
+        send_own(2 + n)
+
+    @pl.loop(here, here + first)
     def _(i):
         x_send(i).wait_recv()
         activate(i)
 
-        @pl.when(i + ahead < late)
-        def _():
-            x_send(i + ahead).start()
-
-        send_own(i + 2)
-        arrived(i - here + 2)
-        late_multiply(i - here)
-
-        @pl.when(i > here)
-        def _():
-            pass_on(i + 1)
-
-    pass_on(late + 1)
-
-    @pl.loop(late - here, late)
+    pass_on(1)
+    pass_on(0)
+    arrived(1)
+    multiply(0, num_o)
+    arrived(0)
+    multiply(num_o, N1)
+
+    @pl.loop(here + first, late)
     def _(i):
-        arrived(i + 2)
-        late_multiply(i)
-
-    z_copy = remote(z.at[yn], zr, z_s, z_r, yn_dev)
-    z_copy.start()
+        x_send(i).wait_recv()
+        activate(i)
+
+    groups = 2 + 2 * pieces
+    for e in range(2 + ready, groups):
+        send_own(e)
+    z_copies = [remote(z.at[yn, half], zr.at[half], z_s.at[half], z_r.at[half], yn_dev) for half in range(2)]
+    pass_on(2)
+    for e in range(2, groups):
+        if e + 1 < groups:
+            pass_on(e + 1)
+        arrived(e)
+        half, n = divmod(e - 2, pieces)
+        multiply_half(half, n)
+        if n == pieces - 1:
+            z_copies[half].start()
+
     o_copy(yn, yi).wait_send()
-    for e in range(2):
+    for e in range(groups):
         to_xn(e, xi).wait_send()
         to_sib(e, xi).wait_send()
         forward(e, xn).wait_send()
 
-    @pl.loop(2, late + 2)
-    def _(e):
-        to_xn(e, xi).wait_send()
-        to_sib(e, xi).wait_send()
-        forward(e, xn).wait_send()
-
     @pl.loop(here, late)
     def _(i):
         x_send(i).wait_send()
 
-    z_copy.wait()
-    y_ref[...] = (x_ref[...].astype(F32) + (z[yi] + zr[...])).astype(BF16)
+    for half in range(2):
+        z_copies[half].wait()
+        total = (z[yi, half] + zr[half]).reshape(act.shape[1], act.shape[2], width)
+        y_ref[:, half] = (x_ref[:, half].astype(F32) + total).astype(BF16)
 
 
 def back(x_loc, o_halves, a1, own, perm, send, wao, wmo):
     rows, width = x_loc.shape
     num_o, num_c = wao.shape[0] // C, wmo.shape[0] // C
-    num_k, late, groups = num_o + num_c, num_c - N1, 2 + num_c - N1
+    num_k, late = num_o + num_c, num_c - N1
+    groups = 2 + 2 * (late // PIECE)
     quarter = rows // 4
     dma = pltpu.SemaphoreType.DMA
     any_spec = pl.BlockSpec(memory_space=pl.ANY)
     vmem_spec = pl.BlockSpec(memory_space=pltpu.VMEM)
-    return pl.pallas_call(
+    y = pl.pallas_call(
         back_kernel,
         name="back",
-        out_shape=jax.ShapeDtypeStruct((rows, width), BF16),
+        out_shape=jax.ShapeDtypeStruct((4, 2, rows // 8, width), BF16),
         in_specs=[vmem_spec] * 3 + [any_spec] * 5,
         out_specs=vmem_spec,
         scratch_shapes=[
             pltpu.VMEM((num_k, C, 2 * width), BF16),
             pltpu.VMEM((late, quarter, 2 * C), F32),
             pltpu.VMEM((late, quarter, 2 * C), F32),
-            pltpu.VMEM((8, rows // 8, num_k * C), BF16),
-            pltpu.VMEM((2, rows, width), F32),
-            pltpu.VMEM((rows, width), F32),
+            pltpu.VMEM((2, 4, rows // 8, num_k * C), BF16),
+            pltpu.VMEM((2, 2, rows // 2, width), F32),
+            pltpu.VMEM((2, rows // 2, width), F32),
             dma((num_k,)), dma((late,)), dma((num_c - N2,)), dma((late,)), dma, dma,
-            dma((groups,)), dma((groups,)), dma((groups,)), dma((groups,)), dma((groups,)), dma((groups,)), dma, dma,
+            dma((groups,)), dma((groups,)), dma((groups,)), dma((groups,)), dma((groups,)), dma((groups,)),
+            dma((2,)), dma((2,)),
         ],
         compiler_params=pltpu.CompilerParams(collective_id=1, has_side_effects=True, vmem_limit_bytes=VMEM_LIMIT),
         cost_estimate=pl.CostEstimate(
             flops=4 * rows * num_k * C * width, bytes_accessed=4 * num_k * C * width, transcendentals=0
         ),
-    )(x_loc, o_halves, a1, own, perm, send, wao, wmo)
+    )(x_loc.reshape(4, 2, rows // 8, width), o_halves, a1, own, perm, send, wao, wmo)
+    return y.reshape(rows, width)
 
 
 def solution(mesh):

time: 146 us -> 142 us (0.973)
  Pallas kernels: 137 us -> 134 us
    pallas_call x1, Pallas kernels: 62.3 us -> 59.1 us  [back(): pl.pallas_call(back_kernel, name='back', out_shape=jax.ShapeDtypeStruct((...]
where the time goes in v3:
time: 142 us
  Pallas kernels  134 us (94%)
  local copies, waits for them, and re-layouts  4.39 us (3%)
  other arithmetic  1.55 us (1%)
  starting transfers between devices  1.52 us (1%)
    pallas_call x1, Pallas kernels, back(): pl.pallas_call(back_kernel, name='back', out_shape=jax.ShapeDtypeStruct((...  59.1 us
    pallas_call x1, Pallas kernels, front(): pl.pallas_call(functools.partial(front_kernel, d_model), name='front', ou...  43 us
    pallas_call x1, Pallas kernels, attend(): pl.pallas_call(attend_kernel, name='attend', grid_spec=pltpu.PrefetchScal...  31.6 us
  transfers between devices with their start and end apart: 1, of which 0 were waited for; matrix products, arithmetic and copies ran while one was open for 3% of the time, Pallas kernels for 22%

profile of v3, /device:TPU:0, one launch (start us, length us, event | category | flops | bytes accessed | tf_op | source)
XLA Modules:
  0.0 141.9 jit_solution(10119106467402419965)
XLA Ops:
  0.6 0.0 copy-start
  0.6 43.0 %front.1 = (bf16[2,16,3200]{2,1,0:T(8,128)(2,1)}, bf16[2,16,3072]{2,1,0:T(8,128)(2,1)}, f32[8,32,1536]{2,1,0:T(8,128)}, f32[4,32,1536]{2,1,0:T(8,128)}, f32[12,32,1536]{2,1,0:T(8,128)}) custom-call(bf16[128,768]{1,0:T(8,128)(2,1)} %x_ref.1, bf16[768]{0:T(1024)(128)(2,1)} %g_ref.1, bf16[1536,3200]{1,0:T(8,128)(2,1)} %wq_hbm.1, bf16[1536,12288]{1,0:T(8,128)(2,1)} %wg_hbm.1, ...), custom_call_target="tpu_custom_call" | custom-call | flops 10921967616 | bytes 85327872 | tf_op jit(solution)/shard_map/front/pallas_call | solution.py:270
  43.7 1.5 %collective-permute-start = (f32[8,32,1536]{2,1,0:T(8,128)}, f32[8,32,1536]{2,1,0:T(8,128)}, u32[]{:S(2)}, u32[]{:S(2)}) collective-permute-start(f32[8,32,1536]{2,1,0:T(8,128)} %get-tuple-element.15), channel_id=1, source_target_pairs={{0,2},{1,3},{2,0},{3,1},{4,6},{5,7},{6,4},{7,5}} | collective-permute-start | bytes 4718600 | tf_op jit(solution)/shard_map/ppermute | solution.py:595
  45.2 0.0 copy-done
  45.2 1.0 fusion.1
  46.2 0.1 concatenate.14
  46.3 0.1 concatenate.15
  46.3 0.1 fusion
  46.4 0.7 pad_maximum_fusion.qkv_ref
  47.2 0.7 pad_maximum_fusion.1
  47.9 31.6 %attend.1 = (bf16[16,4096,128]{2,1,0:T(8,128)(2,1)}, bf16[16,4096,128]{2,1,0:T(8,128)(2,1)}, bf16[16,48,128]{2,1,0:T(8,128)(2,1)}) custom-call(s32[16]{0:T(128)} %len_ref.1, bf16[16,50,128]{2,1,0:T(8,128)(2,1)} %pad_maximum_fusion.qkv_ref, f32[16,1,128]{2,1,0:T(1,128)} %bitcast.12, f32[16,1,128]{2,1,0:T(1,128)} %bitcast.13, bf16[16,4096,128]{2,1,0:T(8,128)(2,1)} %k_ref.1, ...), custom_call_target="tpu_custom_call" | custom-call | flops 25769803776 | bytes 67108864 | tf_op jit(solution)/shard_map/attend/pallas_call | solution.py:340
  79.5 1.0 reshape.28
  80.5 0.7 copy.17
  81.2 0.0 collective-permute-done.perm_hbm
  81.2 59.1 %back.1 = bf16[4,2,16,768]{3,2,1,0:T(8,128)(2,1)} custom-call(bf16[4,2,16,768]{3,2,1,0:T(8,128)(2,1)} %bitcast.11, bf16[2,16,3072]{2,1,0:T(8,128)(2,1)} %bitcast.9, bf16[2,16,3072]{2,1,0:T(8,128)(2,1)} %get-tuple-element.13.a1_ref, f32[12,32,1536]{2,1,0:T(8,128)} %get-tuple-element.14.own_hbm, f32[8,32,1536]{2,1,0:T(8,128)} %collective-permute-done.perm_hbm, ...), custom_call_target="tpu_custom_call" | custom-call | flops 6039797760 | bytes 47185920 | tf_op jit(solution)/shard_map/back/pallas_call | solution.py:547
  140.3 1.6 %copy.19 = bf16[128,768]{1,0:T(8,128)(2,1)} copy(bf16[128,768]{1,0:T(8,128)(2,1)} %bitcast.10) | data formatting | bytes 393216
  (2 shorter events, 0.0 us)
Async XLA Ops:
  0.6 44.6 %copy-start = (s32[16]{0:T(128)S(1)}, s32[16]{0:T(128)}, u32[]{:S(2)}) copy-start(s32[16]{0:T(128)} %len_ref.1) | copy-start | bytes 196
  43.7 37.5 %collective-permute-start = (f32[8,32,1536]{2,1,0:T(8,128)}, f32[8,32,1536]{2,1,0:T(8,128)}, u32[]{:S(2)}, u32[]{:S(2)}) collective-permute-start(f32[8,32,1536]{2,1,0:T(8,128)} %get-tuple-element.15), channel_id=1, source_target_pairs={{0,2},{1,3},{2,0},{3,1},{4,6},{5,7},{6,4},{7,5}} | collective-permute-start | bytes 4718600 | tf_op jit(solution)/shard_map/ppermute | solution.py:595

commit v4 on v3

--- a/solution.py
+++ b/solution.py
@@ -64,12 +64,6 @@
             pltpu.make_async_copy(wu_hbm.at[:, pl.ds(start, C)], wu.at[slot], wu_sem.at[slot]),
         )
 
-    for c in range(num_q):
-        wq_copy(c).start()
-    for i in range(SLOTS):
-        for copy in w_copies(i, i):
-            copy.start()
-
     barrier = pltpu.get_barrier_semaphore()
     offsets = [(dy, dx) for dy in range(2) for dx in range(4)][1:]
     for dy, dx in offsets:
@@ -102,6 +96,11 @@
         stat_copy(k, me).start()
     g_copy(yi).start()
     x_copy(yi).start()
+    for c in range(num_q):
+        wq_copy(c).start()
+    for i in range(SLOTS):
+        for copy in w_copies(i, i):
+            copy.start()
     for k, (dy, dx) in enumerate(offsets):
         stat_copy(k, ((yi + 2 - dy) % 2) * 4 + (xi + 4 - dx) % 4).wait_recv()
     total = stat[0]
@@ -399,8 +398,6 @@
         own_copy(i).start()
     for i in range(here):
         perm_copy(i).start()
-    for k in range(num_k):
-        w_copy(k).start()
     act[yi, xi, :, :o_cols] = o_ref[yi]
     act[:, xi, :, o_cols:o_cols + N1 * C] = a1_ref[...]
     pl.semaphore_wait(barrier, 3)
@@ -472,6 +469,8 @@
     for i in range(here, here + first):
         x_send(i).start()
     o_copy(yn, yi).start()
+    for k in range(num_k):
+        w_copy(k).start()
     z[...] = jnp.zeros_like(z)
 
     @pl.loop(0, here)

time: 142 us -> 137 us (0.965)
  Pallas kernels: 134 us -> 129 us
    pallas_call x1, Pallas kernels: 59.1 us -> 54 us  [back(): pl.pallas_call(back_kernel, name='back', out_shape=jax.ShapeDtypeStruct((...]
  transfers between devices with their start and end apart: 1 -> 1, of which waited for: 0 -> 0; matrix products, arithmetic and copies ran while one was open for 3% -> 3% of each run, Pallas kernels for 22% -> 23%
where the time goes in v4:
time: 137 us
  Pallas kernels  129 us (94%)
  local copies, waits for them, and re-layouts  4.39 us (3%)
  other arithmetic  1.55 us (1%)
  starting transfers between devices  1.51 us (1%)
    pallas_call x1, Pallas kernels, back(): pl.pallas_call(back_kernel, name='back', out_shape=jax.ShapeDtypeStruct((...  54 us
    pallas_call x1, Pallas kernels, front(): pl.pallas_call(functools.partial(front_kernel, d_model), name='front', ou...  43 us
    pallas_call x1, Pallas kernels, attend(): pl.pallas_call(attend_kernel, name='attend', grid_spec=pltpu.PrefetchScal...  31.6 us
  transfers between devices with their start and end apart: 1, of which 0 were waited for; matrix products, arithmetic and copies ran while one was open for 3% of the time, Pallas kernels for 23%

profile of v4, /device:TPU:0, one launch (start us, length us, event | category | flops | bytes accessed | tf_op | source)
XLA Modules:
  0.0 136.8 jit_solution(14996879072871767512)
XLA Ops:
  0.6 0.0 copy-start
  0.6 43.0 %front.1 = (bf16[2,16,3200]{2,1,0:T(8,128)(2,1)}, bf16[2,16,3072]{2,1,0:T(8,128)(2,1)}, f32[8,32,1536]{2,1,0:T(8,128)}, f32[4,32,1536]{2,1,0:T(8,128)}, f32[12,32,1536]{2,1,0:T(8,128)}) custom-call(bf16[128,768]{1,0:T(8,128)(2,1)} %x_ref.1, bf16[768]{0:T(1024)(128)(2,1)} %g_ref.1, bf16[1536,3200]{1,0:T(8,128)(2,1)} %wq_hbm.1, bf16[1536,12288]{1,0:T(8,128)(2,1)} %wg_hbm.1, ...), custom_call_target="tpu_custom_call" | custom-call | flops 10921967616 | bytes 85327872 | tf_op jit(solution)/shard_map/front/pallas_call | solution.py:269
  43.7 1.5 %collective-permute-start = (f32[8,32,1536]{2,1,0:T(8,128)}, f32[8,32,1536]{2,1,0:T(8,128)}, u32[]{:S(2)}, u32[]{:S(2)}) collective-permute-start(f32[8,32,1536]{2,1,0:T(8,128)} %get-tuple-element.15), channel_id=1, source_target_pairs={{0,2},{1,3},{2,0},{3,1},{4,6},{5,7},{6,4},{7,5}} | collective-permute-start | bytes 4718600 | tf_op jit(solution)/shard_map/ppermute | solution.py:594
  45.2 0.0 copy-done
  45.2 1.0 fusion.1
  46.2 0.1 concatenate.14
  46.2 0.1 concatenate.15
  46.3 0.1 fusion
  46.4 0.7 pad_maximum_fusion.qkv_ref
  47.2 0.7 pad_maximum_fusion.1
  47.8 31.6 %attend.1 = (bf16[16,4096,128]{2,1,0:T(8,128)(2,1)}, bf16[16,4096,128]{2,1,0:T(8,128)(2,1)}, bf16[16,48,128]{2,1,0:T(8,128)(2,1)}) custom-call(s32[16]{0:T(128)} %len_ref.1, bf16[16,50,128]{2,1,0:T(8,128)(2,1)} %pad_maximum_fusion.qkv_ref, f32[16,1,128]{2,1,0:T(1,128)} %bitcast.12, f32[16,1,128]{2,1,0:T(1,128)} %bitcast.13, bf16[16,4096,128]{2,1,0:T(8,128)(2,1)} %k_ref.1, ...), custom_call_target="tpu_custom_call" | custom-call | flops 25769803776 | bytes 67108864 | tf_op jit(solution)/shard_map/attend/pallas_call | solution.py:339
  79.5 1.0 reshape.28
  80.4 0.7 copy.17
  81.2 0.0 collective-permute-done.perm_hbm
  81.2 54.0 %back.1 = bf16[4,2,16,768]{3,2,1,0:T(8,128)(2,1)} custom-call(bf16[4,2,16,768]{3,2,1,0:T(8,128)(2,1)} %bitcast.11, bf16[2,16,3072]{2,1,0:T(8,128)(2,1)} %bitcast.9, bf16[2,16,3072]{2,1,0:T(8,128)(2,1)} %get-tuple-element.13.a1_ref, f32[12,32,1536]{2,1,0:T(8,128)} %get-tuple-element.14.own_hbm, f32[8,32,1536]{2,1,0:T(8,128)} %collective-permute-done.perm_hbm, ...), custom_call_target="tpu_custom_call" | custom-call | flops 6039797760 | bytes 47185920 | tf_op jit(solution)/shard_map/back/pallas_call | solution.py:546
  135.2 1.6 %copy.19 = bf16[128,768]{1,0:T(8,128)(2,1)} copy(bf16[128,768]{1,0:T(8,128)(2,1)} %bitcast.10) | data formatting | bytes 393216
  (2 shorter events, 0.0 us)
Async XLA Ops:
  0.6 44.6 %copy-start = (s32[16]{0:T(128)S(1)}, s32[16]{0:T(128)}, u32[]{:S(2)}) copy-start(s32[16]{0:T(128)} %len_ref.1) | copy-start | bytes 196
  43.7 37.5 %collective-permute-start = (f32[8,32,1536]{2,1,0:T(8,128)}, f32[8,32,1536]{2,1,0:T(8,128)}, u32[]{:S(2)}, u32[]{:S(2)}) collective-permute-start(f32[8,32,1536]{2,1,0:T(8,128)} %get-tuple-element.15), channel_id=1, source_target_pairs={{0,2},{1,3},{2,0},{3,1},{4,6},{5,7},{6,4},{7,5}} | collective-permute-start | bytes 4718600 | tf_op jit(solution)/shard_map/ppermute | solution.py:594

commit v5 on v4

--- a/solution.py
+++ b/solution.py
@@ -16,8 +16,8 @@
 CQ = 640
 SLOTS = 3
 N1 = 4
-N2 = 12
-PIECE = 3
+N2 = 13
+PIECES = (3, 3, 3, 2, 1)
 
 
 def remote(src, dst, send_sem, recv_sem, device):
@@ -41,15 +41,18 @@
 
 
 def front_kernel(
-    d_model, x_ref, g_ref, wq_hbm, wg_hbm, wu_hbm,
+    d_model, x_hbm, g_hbm, wq_hbm, wg_hbm, wu_hbm,
     qkv_hbm, a_hbm, perm_hbm, send_hbm, own_hbm,
-    stat, xbuf, gbuf, h, wq, wg, wu, pq, rq, xq, qs, qd, p, r, xr, a,
-    wq_sem, wg_sem, wu_sem, st_s, st_r, xg_s, xg_r,
+    stat, xbuf, gain, gbuf, moments, h, wq, wg, wu, pq, rq, xq, qs, qd, p, r, xr, a,
+    in_sem, wq_sem, wg_sem, wu_sem, st_s, st_r, xg_s, xg_r,
     dq_s, dq_r, xq_s, xq_r, yq_s, yq_r, d_s, d_r, x_s, x_r, out_sem, own_sem, q_sem, a_sem,
 ):
     xi, yi, sib, xn, sibn, yn = places()
     me = yi * 4 + xi
-    rows, width = x_ref.shape
+    sides, side_rows, width = x_hbm.shape
+    rows = sides * side_rows
+    near = xi // 2
+    far = 1 - near
     num_q = wq_hbm.shape[1] // CQ
     num_c = wg_hbm.shape[1] // C
     sib_dev, xn_dev, yn_dev = {"x": sib}, {"x": xn}, {"yz": yn}
@@ -64,12 +67,17 @@
             pltpu.make_async_copy(wu_hbm.at[:, pl.ds(start, C)], wu.at[slot], wu_sem.at[slot]),
         )
 
+    x_in = pltpu.make_async_copy(x_hbm, xbuf.at[yi], in_sem.at[0])
+    g_in = pltpu.make_async_copy(g_hbm, gain, in_sem.at[1])
+    x_in.start()
+    g_in.start()
     barrier = pltpu.get_barrier_semaphore()
     offsets = [(dy, dx) for dy in range(2) for dx in range(4)][1:]
     for dy, dx in offsets:
         pl.semaphore_signal(barrier, inc=1, device_id={"yz": (yi + dy) % 2, "x": (xi + dx) % 4}, device_id_type=MESH)
 
-    x_f32 = x_ref[...].astype(F32)
+    x_in.wait()
+    x_f32 = xbuf[yi].reshape(rows, width).astype(F32)
     lane = lax.broadcasted_iota(jnp.int32, (rows, rows), 1)
     sums = jnp.where(
         lane == 0,
@@ -77,8 +85,8 @@
         jnp.where(lane == 1, jnp.sum(x_f32 * x_f32, axis=1, keepdims=True), 0.0),
     )
     stat[me] = sums.T[0:8, :]
-    gbuf[yi] = jnp.broadcast_to(g_ref[...].astype(F32)[None, :], (8, width))
-    xbuf[yi] = x_ref[...]
+    g_in.wait()
+    gbuf[yi] = jnp.broadcast_to(gain[...].astype(F32)[None, :], (8, width))
     pl.semaphore_wait(barrier, 7)
 
     def stat_copy(k, slot):
@@ -86,16 +94,20 @@
         dev = {"yz": (yi + dy) % 2, "x": (xi + dx) % 4}
         return remote(stat.at[slot], stat.at[slot], st_s.at[k], st_r.at[k], dev)
 
-    def x_copy(slot):
-        return remote(x_ref, xbuf.at[slot], xg_s.at[0], xg_r.at[0], yn_dev)
+    def x_copies(slot):
+        return [
+            remote(xbuf.at[slot, side], xbuf.at[slot, side], xg_s.at[1 + n], xg_r.at[1 + n], yn_dev)
+            for n, side in enumerate((far, near))
+        ]
 
     def g_copy(slot):
-        return remote(gbuf.at[slot], gbuf.at[slot], xg_s.at[1], xg_r.at[1], yn_dev)
+        return remote(gbuf.at[slot], gbuf.at[slot], xg_s.at[0], xg_r.at[0], yn_dev)
 
     for k in range(7):
         stat_copy(k, me).start()
     g_copy(yi).start()
-    x_copy(yi).start()
+    for copy in x_copies(yi):
+        copy.start()
     for c in range(num_q):
         wq_copy(c).start()
     for i in range(SLOTS):
@@ -109,12 +121,14 @@
     cols = jnp.concatenate([total, jnp.zeros((rows - 8, rows), F32)], axis=0).T
     mean = cols[:, 0:1] / d_model
     var = cols[:, 1:2] / d_model - mean * mean
-    scale = lax.rsqrt(var + 1e-6)
+    moments[0] = jnp.broadcast_to(mean, (rows, 128)).reshape(sides, side_rows, 128)
+    moments[1] = jnp.broadcast_to(lax.rsqrt(var + 1e-6), (rows, 128)).reshape(sides, side_rows, 128)
     g_copy(yn).wait_recv()
-    x_copy(yn).wait_recv()
-    for b in range(2):
-        part = (xbuf[b].astype(F32) - mean) * scale * gbuf[b][0:1, :]
-        h[:, b * width:(b + 1) * width] = part.astype(BF16)
+
+    def normalize(side):
+        for b in range(2):
+            part = (xbuf[b, side].astype(F32) - moments[0, side][:, 0:1]) * moments[1, side][:, 0:1]
+            h[side, :, b * width:(b + 1) * width] = (part * gbuf[b][0:1, :]).astype(BF16)
 
     def dq(c, k):
         src = sib if k == 0 else sibn
@@ -123,26 +137,37 @@
     def xq_copy(c):
         return remote(pq.at[c, xn], xq.at[c], xq_s.at[c], xq_r.at[c], xn_dev)
 
-    def q_sum(c):
+    def q_product(c, side):
+        prod = jnp.dot(h[side], wq[c], preferred_element_type=F32)
+        pq[c, pl.ds(2 * side, 2)] = prod.reshape(2, rows // 4, CQ)
+
+    def q_send(c):
         dq(c, 1).wait_recv()
         dq(c, 1).wait_send()
         pq[c, xn] = pq[c, xn] + rq[c, 1]
         xq_copy(c).start()
-        dq(c, 0).wait_recv()
-        dq(c, 0).wait_send()
-        pq[c, xi] = pq[c, xi] + rq[c, 0]
+
+    x_copies(yn)[0].wait_recv()
+    normalize(far)
 
     @pl.loop(0, num_q)
     def _(c):
         wq_copy(c).wait()
-        prod = jnp.dot(h[...], wq[c], preferred_element_type=F32)
-        pq[c] = prod.reshape(4, rows // 4, CQ)
+        q_product(c, far)
         dq(c, 1).start()
-        dq(c, 0).start()
 
         @pl.when(c >= 1)
         def _():
-            q_sum(c - 1)
+            q_send(c - 1)
+
+    x_copies(yn)[1].wait_recv()
+    normalize(near)
+    q_send(num_q - 1)
+
+    @pl.loop(0, num_q)
+    def _(c):
+        q_product(c, near)
+        dq(c, 0).start()
 
     def d_copy(i, k):
         src = sib if k == 0 else sibn
@@ -188,10 +213,11 @@
     def product(i):
         slot = i % SLOTS
         g_w, u_w = w_copies(i, slot)
+        h_all = h[...].reshape(rows, h.shape[2])
         g_w.wait()
-        p[i, :, :, :C] = jnp.dot(h[...], wg[slot], preferred_element_type=F32).reshape(4, rows // 4, C)
+        p[i, :, :, :C] = jnp.dot(h_all, wg[slot], preferred_element_type=F32).reshape(4, rows // 4, C)
         u_w.wait()
-        p[i, :, :, C:] = jnp.dot(h[...], wu[slot], preferred_element_type=F32).reshape(4, rows // 4, C)
+        p[i, :, :, C:] = jnp.dot(h_all, wu[slot], preferred_element_type=F32).reshape(4, rows // 4, C)
         d_copy(i, 1).start()
         d_copy(i, 0).start()
 
@@ -201,7 +227,6 @@
                 copy.start()
 
     product(0)
-    q_sum(num_q - 1)
 
     def step(i):
         product(i)
@@ -212,9 +237,12 @@
 
     @pl.loop(0, num_q)
     def _(c):
+        dq(c, 0).wait_recv()
+        dq(c, 0).wait_send()
+        mine = pq[c, xi] + rq[c, 0]
         xq_copy(c).wait_recv()
         xq_copy(c).wait_send()
-        value = (pq[c, xi] + xq[c]).astype(BF16)
+        value = (mine + xq[c]).astype(BF16)
         qs[:, :, pl.ds(pl.multiple_of(c * CQ, CQ), CQ)] = value.reshape(2, rows // 8, CQ)
 
     def yq_copy(k):
@@ -241,7 +269,8 @@
     for k in range(7):
         stat_copy(k, me).wait_send()
     g_copy(yi).wait_send()
-    x_copy(yi).wait_send()
+    for copy in x_copies(yi):
+        copy.wait_send()
     yq_copy(yi).wait_send()
 
     @pl.loop(N1, N2)
@@ -265,7 +294,6 @@
     quarter = rows // 4
     dma = pltpu.SemaphoreType.DMA
     any_spec = pl.BlockSpec(memory_space=pl.ANY)
-    vmem_spec = pl.BlockSpec(memory_space=pltpu.VMEM)
     return pl.pallas_call(
         functools.partial(front_kernel, d_model),
         name="front",
@@ -276,13 +304,15 @@
             jax.ShapeDtypeStruct((num_c - N2, quarter, 2 * C), F32),
             jax.ShapeDtypeStruct((num_c - N1, quarter, 2 * C), F32),
         ),
-        in_specs=[vmem_spec, vmem_spec, any_spec, any_spec, any_spec],
+        in_specs=[any_spec] * 5,
         out_specs=(any_spec,) * 5,
         scratch_shapes=[
             pltpu.VMEM((8, 8, rows), F32),
-            pltpu.VMEM((2, rows, width), BF16),
+            pltpu.VMEM((2, 2, rows // 2, width), BF16),
+            pltpu.VMEM((width,), BF16),
             pltpu.VMEM((2, 8, width), F32),
-            pltpu.VMEM((rows, depth), BF16),
+            pltpu.VMEM((2, 2, rows // 2, 128), F32),
+            pltpu.VMEM((2, rows // 2, depth), BF16),
             pltpu.VMEM((num_q, depth, CQ), BF16),
             pltpu.VMEM((SLOTS, depth, C), BF16),
             pltpu.VMEM((SLOTS, depth, C), BF16),
@@ -295,7 +325,7 @@
             pltpu.VMEM((num_c, 2, quarter, 2 * C), F32),
             pltpu.VMEM((N1, quarter, 2 * C), F32),
             pltpu.VMEM((2, rows // 8, N1 * C), BF16),
-            dma((num_q,)), dma((SLOTS,)), dma((SLOTS,)), dma((7,)), dma((7,)), dma((2,)), dma((2,)),
+            dma((2,)), dma((num_q,)), dma((SLOTS,)), dma((SLOTS,)), dma((7,)), dma((7,)), dma((3,)), dma((3,)),
             dma((num_q, 2)), dma((num_q, 2)), dma((num_q,)), dma((num_q,)), dma, dma,
             dma((num_c, 2)), dma((num_c, 2)), dma((N1,)), dma((N1,)), dma((num_c,)), dma((num_c,)), dma, dma,
         ],
@@ -305,7 +335,7 @@
             bytes_accessed=2 * depth * (q_cols + 2 * wgate.shape[1]),
             transcendentals=0,
         ),
-    )(x_loc, gain_loc, wqkv, wgate, wup)
+    )(x_loc.reshape(2, rows // 2, width), gain_loc, wqkv, wgate, wup)
 
 
 def attend_kernel(len_ref, qkv_ref, cos_ref, sin_ref, k_ref, v_ref, ko_ref, vo_ref, o_ref):
@@ -363,20 +393,21 @@
 
 
 def back_kernel(
-    x_ref, o_ref, a1_ref, own_hbm, perm_hbm, send_hbm, wao_hbm, wmo_hbm, y_ref,
+    o_hbm, a1_hbm, own_hbm, perm_hbm, send_hbm, wao_hbm, wmo_hbm, z_hbm,
     w, own, xr, act, z, zr,
-    w_sem, own_sem, x_s, x_r, o_s, o_r, sib_s, sib_r, xn_s, xn_r, fwd_s, fwd_r, z_s, z_r,
+    in_sem, out_sem, w_sem, own_sem, x_s, x_r, o_s, o_r, sib_s, sib_r, xn_s, xn_r, fwd_s, fwd_r, z_s, z_r,
 ):
     xi, yi, sib, xn, _, yn = places()
     sib_dev, xn_dev, yn_dev = {"x": sib}, {"x": xn}, {"yz": yn}
-    width = x_ref.shape[3]
+    width = z_hbm.shape[3]
     half_rows = act.shape[1] * act.shape[2]
     num_o, num_c = wao_hbm.shape[0] // C, wmo_hbm.shape[0] // C
     num_k = num_o + num_c
     o_cols = wao_hbm.shape[0]
     late = num_c - N1
     here = N2 - N1
-    pieces = late // PIECE
+    pieces = len(PIECES)
+    starts = [sum(PIECES[:n]) for n in range(pieces + 1)]
 
     def w_copy(k):
         src = wao_hbm.at[pl.ds(k * C, C), :] if k < num_o else wmo_hbm.at[pl.ds((k - num_o) * C, C), :]
@@ -394,16 +425,18 @@
     barrier = pltpu.get_barrier_semaphore()
     for dev in (sib_dev, xn_dev, yn_dev):
         pl.semaphore_signal(barrier, inc=1, device_id=dev, device_id_type=MESH)
+    o_in = pltpu.make_async_copy(o_hbm.at[yi], act.at[yi, xi, :, 0:o_cols], in_sem.at[0])
+    a1_in = pltpu.make_async_copy(a1_hbm, act.at[:, xi, :, pl.ds(o_cols, N1 * C)], in_sem.at[1])
+    o_in.start()
+    a1_in.start()
     for i in range(late):
         own_copy(i).start()
     for i in range(here):
         perm_copy(i).start()
-    act[yi, xi, :, :o_cols] = o_ref[yi]
-    act[:, xi, :, o_cols:o_cols + N1 * C] = a1_ref[...]
     pl.semaphore_wait(barrier, 3)
 
     def o_copy(half, row):
-        return remote(o_ref.at[half], act.at[row, xi, :, 0:o_cols], o_s, o_r, yn_dev)
+        return remote(o_hbm.at[half], act.at[row, xi, :, 0:o_cols], o_s, o_r, yn_dev)
 
     def block_of(e, owner):
         if e == 0:
@@ -411,7 +444,7 @@
         if e == 1:
             return act.at[:, owner, :, pl.ds(0, o_cols)]
         half, n = divmod(e - 2, pieces)
-        return act.at[half, owner, :, pl.ds(o_cols + (N1 + n * PIECE) * C, PIECE * C)]
+        return act.at[half, owner, :, pl.ds(o_cols + (N1 + starts[n]) * C, PIECES[n] * C)]
 
     def to_sib(e, owner):
         block = block_of(e, owner)
@@ -453,19 +486,19 @@
             lhs = act[:, :, :, pl.ds(pl.multiple_of(k * C, C), C)].reshape(2 * half_rows, C)
             for b in range(2):
                 prod = jnp.dot(lhs, w[k, :, b * width:(b + 1) * width], preferred_element_type=F32)
-                z[b] = z[b] + prod.reshape(2, half_rows, width)
+                z[b] = z[b] + prod.reshape(z.shape[1:])
 
     def multiply_half(half, n):
-        @pl.loop(num_o + N1 + n * PIECE, num_o + N1 + (n + 1) * PIECE)
+        @pl.loop(num_o + N1 + starts[n], num_o + N1 + starts[n + 1])
         def _(k):
             if half == 0:
                 w_wait(k)
             lhs = act[half, :, :, pl.ds(pl.multiple_of(k * C, C), C)].reshape(half_rows, C)
             for b in range(2):
                 prod = jnp.dot(lhs, w[k, :, b * width:(b + 1) * width], preferred_element_type=F32)
-                z[b, half] = z[b, half] + prod
-
-    first = (late - here) // 2
+                z[b, half] = z[b, half] + prod.reshape(z.shape[2:])
+
+    first = (late - here + 1) // 2
     for i in range(here, here + first):
         x_send(i).start()
     o_copy(yn, yi).start()
@@ -478,12 +511,14 @@
         perm_copy(i).wait()
         activate(i)
 
+    a1_in.wait()
+    o_in.wait()
     o_copy(yi, yn).wait_recv()
     send_own(1)
     send_own(0)
     for i in range(here + first, late):
         x_send(i).start()
-    ready = here // PIECE
+    ready = sum(end <= here for end in starts[1:])
     for n in range(ready):
         send_own(2 + n)
 
@@ -528,35 +563,37 @@
     def _(i):
         x_send(i).wait_send()
 
+    outs = [pltpu.make_async_copy(zr.at[half], z_hbm.at[:, half], out_sem.at[half]) for half in range(2)]
     for half in range(2):
         z_copies[half].wait()
-        total = (z[yi, half] + zr[half]).reshape(act.shape[1], act.shape[2], width)
-        y_ref[:, half] = (x_ref[:, half].astype(F32) + total).astype(BF16)
+        zr[half] = z[yi, half] + zr[half]
+        outs[half].start()
+    for half in range(2):
+        outs[half].wait()
 
 
 def back(x_loc, o_halves, a1, own, perm, send, wao, wmo):
     rows, width = x_loc.shape
     num_o, num_c = wao.shape[0] // C, wmo.shape[0] // C
     num_k, late = num_o + num_c, num_c - N1
-    groups = 2 + 2 * (late // PIECE)
+    groups = 2 + 2 * len(PIECES)
     quarter = rows // 4
     dma = pltpu.SemaphoreType.DMA
     any_spec = pl.BlockSpec(memory_space=pl.ANY)
-    vmem_spec = pl.BlockSpec(memory_space=pltpu.VMEM)
-    y = pl.pallas_call(
+    z = pl.pallas_call(
         back_kernel,
         name="back",
-        out_shape=jax.ShapeDtypeStruct((4, 2, rows // 8, width), BF16),
-        in_specs=[vmem_spec] * 3 + [any_spec] * 5,
-        out_specs=vmem_spec,
+        out_shape=jax.ShapeDtypeStruct((4, 2, rows // 8, width), F32),
+        in_specs=[any_spec] * 7,
+        out_specs=any_spec,
         scratch_shapes=[
             pltpu.VMEM((num_k, C, 2 * width), BF16),
             pltpu.VMEM((late, quarter, 2 * C), F32),
             pltpu.VMEM((late, quarter, 2 * C), F32),
             pltpu.VMEM((2, 4, rows // 8, num_k * C), BF16),
-            pltpu.VMEM((2, 2, rows // 2, width), F32),
-            pltpu.VMEM((2, rows // 2, width), F32),
-            dma((num_k,)), dma((late,)), dma((num_c - N2,)), dma((late,)), dma, dma,
+            pltpu.VMEM((2, 2, 4, rows // 8, width), F32),
+            pltpu.VMEM((2, 4, rows // 8, width), F32),
+            dma((2,)), dma((2,)), dma((num_k,)), dma((late,)), dma((num_c - N2,)), dma((late,)), dma, dma,
             dma((groups,)), dma((groups,)), dma((groups,)), dma((groups,)), dma((groups,)), dma((groups,)),
             dma((2,)), dma((2,)),
         ],
@@ -564,8 +601,8 @@
         cost_estimate=pl.CostEstimate(
             flops=4 * rows * num_k * C * width, bytes_accessed=4 * num_k * C * width, transcendentals=0
         ),
-    )(x_loc.reshape(4, 2, rows // 8, width), o_halves, a1, own, perm, send, wao, wmo)
-    return y.reshape(rows, width)
+    )(o_halves, a1, own, perm, send, wao, wmo)
+    return (x_loc.astype(F32) + z.reshape(rows, width)).astype(BF16)
 
 
 def solution(mesh):

time: 137 us -> 136 us (level)
  Pallas kernels: 129 us -> 124 us
  waiting for transfers between devices: 0.01 us -> 3.62 us
  other arithmetic: 1.55 us -> 3.31 us
  local copies, waits for them, and re-layouts: 4.39 us -> 2.77 us
    pallas_call x1, Pallas kernels: 54 us -> 49.8 us  [back(): pl.pallas_call(back_kernel, name='back', out_shape=jax.ShapeDtypeStruct((...]
    ppermute x1, waiting for transfers between devices: 0.01 us -> 3.62 us  [local_layer(): perm = lax.ppermute(perm, 'x', across)]
    convert_element_type x0 -> x1, other arithmetic: none -> 1.76 us  [back(): return (x_loc.astype(F32) + z.reshape(rows, width)).astype(BF16)]
    unnamed x3 -> x2, local copies, waits for them, and re-layouts: 1.62 us -> 0.01 us
  transfers between devices with their start and end apart: 1 -> 1, of which waited for: 0 -> 1; matrix products, arithmetic and copies ran while one was open for 3% -> 3% of each run, Pallas kernels for 23% -> 23%
where the time goes in v5:
time: 136 us; the launch traced here: 135 us
  Pallas kernels  124 us (91%)
  waiting for transfers between devices  3.62 us (3%)
  other arithmetic  3.31 us (2%)
  local copies, waits for them, and re-layouts  2.77 us (2%)
    pallas_call x1, Pallas kernels, back(): pl.pallas_call(back_kernel, name='back', out_shape=jax.ShapeDtypeStruct((...  49.8 us
    pallas_call x1, Pallas kernels, front(): pl.pallas_call(functools.partial(front_kernel, d_model), name='front', ou...  42.3 us
    pallas_call x1, Pallas kernels, attend(): pl.pallas_call(attend_kernel, name='attend', grid_spec=pltpu.PrefetchScal...  31.6 us
    ppermute x1, waiting for transfers between devices, local_layer(): perm = lax.ppermute(perm, 'x', across)  3.62 us
  transfers between devices with their start and end apart: 1, of which 1 were waited for; matrix products, arithmetic and copies ran while one was open for 3% of the time, Pallas kernels for 23%

profile of v5, /device:TPU:0, one launch (start us, length us, event | category | flops | bytes accessed | tf_op | source)
XLA Modules:
  0.0 135.2 jit_solution(4234351832428811199)
XLA Ops:
  0.6 0.0 copy-start
  0.6 42.3 %front.1 = (bf16[2,16,3200]{2,1,0:T(8,128)(2,1)}, bf16[2,16,3072]{2,1,0:T(8,128)(2,1)}, f32[9,32,1536]{2,1,0:T(8,128)}, f32[3,32,1536]{2,1,0:T(8,128)}, f32[12,32,1536]{2,1,0:T(8,128)}) custom-call(bf16[2,64,768]{2,1,0:T(8,128)(2,1)} %bitcast.13, bf16[768]{0:T(1024)(128)(2,1)} %g_hbm.1, bf16[1536,3200]{1,0:T(8,128)(2,1)} %wq_hbm.1, ...), custom_call_target="tpu_custom_call" | custom-call | flops 10921967616 | bytes 85327872 | tf_op jit(solution)/shard_map/front/pallas_call | solution.py:297
  42.9 1.1 collective-permute-start
  44.0 0.0 copy-done
  44.0 1.0 fusion.2
  45.0 0.1 concatenate.14
  45.1 0.1 concatenate.15
  45.1 0.1 fusion.1
  45.3 0.7 pad_maximum_fusion.qkv_ref
  46.0 0.7 pad_maximum_fusion.1
  46.7 31.6 %attend.1 = (bf16[16,4096,128]{2,1,0:T(8,128)(2,1)}, bf16[16,4096,128]{2,1,0:T(8,128)(2,1)}, bf16[16,48,128]{2,1,0:T(8,128)(2,1)}) custom-call(s32[16]{0:T(128)} %len_ref.1, bf16[16,50,128]{2,1,0:T(8,128)(2,1)} %pad_maximum_fusion.qkv_ref, f32[16,1,128]{2,1,0:T(1,128)} %bitcast.14, f32[16,1,128]{2,1,0:T(1,128)} %bitcast.15, bf16[16,4096,128]{2,1,0:T(8,128)(2,1)} %k_ref.1, ...), custom_call_target="tpu_custom_call" | custom-call | flops 25769803776 | bytes 67108864 | tf_op jit(solution)/shard_map/attend/pallas_call | solution.py:369
  78.3 1.0 reshape.28
  79.3 0.7 copy.17
  80.0 3.6 %collective-permute-done.perm_hbm = f32[9,32,1536]{2,1,0:T(8,128)} collective-permute-done((f32[9,32,1536]{2,1,0:T(8,128)}, f32[9,32,1536]{2,1,0:T(8,128)}, u32[]{:S(2)}, u32[]{:S(2)}) %collective-permute-start) | collective-permute-done | bytes 1769504 | tf_op jit(solution)/shard_map/ppermute | solution.py:631
  83.6 49.8 %back.1 = f32[4,2,16,768]{3,2,1,0:T(8,128)} custom-call(bf16[2,16,3072]{2,1,0:T(8,128)(2,1)} %bitcast.12, bf16[2,16,3072]{2,1,0:T(8,128)(2,1)} %get-tuple-element.13.a1_hbm, f32[12,32,1536]{2,1,0:T(8,128)} %get-tuple-element.14.own_hbm, f32[9,32,1536]{2,1,0:T(8,128)} %collective-permute-done.perm_hbm, f32[3,32,1536]{2,1,0:T(8,128)} %get-tuple-element.16.send_hbm, ...), custom_call_target="tpu_custom_call" | custom-call | flops 6039797760 | bytes 47185920 | tf_op jit(solution)/shard_map/back/pallas_call | solution.py:583
  133.5 1.8 %fusion = bf16[128,768]{1,0:T(8,128)(2,1)} fusion(f32[4,2,16,768]{3,2,1,0:T(8,128)} %back.1, bf16[128,768]{1,0:T(8,128)(2,1)} %param.10), kind=kLoop, calls=%fused_computation.1 | loop fusion | flops 294912 | bytes 786432 | tf_op jit(solution)/shard_map/convert_element_type | solution.py:605
  (2 shorter events, 0.0 us)
Async XLA Ops:
  0.6 43.4 %copy-start = (s32[16]{0:T(128)S(1)}, s32[16]{0:T(128)}, u32[]{:S(2)}) copy-start(s32[16]{0:T(128)} %len_ref.1) | copy-start | bytes 196
  42.9 40.7 %collective-permute-start = (f32[9,32,1536]{2,1,0:T(8,128)}, f32[9,32,1536]{2,1,0:T(8,128)}, u32[]{:S(2)}, u32[]{:S(2)}) collective-permute-start(f32[9,32,1536]{2,1,0:T(8,128)} %get-tuple-element.15), channel_id=1, source_target_pairs={{0,2},{1,3},{2,0},{3,1},{4,6},{5,7},{6,4},{7,5}} | collective-permute-start | bytes 5308424 | tf_op jit(solution)/shard_map/ppermute | solution.py:631

commit v6 on v5

--- a/solution.py
+++ b/solution.py
@@ -14,10 +14,11 @@
 
 C = 768
 CQ = 640
+PER_STEP = 2
 SLOTS = 3
-N1 = 4
+N1 = 5
 N2 = 13
-PIECES = (3, 3, 3, 2, 1)
+PIECES = (3, 3, 2, 2, 1)
 
 
 def remote(src, dst, send_sem, recv_sem, device):
@@ -339,44 +340,45 @@
 
 
 def attend_kernel(len_ref, qkv_ref, cos_ref, sin_ref, k_ref, v_ref, ko_ref, vo_ref, o_ref):
-    pos = len_ref[pl.program_id(0)]
-    qkv = qkv_ref[0]
-    heads, head_dim = qkv.shape[0] - 2, qkv.shape[1]
-    wide = qkv.astype(F32)
-    turned = (wide * cos_ref[0] + pltpu.roll(wide, head_dim // 2, 1) * sin_ref[0]).astype(BF16)
-    query = turned[:heads]
     ko_ref[...] = k_ref[...]
     vo_ref[...] = v_ref[...]
-    base = pl.multiple_of((pos // 16) * 16, 16)
-    here = lax.broadcasted_iota(jnp.int32, (16, head_dim), 0) == pos - base
-    for out, new in ((ko_ref, turned[heads:heads + 1]), (vo_ref, qkv[heads + 1:heads + 2])):
-        tile = out[0, pl.ds(base, 16), :].astype(F32)
-        out[0, pl.ds(base, 16), :] = jnp.where(here, new.astype(F32), tile).astype(BF16)
-    scores = lax.dot_general(query, ko_ref[0], (((1,), (1,)), ((), ())), preferred_element_type=F32)
-    scores = scores * head_dim ** -0.5
-    at = lax.broadcasted_iota(jnp.int32, scores.shape, 1)
-    scores = jnp.where(at <= pos, scores, -1e30)
-    weight = jnp.exp(scores - jnp.max(scores, axis=1, keepdims=True))
-    probs = (weight / jnp.sum(weight, axis=1, keepdims=True)).astype(BF16)
-    o_ref[0] = jnp.dot(probs, vo_ref[0], preferred_element_type=F32).astype(BF16)
+    for n in range(PER_STEP):
+        pos = len_ref[pl.program_id(0) * PER_STEP + n]
+        qkv = qkv_ref[n]
+        heads, head_dim = qkv.shape[0] - 2, qkv.shape[1]
+        wide = qkv.astype(F32)
+        turned = (wide * cos_ref[n] + pltpu.roll(wide, head_dim // 2, 1) * sin_ref[n]).astype(BF16)
+        query = turned[:heads]
+        base = pl.multiple_of((pos // 16) * 16, 16)
+        here = lax.broadcasted_iota(jnp.int32, (16, head_dim), 0) == pos - base
+        for out, new in ((ko_ref, turned[heads:heads + 1]), (vo_ref, qkv[heads + 1:heads + 2])):
+            tile = out[n, pl.ds(base, 16), :].astype(F32)
+            out[n, pl.ds(base, 16), :] = jnp.where(here, new.astype(F32), tile).astype(BF16)
+        scores = lax.dot_general(query, ko_ref[n], (((1,), (1,)), ((), ())), preferred_element_type=F32)
+        scores = scores * head_dim ** -0.5
+        at = lax.broadcasted_iota(jnp.int32, scores.shape, 1)
+        scores = jnp.where(at <= pos, scores, -1e30)
+        weight = jnp.exp(scores - jnp.max(scores, axis=1, keepdims=True))
+        probs = (weight / jnp.sum(weight, axis=1, keepdims=True)).astype(BF16)
+        o_ref[n] = jnp.dot(probs, vo_ref[n], preferred_element_type=F32).astype(BF16)
 
 
 def attend(qkv, cos, sin, k_cache, v_cache, ctx_len):
     reqs, length, head_dim = k_cache.shape
     heads = qkv.shape[1] - 2
-    cache_spec = pl.BlockSpec((1, length, head_dim), lambda i, lens: (i, 0, 0))
-    table_spec = pl.BlockSpec((1, 1, head_dim), lambda i, lens: (i, 0, 0))
+    cache_spec = pl.BlockSpec((PER_STEP, length, head_dim), lambda i, lens: (i, 0, 0))
+    table_spec = pl.BlockSpec((PER_STEP, 1, head_dim), lambda i, lens: (i, 0, 0))
     return pl.pallas_call(
         attend_kernel,
         name="attend",
         grid_spec=pltpu.PrefetchScalarGridSpec(
             num_scalar_prefetch=1,
-            grid=(reqs,),
+            grid=(reqs // PER_STEP,),
             in_specs=[
-                pl.BlockSpec((1, heads + 2, head_dim), lambda i, lens: (i, 0, 0)),
+                pl.BlockSpec((PER_STEP, heads + 2, head_dim), lambda i, lens: (i, 0, 0)),
                 table_spec, table_spec, cache_spec, cache_spec,
             ],
-            out_specs=[cache_spec, cache_spec, pl.BlockSpec((1, heads, head_dim), lambda i, lens: (i, 0, 0))],
+            out_specs=[cache_spec, cache_spec, pl.BlockSpec((PER_STEP, heads, head_dim), lambda i, lens: (i, 0, 0))],
         ),
         out_shape=(
             jax.ShapeDtypeStruct(k_cache.shape, BF16),

time: 136 us -> 133 us (0.978)
    pallas_call x1, Pallas kernels: 31.6 us -> 28.3 us  [attend(): pl.pallas_call(attend_kernel, name='attend', grid_spec=pltpu.PrefetchScal...]
    pallas_call x1, Pallas kernels: 42.3 us -> 45.3 us  [front(): pl.pallas_call(functools.partial(front_kernel, d_model), name='front', ou...]
  transfers between devices with their start and end apart: 1 -> 1, of which waited for: 1 -> 1; matrix products, arithmetic and copies ran while one was open for 3% -> 3% of each run, Pallas kernels for 23% -> 21%
where the time goes in v6:
time: 133 us
  Pallas kernels  123 us (92%)
  other arithmetic  3.31 us (2%)
  local copies, waits for them, and re-layouts  2.77 us (2%)
  waiting for transfers between devices  2.45 us (2%)
    pallas_call x1, Pallas kernels, back(): pl.pallas_call(back_kernel, name='back', out_shape=jax.ShapeDtypeStruct((...  49.4 us
    pallas_call x1, Pallas kernels, front(): pl.pallas_call(functools.partial(front_kernel, d_model), name='front', ou...  45.3 us
    pallas_call x1, Pallas kernels, attend(): pl.pallas_call(attend_kernel, name='attend', grid_spec=pltpu.PrefetchScal...  28.3 us
  transfers between devices with their start and end apart: 1, of which 1 were waited for; matrix products, arithmetic and copies ran while one was open for 3% of the time, Pallas kernels for 21%

profile of v6, /device:TPU:0, one launch (start us, length us, event | category | flops | bytes accessed | tf_op | source)
XLA Modules:
  0.0 133.2 jit_solution(2888458441184007498)
XLA Ops:
  0.6 0.0 copy-start
  0.6 45.3 %front.1 = (bf16[2,16,3200]{2,1,0:T(8,128)(2,1)}, bf16[2,16,3840]{2,1,0:T(8,128)(2,1)}, f32[8,32,1536]{2,1,0:T(8,128)}, f32[3,32,1536]{2,1,0:T(8,128)}, f32[11,32,1536]{2,1,0:T(8,128)}) custom-call(bf16[2,64,768]{2,1,0:T(8,128)(2,1)} %bitcast.13, bf16[768]{0:T(1024)(128)(2,1)} %g_hbm.1, bf16[1536,3200]{1,0:T(8,128)(2,1)} %wq_hbm.1, ...), custom_call_target="tpu_custom_call" | custom-call | flops 10921967616 | bytes 85327872 | tf_op jit(solution)/shard_map/front/pallas_call | solution.py:298
  45.9 1.0 collective-permute-start
  46.9 0.0 copy-done
  46.9 1.0 fusion.2
  47.9 0.1 concatenate.14
  48.0 0.1 concatenate.15
  48.0 0.1 fusion.1
  48.1 0.7 pad_maximum_fusion.qkv_ref
  48.9 0.7 pad_maximum_fusion.1
  49.6 28.3 %attend.1 = (bf16[16,4096,128]{2,1,0:T(8,128)(2,1)}, bf16[16,4096,128]{2,1,0:T(8,128)(2,1)}, bf16[16,48,128]{2,1,0:T(8,128)(2,1)}) custom-call(s32[16]{0:T(128)} %len_ref.1, bf16[16,50,128]{2,1,0:T(8,128)(2,1)} %pad_maximum_fusion.qkv_ref, f32[16,1,128]{2,1,0:T(1,128)} %bitcast.14, f32[16,1,128]{2,1,0:T(1,128)} %bitcast.15, bf16[16,4096,128]{2,1,0:T(8,128)(2,1)} %k_ref.1, ...), custom_call_target="tpu_custom_call" | custom-call | flops 25769803776 | bytes 67108864 | tf_op jit(solution)/shard_map/attend/pallas_call | solution.py:371
  77.9 1.0 reshape.28
  78.9 0.7 copy.17
  79.6 2.5 %collective-permute-done.perm_hbm = f32[8,32,1536]{2,1,0:T(8,128)} collective-permute-done((f32[8,32,1536]{2,1,0:T(8,128)}, f32[8,32,1536]{2,1,0:T(8,128)}, u32[]{:S(2)}, u32[]{:S(2)}) %collective-permute-start) | collective-permute-done | bytes 1572896 | tf_op jit(solution)/shard_map/ppermute | solution.py:633
  82.0 49.4 %back.1 = f32[4,2,16,768]{3,2,1,0:T(8,128)} custom-call(bf16[2,16,3072]{2,1,0:T(8,128)(2,1)} %bitcast.12, bf16[2,16,3840]{2,1,0:T(8,128)(2,1)} %get-tuple-element.13.a1_hbm, f32[11,32,1536]{2,1,0:T(8,128)} %get-tuple-element.14.own_hbm, f32[8,32,1536]{2,1,0:T(8,128)} %collective-permute-done.perm_hbm, f32[3,32,1536]{2,1,0:T(8,128)} %get-tuple-element.16.send_hbm, ...), custom_call_target="tpu_custom_call" | custom-call | flops 6039797760 | bytes 47185920 | tf_op jit(solution)/shard_map/back/pallas_call | solution.py:585
  131.4 1.8 %fusion = bf16[128,768]{1,0:T(8,128)(2,1)} fusion(f32[4,2,16,768]{3,2,1,0:T(8,128)} %back.1, bf16[128,768]{1,0:T(8,128)(2,1)} %param.10), kind=kLoop, calls=%fused_computation.1 | loop fusion | flops 294912 | bytes 786432 | tf_op jit(solution)/shard_map/convert_element_type | solution.py:607
  (2 shorter events, 0.0 us)
Async XLA Ops:
  0.6 46.3 %copy-start = (s32[16]{0:T(128)S(1)}, s32[16]{0:T(128)}, u32[]{:S(2)}) copy-start(s32[16]{0:T(128)} %len_ref.1) | copy-start | bytes 196
  45.9 36.1 %collective-permute-start = (f32[8,32,1536]{2,1,0:T(8,128)}, f32[8,32,1536]{2,1,0:T(8,128)}, u32[]{:S(2)}, u32[]{:S(2)}) collective-permute-start(f32[8,32,1536]{2,1,0:T(8,128)} %get-tuple-element.15), channel_id=1, source_target_pairs={{0,2},{1,3},{2,0},{3,1},{4,6},{5,7},{6,4},{7,5}} | collective-permute-start | bytes 4718600 | tf_op jit(solution)/shard_map/ppermute | solution.py:633

commit v7 on v6

--- a/solution.py
+++ b/solution.py
@@ -18,6 +18,7 @@
 SLOTS = 3
 N1 = 5
 N2 = 13
+FULL = 5
 PIECES = (3, 3, 2, 2, 1)
 
 
@@ -43,10 +44,10 @@
 
 def front_kernel(
     d_model, x_hbm, g_hbm, wq_hbm, wg_hbm, wu_hbm,
-    qkv_hbm, a_hbm, perm_hbm, send_hbm, own_hbm,
-    stat, xbuf, gain, gbuf, moments, h, wq, wg, wu, pq, rq, xq, qs, qd, p, r, xr, a,
+    qkv_hbm, got_hbm, perm_hbm, send_hbm, own_hbm,
+    stat, xbuf, gain, gbuf, moments, h, wq, wg, wu, pq, rq, xq, qs, qd, p, r,
     in_sem, wq_sem, wg_sem, wu_sem, st_s, st_r, xg_s, xg_r,
-    dq_s, dq_r, xq_s, xq_r, yq_s, yq_r, d_s, d_r, x_s, x_r, out_sem, own_sem, q_sem, a_sem,
+    dq_s, dq_r, xq_s, xq_r, yq_s, yq_r, d_s, d_r, x_s, x_r, out_sem, own_sem, q_sem,
 ):
     xi, yi, sib, xn, sibn, yn = places()
     me = yi * 4 + xi
@@ -175,7 +176,7 @@
         return remote(p.at[i, src], r.at[i, k], d_s.at[i, k], d_r.at[i, k], sib_dev)
 
     def x_send(i):
-        return remote(p.at[i, xn], xr.at[i], x_s.at[i], x_r.at[i], xn_dev)
+        return remote(p.at[i, xn], got_hbm.at[i], x_s.at[i], x_r.at[i], xn_dev)
 
     def perm_copy(i):
         return pltpu.make_async_copy(p.at[i, xn], perm_hbm.at[i - N1], out_sem.at[i])
@@ -184,7 +185,7 @@
         return pltpu.make_async_copy(p.at[i, xn], send_hbm.at[i - N2], out_sem.at[i])
 
     def own_copy(i):
-        return pltpu.make_async_copy(p.at[i, xi], own_hbm.at[i - N1], own_sem.at[i])
+        return pltpu.make_async_copy(p.at[i, xi], own_hbm.at[i], own_sem.at[i])
 
     def chip_sum(i):
         d_copy(i, 1).wait_recv()
@@ -206,10 +207,7 @@
         d_copy(i, 0).wait_recv()
         d_copy(i, 0).wait_send()
         p[i, xi] = p[i, xi] + r[i, 0]
-
-        @pl.when(i >= N1)
-        def _():
-            own_copy(i).start()
+        own_copy(i).start()
 
     def product(i):
         slot = i % SLOTS
@@ -258,15 +256,6 @@
     q_out = pltpu.make_async_copy(qd, qkv_hbm, q_sem)
     q_out.start()
 
-    @pl.loop(0, N1)
-    def _(i):
-        x_send(i).wait_recv()
-        x_send(i).wait_send()
-        act = activation(p[i, xi] + xr[i])
-        a[:, :, pl.ds(pl.multiple_of(i * C, C), C)] = act.reshape(2, rows // 8, C)
-
-    a_out = pltpu.make_async_copy(a, a_hbm, a_sem)
-    a_out.start()
     for k in range(7):
         stat_copy(k, me).wait_send()
     g_copy(yi).wait_send()
@@ -274,18 +263,23 @@
         copy.wait_send()
     yq_copy(yi).wait_send()
 
+    @pl.loop(0, num_c)
+    def _(i):
+        own_copy(i).wait()
+
     @pl.loop(N1, N2)
     def _(i):
         perm_copy(i).wait()
-        own_copy(i).wait()
 
     @pl.loop(N2, num_c)
     def _(i):
         send_copy(i).wait()
-        own_copy(i).wait()
 
     q_out.wait()
-    a_out.wait()
+
+    @pl.loop(0, N1)
+    def _(i):
+        x_send(i).wait()
 
 
 def front(x_loc, gain_loc, wqkv, wgate, wup, d_model):
@@ -300,10 +294,10 @@
         name="front",
         out_shape=(
             jax.ShapeDtypeStruct((2, rows // 8, q_cols), BF16),
-            jax.ShapeDtypeStruct((2, rows // 8, N1 * C), BF16),
+            jax.ShapeDtypeStruct((N1, quarter, 2 * C), F32),
             jax.ShapeDtypeStruct((N2 - N1, quarter, 2 * C), F32),
             jax.ShapeDtypeStruct((num_c - N2, quarter, 2 * C), F32),
-            jax.ShapeDtypeStruct((num_c - N1, quarter, 2 * C), F32),
+            jax.ShapeDtypeStruct((num_c, quarter, 2 * C), F32),
         ),
         in_specs=[any_spec] * 5,
         out_specs=(any_spec,) * 5,
@@ -324,11 +318,9 @@
             pltpu.VMEM((2, rows // 8, q_cols), BF16),
             pltpu.VMEM((num_c, 4, quarter, 2 * C), F32),
             pltpu.VMEM((num_c, 2, quarter, 2 * C), F32),
-            pltpu.VMEM((N1, quarter, 2 * C), F32),
-            pltpu.VMEM((2, rows // 8, N1 * C), BF16),
             dma((2,)), dma((num_q,)), dma((SLOTS,)), dma((SLOTS,)), dma((7,)), dma((7,)), dma((3,)), dma((3,)),
             dma((num_q, 2)), dma((num_q, 2)), dma((num_q,)), dma((num_q,)), dma, dma,
-            dma((num_c, 2)), dma((num_c, 2)), dma((N1,)), dma((N1,)), dma((num_c,)), dma((num_c,)), dma, dma,
+            dma((num_c, 2)), dma((num_c, 2)), dma((N1,)), dma((N1,)), dma((num_c,)), dma((num_c,)), dma,
         ],
         compiler_params=pltpu.CompilerParams(collective_id=0, has_side_effects=True, vmem_limit_bytes=VMEM_LIMIT),
         cost_estimate=pl.CostEstimate(
@@ -395,21 +387,19 @@
 
 
 def back_kernel(
-    o_hbm, a1_hbm, own_hbm, perm_hbm, send_hbm, wao_hbm, wmo_hbm, z_hbm,
-    w, own, xr, act, z, zr,
-    in_sem, out_sem, w_sem, own_sem, x_s, x_r, o_s, o_r, sib_s, sib_r, xn_s, xn_r, fwd_s, fwd_r, z_s, z_r,
+    o_hbm, own_hbm, got_hbm, perm_hbm, send_hbm, wao_hbm, wmo_hbm, z_out,
+    w, own, xr, xs, act, z, zr,
+    in_sem, w_sem, own_sem, x_s, x_r, o_s, o_r, sib_s, sib_r, xn_s, xn_r, fwd_s, fwd_r, z_s, z_r,
 ):
     xi, yi, sib, xn, _, yn = places()
     sib_dev, xn_dev, yn_dev = {"x": sib}, {"x": xn}, {"yz": yn}
-    width = z_hbm.shape[3]
+    width = z_out.shape[3]
     half_rows = act.shape[1] * act.shape[2]
     num_o, num_c = wao_hbm.shape[0] // C, wmo_hbm.shape[0] // C
     num_k = num_o + num_c
     o_cols = wao_hbm.shape[0]
-    late = num_c - N1
-    here = N2 - N1
     pieces = len(PIECES)
-    starts = [sum(PIECES[:n]) for n in range(pieces + 1)]
+    starts = [FULL + sum(PIECES[:n]) for n in range(pieces + 1)]
 
     def w_copy(k):
         src = wao_hbm.at[pl.ds(k * C, C), :] if k < num_o else wmo_hbm.at[pl.ds((k - num_o) * C, C), :]
@@ -418,23 +408,26 @@
     def own_copy(i):
         return pltpu.make_async_copy(own_hbm.at[i], own.at[i], own_sem.at[i])
 
-    def perm_copy(i):
-        return pltpu.make_async_copy(perm_hbm.at[i], xr.at[i], x_r.at[i])
+    def here_copy(i):
+        src = got_hbm.at[i] if i < N1 else perm_hbm.at[i - N1]
+        return pltpu.make_async_copy(src, xr.at[i], x_r.at[i])
 
     def x_send(i):
-        return remote(send_hbm.at[i - here], xr.at[i], x_s.at[i - here], x_r.at[i], xn_dev)
+        return remote(xs.at[i - N2], xr.at[i], x_s.at[i - N2], x_r.at[i], xn_dev)
 
     barrier = pltpu.get_barrier_semaphore()
     for dev in (sib_dev, xn_dev, yn_dev):
         pl.semaphore_signal(barrier, inc=1, device_id=dev, device_id_type=MESH)
+    xs_in = pltpu.make_async_copy(send_hbm, xs, in_sem.at[1])
+    xs_in.start()
     o_in = pltpu.make_async_copy(o_hbm.at[yi], act.at[yi, xi, :, 0:o_cols], in_sem.at[0])
-    a1_in = pltpu.make_async_copy(a1_hbm, act.at[:, xi, :, pl.ds(o_cols, N1 * C)], in_sem.at[1])
     o_in.start()
-    a1_in.start()
-    for i in range(late):
+    for i in range(N2):
         own_copy(i).start()
-    for i in range(here):
-        perm_copy(i).start()
+        here_copy(i).start()
+    for i in range(N2, num_c):
+        own_copy(i).start()
+    xs_in.wait()
     pl.semaphore_wait(barrier, 3)
 
     def o_copy(half, row):
@@ -442,11 +435,11 @@
 
     def block_of(e, owner):
         if e == 0:
-            return act.at[:, owner, :, pl.ds(o_cols, N1 * C)]
+            return act.at[:, owner, :, pl.ds(o_cols, FULL * C)]
         if e == 1:
             return act.at[:, owner, :, pl.ds(0, o_cols)]
         half, n = divmod(e - 2, pieces)
-        return act.at[half, owner, :, pl.ds(o_cols + (N1 + starts[n]) * C, PIECES[n] * C)]
+        return act.at[half, owner, :, pl.ds(o_cols + starts[n] * C, PIECES[n] * C)]
 
     def to_sib(e, owner):
         block = block_of(e, owner)
@@ -475,7 +468,7 @@
     def activate(i):
         own_copy(i).wait()
         value = activation(own[i] + xr[i])
-        start = pl.multiple_of(o_cols + (N1 + i) * C, C)
+        start = pl.multiple_of(o_cols + i * C, C)
         act[:, xi, :, pl.ds(start, C)] = value.reshape(2, value.shape[0] // 2, C)
 
     def w_wait(k):
@@ -490,8 +483,16 @@
                 prod = jnp.dot(lhs, w[k, :, b * width:(b + 1) * width], preferred_element_type=F32)
                 z[b] = z[b] + prod.reshape(z.shape[1:])
 
+    def multiply_one(half, n, b):
+        @pl.loop(num_o + starts[n], num_o + starts[n + 1])
+        def _(k):
+            lhs = act[half, :, :, pl.ds(pl.multiple_of(k * C, C), C)].reshape(half_rows, C)
+            cols = pl.ds(pl.multiple_of(b * width, width), width)
+            prod = jnp.dot(lhs, w[k, :, cols], preferred_element_type=F32)
+            z[b, half] = z[b, half] + prod.reshape(z.shape[2:])
+
     def multiply_half(half, n):
-        @pl.loop(num_o + N1 + starts[n], num_o + N1 + starts[n + 1])
+        @pl.loop(num_o + starts[n], num_o + starts[n + 1])
         def _(k):
             if half == 0:
                 w_wait(k)
@@ -500,43 +501,40 @@
                 prod = jnp.dot(lhs, w[k, :, b * width:(b + 1) * width], preferred_element_type=F32)
                 z[b, half] = z[b, half] + prod.reshape(z.shape[2:])
 
-    first = (late - here + 1) // 2
-    for i in range(here, here + first):
+    first = (num_c - N2 + 1) // 2
+    for i in range(N2, N2 + first):
         x_send(i).start()
     o_copy(yn, yi).start()
     for k in range(num_k):
         w_copy(k).start()
     z[...] = jnp.zeros_like(z)
 
-    @pl.loop(0, here)
-    def _(i):
-        perm_copy(i).wait()
+    def start_here(i):
+        pltpu.make_async_copy(got_hbm.at[0], xr.at[i], x_r.at[i]).wait()
         activate(i)
 
-    a1_in.wait()
+    pl.loop(0, FULL)(start_here)
     o_in.wait()
     o_copy(yi, yn).wait_recv()
     send_own(1)
+    for i in range(N2 + first, num_c):
+        x_send(i).start()
     send_own(0)
-    for i in range(here + first, late):
-        x_send(i).start()
-    ready = sum(end <= here for end in starts[1:])
+    pl.loop(FULL, N2)(start_here)
+    ready = sum(end <= N2 for end in starts[1:])
     for n in range(ready):
         send_own(2 + n)
 
-    @pl.loop(here, here + first)
+    @pl.loop(N2, N2 + first)
     def _(i):
         x_send(i).wait_recv()
         activate(i)
 
     pass_on(1)
-    pass_on(0)
     arrived(1)
     multiply(0, num_o)
-    arrived(0)
-    multiply(num_o, N1)
-
-    @pl.loop(here + first, late)
+
+    @pl.loop(N2 + first, num_c)
     def _(i):
         x_send(i).wait_recv()
         activate(i)
@@ -544,6 +542,9 @@
     groups = 2 + 2 * pieces
     for e in range(2 + ready, groups):
         send_own(e)
+    pass_on(0)
+    arrived(0)
+    multiply(num_o, FULL)
     z_copies = [remote(z.at[yn, half], zr.at[half], z_s.at[half], z_r.at[half], yn_dev) for half in range(2)]
     pass_on(2)
     for e in range(2, groups):
@@ -551,9 +552,13 @@
             pass_on(e + 1)
         arrived(e)
         half, n = divmod(e - 2, pieces)
-        multiply_half(half, n)
+        if e + 1 < groups:
+            multiply_half(half, n)
+        else:
+            multiply_one(half, n, yn)
         if n == pieces - 1:
             z_copies[half].start()
+    multiply_one(1, pieces - 1, yi)
 
     o_copy(yn, yi).wait_send()
     for e in range(groups):
@@ -561,23 +566,19 @@
         to_sib(e, xi).wait_send()
         forward(e, xn).wait_send()
 
-    @pl.loop(here, late)
+    @pl.loop(N2, num_c)
     def _(i):
         x_send(i).wait_send()
 
-    outs = [pltpu.make_async_copy(zr.at[half], z_hbm.at[:, half], out_sem.at[half]) for half in range(2)]
     for half in range(2):
         z_copies[half].wait()
-        zr[half] = z[yi, half] + zr[half]
-        outs[half].start()
-    for half in range(2):
-        outs[half].wait()
-
-
-def back(x_loc, o_halves, a1, own, perm, send, wao, wmo):
+        z_out[:, half] = z[yi, half] + zr[half]
+
+
+def back(x_loc, o_halves, own, got, perm, send, wao, wmo):
     rows, width = x_loc.shape
     num_o, num_c = wao.shape[0] // C, wmo.shape[0] // C
-    num_k, late = num_o + num_c, num_c - N1
+    num_k = num_o + num_c
     groups = 2 + 2 * len(PIECES)
     quarter = rows // 4
     dma = pltpu.SemaphoreType.DMA
@@ -587,15 +588,16 @@
         name="back",
         out_shape=jax.ShapeDtypeStruct((4, 2, rows // 8, width), F32),
         in_specs=[any_spec] * 7,
-        out_specs=any_spec,
+        out_specs=pl.BlockSpec(memory_space=pltpu.VMEM),
         scratch_shapes=[
             pltpu.VMEM((num_k, C, 2 * width), BF16),
-            pltpu.VMEM((late, quarter, 2 * C), F32),
-            pltpu.VMEM((late, quarter, 2 * C), F32),
+            pltpu.VMEM((num_c, quarter, 2 * C), F32),
+            pltpu.VMEM((num_c, quarter, 2 * C), F32),
+            pltpu.VMEM((num_c - N2, quarter, 2 * C), F32),
             pltpu.VMEM((2, 4, rows // 8, num_k * C), BF16),
             pltpu.VMEM((2, 2, 4, rows // 8, width), F32),
             pltpu.VMEM((2, 4, rows // 8, width), F32),
-            dma((2,)), dma((2,)), dma((num_k,)), dma((late,)), dma((num_c - N2,)), dma((late,)), dma, dma,
+            dma((2,)), dma((num_k,)), dma((num_c,)), dma((num_c - N2,)), dma((num_c,)), dma, dma,
             dma((groups,)), dma((groups,)), dma((groups,)), dma((groups,)), dma((groups,)), dma((groups,)),
             dma((2,)), dma((2,)),
         ],
@@ -603,7 +605,7 @@
         cost_estimate=pl.CostEstimate(
             flops=4 * rows * num_k * C * width, bytes_accessed=4 * num_k * C * width, transcendentals=0
         ),
-    )(o_halves, a1, own, perm, send, wao, wmo)
+    )(o_halves, own, got, perm, send, wao, wmo)
     return (x_loc.astype(F32) + z.reshape(rows, width)).astype(BF16)
 
 
@@ -627,14 +629,14 @@
         cos = jnp.concatenate([cos, cos], axis=1)[:, None, :]
         sin = jnp.concatenate([-sin, sin], axis=1)[:, None, :]
 
-        qkv, a1, perm, send, own = front(
+        qkv, got, perm, send, own = front(
             x_loc, gain_loc, wqkv_loc, wgate_loc, wup_loc, d_model
         )
         perm = lax.ppermute(perm, "x", across)
         qkv = jnp.concatenate([qkv[0], qkv[1]], axis=1).reshape(reqs, -1, head_dim)
         k_all, v_all, attn = attend(qkv, cos, sin, kc_loc, vc_loc, len_loc)
         o_halves = jnp.swapaxes(attn.reshape(reqs, 2, -1), 0, 1)
-        y_loc = back(x_loc, o_halves, a1, own, perm, send, wao_loc, wmo_loc)
+        y_loc = back(x_loc, o_halves, own, got, perm, send, wao_loc, wmo_loc)
         return y_loc, k_all, v_all
 
     in_specs = (row_spec, P(both_axes), in_w_spec, in_w_spec, in_w_spec, out_w_spec, out_w_spec, cache_spec, cache_spec, len_spec)

time: 133 us -> 136 us (1.023)
  Pallas kernels: 123 us -> 126 us
    pallas_call x1, Pallas kernels: 49.4 us -> 52.9 us  [back(): pl.pallas_call(back_kernel, name='back', out_shape=jax.ShapeDtypeStruct((...]
where the time goes in v7:
time: 136 us
  Pallas kernels  126 us (93%)
  other arithmetic  3.31 us (2%)
  local copies, waits for them, and re-layouts  2.77 us (2%)
  waiting for transfers between devices  2.55 us (2%)
    pallas_call x1, Pallas kernels, back(): pl.pallas_call(back_kernel, name='back', out_shape=jax.ShapeDtypeStruct((...  52.9 us
    pallas_call x1, Pallas kernels, front(): pl.pallas_call(functools.partial(front_kernel, d_model), name='front', ou...  44.5 us
    pallas_call x1, Pallas kernels, attend(): pl.pallas_call(attend_kernel, name='attend', grid_spec=pltpu.PrefetchScal...  28.3 us
  transfers between devices with their start and end apart: 1, of which 1 were waited for; matrix products, arithmetic and copies ran while one was open for 3% of the time, Pallas kernels for 21%

profile of v7, /device:TPU:0, one launch (start us, length us, event | category | flops | bytes accessed | tf_op | source)
XLA Modules:
  0.0 136.1 jit_solution(13408124958675097024)
XLA Ops:
  0.6 0.0 copy-start
  0.6 44.5 %front.1 = (bf16[2,16,3200]{2,1,0:T(8,128)(2,1)}, f32[5,32,1536]{2,1,0:T(8,128)}, f32[8,32,1536]{2,1,0:T(8,128)}, f32[3,32,1536]{2,1,0:T(8,128)}, f32[16,32,1536]{2,1,0:T(8,128)}) custom-call(bf16[2,64,768]{2,1,0:T(8,128)(2,1)} %bitcast.13, bf16[768]{0:T(1024)(128)(2,1)} %g_hbm.1, bf16[1536,3200]{1,0:T(8,128)(2,1)} %wq_hbm.1, bf16[1536,12288]{1,0:T(8,128)(2,1)} %wg_hbm.1, ...), custom_call_target="tpu_custom_call" | custom-call | flops 10921967616 | bytes 85327872 | tf_op jit(solution)/shard_map/front/pallas_call | solution.py:292
  45.2 1.0 collective-permute-start
  46.1 0.0 copy-done
  46.2 1.0 fusion.2
  47.1 0.1 concatenate.14
  47.2 0.1 concatenate.15
  47.3 0.1 fusion.1
  47.4 0.7 pad_maximum_fusion.qkv_ref
  48.1 0.7 pad_maximum_fusion.1
  48.8 28.3 %attend.1 = (bf16[16,4096,128]{2,1,0:T(8,128)(2,1)}, bf16[16,4096,128]{2,1,0:T(8,128)(2,1)}, bf16[16,48,128]{2,1,0:T(8,128)(2,1)}) custom-call(s32[16]{0:T(128)} %len_ref.1, bf16[16,50,128]{2,1,0:T(8,128)(2,1)} %pad_maximum_fusion.qkv_ref, f32[16,1,128]{2,1,0:T(1,128)} %bitcast.14, f32[16,1,128]{2,1,0:T(1,128)} %bitcast.15, bf16[16,4096,128]{2,1,0:T(8,128)(2,1)} %k_ref.1, ...), custom_call_target="tpu_custom_call" | custom-call | flops 25769803776 | bytes 67108864 | tf_op jit(solution)/shard_map/attend/pallas_call | solution.py:363
  77.1 1.0 reshape.28
  78.1 0.7 copy.17
  78.8 2.6 %collective-permute-done.perm_hbm = f32[8,32,1536]{2,1,0:T(8,128)} collective-permute-done((f32[8,32,1536]{2,1,0:T(8,128)}, f32[8,32,1536]{2,1,0:T(8,128)}, u32[]{:S(2)}, u32[]{:S(2)}) %collective-permute-start) | collective-permute-done | bytes 1572896 | tf_op jit(solution)/shard_map/ppermute | solution.py:635
  81.4 52.9 %back.1 = f32[4,2,16,768]{3,2,1,0:T(8,128)} custom-call(bf16[2,16,3072]{2,1,0:T(8,128)(2,1)} %bitcast.12, f32[16,32,1536]{2,1,0:T(8,128)} %get-tuple-element.13.own_hbm, f32[5,32,1536]{2,1,0:T(8,128)} %get-tuple-element.14.got_hbm, f32[8,32,1536]{2,1,0:T(8,128)} %collective-permute-done.perm_hbm, f32[3,32,1536]{2,1,0:T(8,128)} %get-tuple-element.16.send_hbm, ...), custom_call_target="tpu_custom_call" | custom-call | flops 6039797760 | bytes 47185920 | tf_op jit(solution)/shard_map/back/pallas_call | solution.py:586
  134.3 1.8 %fusion = bf16[128,768]{1,0:T(8,128)(2,1)} fusion(f32[4,2,16,768]{3,2,1,0:T(8,128)} %back.1, bf16[128,768]{1,0:T(8,128)(2,1)} %param.10), kind=kLoop, calls=%fused_computation.1 | loop fusion | flops 294912 | bytes 786432 | tf_op jit(solution)/shard_map/convert_element_type | solution.py:609
  (2 shorter events, 0.0 us)
Async XLA Ops:
  0.6 45.5 %copy-start = (s32[16]{0:T(128)S(1)}, s32[16]{0:T(128)}, u32[]{:S(2)}) copy-start(s32[16]{0:T(128)} %len_ref.1) | copy-start | bytes 196
  45.2 36.2 %collective-permute-start = (f32[8,32,1536]{2,1,0:T(8,128)}, f32[8,32,1536]{2,1,0:T(8,128)}, u32[]{:S(2)}, u32[]{:S(2)}) collective-permute-start(f32[8,32,1536]{2,1,0:T(8,128)} %get-tuple-element.15), channel_id=1, source_target_pairs={{0,2},{1,3},{2,0},{3,1},{4,6},{5,7},{6,4},{7,5}} | collective-permute-start | bytes 4718600 | tf_op jit(solution)/shard_map/ppermute | solution.py:635

commit v8 on v7

--- a/solution.py
+++ b/solution.py
@@ -96,11 +96,9 @@
         dev = {"yz": (yi + dy) % 2, "x": (xi + dx) % 4}
         return remote(stat.at[slot], stat.at[slot], st_s.at[k], st_r.at[k], dev)
 
-    def x_copies(slot):
-        return [
-            remote(xbuf.at[slot, side], xbuf.at[slot, side], xg_s.at[1 + n], xg_r.at[1 + n], yn_dev)
-            for n, side in enumerate((far, near))
-        ]
+    def x_copy(slot, n):
+        block = xbuf.at[slot, (far, near)[n]]
+        return remote(block, block, xg_s.at[1 + n], xg_r.at[1 + n], yn_dev)
 
     def g_copy(slot):
         return remote(gbuf.at[slot], gbuf.at[slot], xg_s.at[0], xg_r.at[0], yn_dev)
@@ -108,8 +106,8 @@
     for k in range(7):
         stat_copy(k, me).start()
     g_copy(yi).start()
-    for copy in x_copies(yi):
-        copy.start()
+    x_copy(yi, 0).start()
+    x_copy(yi, 1).start()
     for c in range(num_q):
         wq_copy(c).start()
     for i in range(SLOTS):
@@ -149,7 +147,7 @@
         pq[c, xn] = pq[c, xn] + rq[c, 1]
         xq_copy(c).start()
 
-    x_copies(yn)[0].wait_recv()
+    x_copy(yn, 0).wait_recv()
     normalize(far)
 
     @pl.loop(0, num_q)
@@ -162,7 +160,7 @@
         def _():
             q_send(c - 1)
 
-    x_copies(yn)[1].wait_recv()
+    x_copy(yn, 1).wait_recv()
     normalize(near)
     q_send(num_q - 1)
 
@@ -259,8 +257,8 @@
     for k in range(7):
         stat_copy(k, me).wait_send()
     g_copy(yi).wait_send()
-    for copy in x_copies(yi):
-        copy.wait_send()
+    x_copy(yi, 0).wait_send()
+    x_copy(yi, 1).wait_send()
     yq_copy(yi).wait_send()
 
     @pl.loop(0, num_c)
@@ -468,7 +466,7 @@
     def activate(i):
         own_copy(i).wait()
         value = activation(own[i] + xr[i])
-        start = pl.multiple_of(o_cols + i * C, C)
+        start = o_cols + i * C if isinstance(i, int) else pl.multiple_of(o_cols + i * C, C)
         act[:, xi, :, pl.ds(start, C)] = value.reshape(2, value.shape[0] // 2, C)
 
     def w_wait(k):
@@ -505,8 +503,14 @@
     for i in range(N2, N2 + first):
         x_send(i).start()
     o_copy(yn, yi).start()
-    for k in range(num_k):
-        w_copy(k).start()
+    unread = list(range(num_k))
+
+    def read_weights(count):
+        for k in unread[:count]:
+            w_copy(k).start()
+        del unread[:count]
+
+    read_weights(2)
     z[...] = jnp.zeros_like(z)
 
     def start_here(i):
@@ -520,29 +524,31 @@
     for i in range(N2 + first, num_c):
         x_send(i).start()
     send_own(0)
+    read_weights(2)
     pl.loop(FULL, N2)(start_here)
     ready = sum(end <= N2 for end in starts[1:])
     for n in range(ready):
         send_own(2 + n)
-
-    @pl.loop(N2, N2 + first)
-    def _(i):
+    read_weights(2)
+    for i in range(N2, N2 + first):
         x_send(i).wait_recv()
         activate(i)
-
+        read_weights(2)
     pass_on(1)
+    read_weights(2)
     arrived(1)
     multiply(0, num_o)
-
-    @pl.loop(N2 + first, num_c)
-    def _(i):
+    read_weights(2)
+
+    for i in range(N2 + first, num_c):
         x_send(i).wait_recv()
         activate(i)
-
+        read_weights(2)
     groups = 2 + 2 * pieces
     for e in range(2 + ready, groups):
         send_own(e)
     pass_on(0)
+    read_weights(num_k)
     arrived(0)
     multiply(num_o, FULL)
     z_copies = [remote(z.at[yn, half], zr.at[half], z_s.at[half], z_r.at[half], yn_dev) for half in range(2)]

time: 136 us -> 136 us (level)
  no operation moved by 1% of the time
where the time goes in v8:
time: 136 us
  Pallas kernels  126 us (93%)
  other arithmetic  3.31 us (2%)
  local copies, waits for them, and re-layouts  2.77 us (2%)
  waiting for transfers between devices  2.55 us (2%)
    pallas_call x1, Pallas kernels, back(): pl.pallas_call(back_kernel, name='back', out_shape=jax.ShapeDtypeStruct((...  52.9 us
    pallas_call x1, Pallas kernels, front(): pl.pallas_call(functools.partial(front_kernel, d_model), name='front', ou...  44.5 us
    pallas_call x1, Pallas kernels, attend(): pl.pallas_call(attend_kernel, name='attend', grid_spec=pltpu.PrefetchScal...  28.3 us
  transfers between devices with their start and end apart: 1, of which 1 were waited for; matrix products, arithmetic and copies ran while one was open for 3% of the time, Pallas kernels for 21%

profile of v8, /device:TPU:0, one launch (start us, length us, event | category | flops | bytes accessed | tf_op | source)
XLA Modules:
  0.0 136.1 jit_solution(3082451188600413102)
XLA Ops:
  0.6 0.0 copy-start
  0.6 44.5 %front.1 = (bf16[2,16,3200]{2,1,0:T(8,128)(2,1)}, f32[5,32,1536]{2,1,0:T(8,128)}, f32[8,32,1536]{2,1,0:T(8,128)}, f32[3,32,1536]{2,1,0:T(8,128)}, f32[16,32,1536]{2,1,0:T(8,128)}) custom-call(bf16[2,64,768]{2,1,0:T(8,128)(2,1)} %bitcast.13, bf16[768]{0:T(1024)(128)(2,1)} %g_hbm.1, bf16[1536,3200]{1,0:T(8,128)(2,1)} %wq_hbm.1, bf16[1536,12288]{1,0:T(8,128)(2,1)} %wg_hbm.1, ...), custom_call_target="tpu_custom_call" | custom-call | flops 10921967616 | bytes 85327872 | tf_op jit(solution)/shard_map/front/pallas_call | solution.py:290
  45.2 1.0 collective-permute-start
  46.1 0.0 copy-done
  46.2 1.0 fusion.2
  47.1 0.1 concatenate.14
  47.2 0.1 concatenate.15
  47.3 0.1 fusion.1
  47.4 0.7 pad_maximum_fusion.qkv_ref
  48.1 0.7 pad_maximum_fusion.1
  48.8 28.3 %attend.1 = (bf16[16,4096,128]{2,1,0:T(8,128)(2,1)}, bf16[16,4096,128]{2,1,0:T(8,128)(2,1)}, bf16[16,48,128]{2,1,0:T(8,128)(2,1)}) custom-call(s32[16]{0:T(128)} %len_ref.1, bf16[16,50,128]{2,1,0:T(8,128)(2,1)} %pad_maximum_fusion.qkv_ref, f32[16,1,128]{2,1,0:T(1,128)} %bitcast.14, f32[16,1,128]{2,1,0:T(1,128)} %bitcast.15, bf16[16,4096,128]{2,1,0:T(8,128)(2,1)} %k_ref.1, ...), custom_call_target="tpu_custom_call" | custom-call | flops 25769803776 | bytes 67108864 | tf_op jit(solution)/shard_map/attend/pallas_call | solution.py:361
  77.1 1.0 reshape.28
  78.1 0.7 copy.17
  78.8 2.6 %collective-permute-done.perm_hbm = f32[8,32,1536]{2,1,0:T(8,128)} collective-permute-done((f32[8,32,1536]{2,1,0:T(8,128)}, f32[8,32,1536]{2,1,0:T(8,128)}, u32[]{:S(2)}, u32[]{:S(2)}) %collective-permute-start) | collective-permute-done | bytes 1572896 | tf_op jit(solution)/shard_map/ppermute | solution.py:641
  81.4 52.9 %back.1 = f32[4,2,16,768]{3,2,1,0:T(8,128)} custom-call(bf16[2,16,3072]{2,1,0:T(8,128)(2,1)} %bitcast.12, f32[16,32,1536]{2,1,0:T(8,128)} %get-tuple-element.13.own_hbm, f32[5,32,1536]{2,1,0:T(8,128)} %get-tuple-element.14.got_hbm, f32[8,32,1536]{2,1,0:T(8,128)} %collective-permute-done.perm_hbm, f32[3,32,1536]{2,1,0:T(8,128)} %get-tuple-element.16.send_hbm, ...), custom_call_target="tpu_custom_call" | custom-call | flops 6039797760 | bytes 47185920 | tf_op jit(solution)/shard_map/back/pallas_call | solution.py:592
  134.3 1.8 %fusion = bf16[128,768]{1,0:T(8,128)(2,1)} fusion(f32[4,2,16,768]{3,2,1,0:T(8,128)} %back.1, bf16[128,768]{1,0:T(8,128)(2,1)} %param.10), kind=kLoop, calls=%fused_computation.1 | loop fusion | flops 294912 | bytes 786432 | tf_op jit(solution)/shard_map/convert_element_type | solution.py:615
  (2 shorter events, 0.0 us)
Async XLA Ops:
  0.6 45.5 %copy-start = (s32[16]{0:T(128)S(1)}, s32[16]{0:T(128)}, u32[]{:S(2)}) copy-start(s32[16]{0:T(128)} %len_ref.1) | copy-start | bytes 196
  45.2 36.2 %collective-permute-start = (f32[8,32,1536]{2,1,0:T(8,128)}, f32[8,32,1536]{2,1,0:T(8,128)}, u32[]{:S(2)}, u32[]{:S(2)}) collective-permute-start(f32[8,32,1536]{2,1,0:T(8,128)} %get-tuple-element.15), channel_id=1, source_target_pairs={{0,2},{1,3},{2,0},{3,1},{4,6},{5,7},{6,4},{7,5}} | collective-permute-start | bytes 4718600 | tf_op jit(solution)/shard_map/ppermute | solution.py:641

commit v9 on v8

--- a/solution.py
+++ b/solution.py
@@ -19,7 +19,7 @@
 N1 = 5
 N2 = 13
 FULL = 5
-PIECES = (3, 3, 2, 2, 1)
+PIECES = (8, 3)
 
 
 def remote(src, dst, send_sem, recv_sem, device):
@@ -386,8 +386,8 @@
 
 def back_kernel(
     o_hbm, own_hbm, got_hbm, perm_hbm, send_hbm, wao_hbm, wmo_hbm, z_out,
-    w, own, xr, xs, act, z, zr,
-    in_sem, w_sem, own_sem, x_s, x_r, o_s, o_r, sib_s, sib_r, xn_s, xn_r, fwd_s, fwd_r, z_s, z_r,
+    w, own, xr, act, z, zr,
+    in_sem, out_sem, w_sem, own_sem, x_s, x_r, o_s, o_r, sib_s, sib_r, xn_s, xn_r, fwd_s, fwd_r, z_s, z_r,
 ):
     xi, yi, sib, xn, _, yn = places()
     sib_dev, xn_dev, yn_dev = {"x": sib}, {"x": xn}, {"yz": yn}
@@ -411,21 +411,18 @@
         return pltpu.make_async_copy(src, xr.at[i], x_r.at[i])
 
     def x_send(i):
-        return remote(xs.at[i - N2], xr.at[i], x_s.at[i - N2], x_r.at[i], xn_dev)
+        return remote(send_hbm.at[i - N2], xr.at[i], x_s.at[i - N2], x_r.at[i], xn_dev)
 
     barrier = pltpu.get_barrier_semaphore()
     for dev in (sib_dev, xn_dev, yn_dev):
         pl.semaphore_signal(barrier, inc=1, device_id=dev, device_id_type=MESH)
-    xs_in = pltpu.make_async_copy(send_hbm, xs, in_sem.at[1])
-    xs_in.start()
-    o_in = pltpu.make_async_copy(o_hbm.at[yi], act.at[yi, xi, :, 0:o_cols], in_sem.at[0])
+    o_in = pltpu.make_async_copy(o_hbm.at[yi], act.at[yi, xi, :, 0:o_cols], in_sem)
     o_in.start()
     for i in range(N2):
         own_copy(i).start()
         here_copy(i).start()
     for i in range(N2, num_c):
         own_copy(i).start()
-    xs_in.wait()
     pl.semaphore_wait(barrier, 3)
 
     def o_copy(half, row):
@@ -521,9 +518,9 @@
     o_in.wait()
     o_copy(yi, yn).wait_recv()
     send_own(1)
+    send_own(0)
     for i in range(N2 + first, num_c):
         x_send(i).start()
-    send_own(0)
     read_weights(2)
     pl.loop(FULL, N2)(start_here)
     ready = sum(end <= N2 for end in starts[1:])
@@ -576,9 +573,13 @@
     def _(i):
         x_send(i).wait_send()
 
+    outs = [pltpu.make_async_copy(zr.at[half], z_out.at[:, half], out_sem.at[half]) for half in range(2)]
     for half in range(2):
         z_copies[half].wait()
-        z_out[:, half] = z[yi, half] + zr[half]
+        zr[half] = z[yi, half] + zr[half]
+        outs[half].start()
+    for half in range(2):
+        outs[half].wait()
 
 
 def back(x_loc, o_halves, own, got, perm, send, wao, wmo):
@@ -594,16 +595,15 @@
         name="back",
         out_shape=jax.ShapeDtypeStruct((4, 2, rows // 8, width), F32),
         in_specs=[any_spec] * 7,
-        out_specs=pl.BlockSpec(memory_space=pltpu.VMEM),
+        out_specs=any_spec,
         scratch_shapes=[
             pltpu.VMEM((num_k, C, 2 * width), BF16),
             pltpu.VMEM((num_c, quarter, 2 * C), F32),
             pltpu.VMEM((num_c, quarter, 2 * C), F32),
-            pltpu.VMEM((num_c - N2, quarter, 2 * C), F32),
             pltpu.VMEM((2, 4, rows // 8, num_k * C), BF16),
             pltpu.VMEM((2, 2, 4, rows // 8, width), F32),
             pltpu.VMEM((2, 4, rows // 8, width), F32),
-            dma((2,)), dma((num_k,)), dma((num_c,)), dma((num_c - N2,)), dma((num_c,)), dma, dma,
+            dma, dma((2,)), dma((num_k,)), dma((num_c,)), dma((num_c - N2,)), dma((num_c,)), dma, dma,
             dma((groups,)), dma((groups,)), dma((groups,)), dma((groups,)), dma((groups,)), dma((groups,)),
             dma((2,)), dma((2,)),
         ],

time: 136 us -> 134 us (0.985)
  Pallas kernels: 126 us -> 123 us
    pallas_call x1, Pallas kernels: 52.9 us -> 50.3 us  [back(): pl.pallas_call(back_kernel, name='back', out_shape=jax.ShapeDtypeStruct((...]
where the time goes in v9:
time: 134 us; the launch traced here: 133 us
  Pallas kernels  123 us (92%)
  other arithmetic  3.31 us (2%)
  local copies, waits for them, and re-layouts  2.77 us (2%)
  waiting for transfers between devices  2.55 us (2%)
    pallas_call x1, Pallas kernels, back(): pl.pallas_call(back_kernel, name='back', out_shape=jax.ShapeDtypeStruct((...  50.3 us
    pallas_call x1, Pallas kernels, front(): pl.pallas_call(functools.partial(front_kernel, d_model), name='front', ou...  44.5 us
    pallas_call x1, Pallas kernels, attend(): pl.pallas_call(attend_kernel, name='attend', grid_spec=pltpu.PrefetchScal...  28.3 us
  transfers between devices with their start and end apart: 1, of which 1 were waited for; matrix products, arithmetic and copies ran while one was open for 3% of the time, Pallas kernels for 21%

profile of v9, /device:TPU:0, one launch (start us, length us, event | category | flops | bytes accessed | tf_op | source)
XLA Modules:
  0.0 133.4 jit_solution(18410336110971886242)
XLA Ops:
  0.6 0.0 copy-start
  0.6 44.5 %front.1 = (bf16[2,16,3200]{2,1,0:T(8,128)(2,1)}, f32[5,32,1536]{2,1,0:T(8,128)}, f32[8,32,1536]{2,1,0:T(8,128)}, f32[3,32,1536]{2,1,0:T(8,128)}, f32[16,32,1536]{2,1,0:T(8,128)}) custom-call(bf16[2,64,768]{2,1,0:T(8,128)(2,1)} %bitcast.13, bf16[768]{0:T(1024)(128)(2,1)} %g_hbm.1, bf16[1536,3200]{1,0:T(8,128)(2,1)} %wq_hbm.1, bf16[1536,12288]{1,0:T(8,128)(2,1)} %wg_hbm.1, ...), custom_call_target="tpu_custom_call" | custom-call | flops 10921967616 | bytes 85327872 | tf_op jit(solution)/shard_map/front/pallas_call | solution.py:290
  45.2 1.0 collective-permute-start
  46.1 0.0 copy-done
  46.2 1.0 fusion.2
  47.1 0.1 concatenate.14
  47.2 0.1 concatenate.15
  47.3 0.1 fusion.1
  47.4 0.7 pad_maximum_fusion.qkv_ref
  48.1 0.7 pad_maximum_fusion.1
  48.8 28.3 %attend.1 = (bf16[16,4096,128]{2,1,0:T(8,128)(2,1)}, bf16[16,4096,128]{2,1,0:T(8,128)(2,1)}, bf16[16,48,128]{2,1,0:T(8,128)(2,1)}) custom-call(s32[16]{0:T(128)} %len_ref.1, bf16[16,50,128]{2,1,0:T(8,128)(2,1)} %pad_maximum_fusion.qkv_ref, f32[16,1,128]{2,1,0:T(1,128)} %bitcast.14, f32[16,1,128]{2,1,0:T(1,128)} %bitcast.15, bf16[16,4096,128]{2,1,0:T(8,128)(2,1)} %k_ref.1, ...), custom_call_target="tpu_custom_call" | custom-call | flops 25769803776 | bytes 67108864 | tf_op jit(solution)/shard_map/attend/pallas_call | solution.py:361
  77.1 1.0 reshape.28
  78.1 0.7 copy.17
  78.8 2.6 %collective-permute-done.perm_hbm = f32[8,32,1536]{2,1,0:T(8,128)} collective-permute-done((f32[8,32,1536]{2,1,0:T(8,128)}, f32[8,32,1536]{2,1,0:T(8,128)}, u32[]{:S(2)}, u32[]{:S(2)}) %collective-permute-start) | collective-permute-done | bytes 1572896 | tf_op jit(solution)/shard_map/ppermute | solution.py:641
  81.4 50.3 %back.1 = f32[4,2,16,768]{3,2,1,0:T(8,128)} custom-call(bf16[2,16,3072]{2,1,0:T(8,128)(2,1)} %bitcast.12, f32[16,32,1536]{2,1,0:T(8,128)} %get-tuple-element.13.own_hbm, f32[5,32,1536]{2,1,0:T(8,128)} %get-tuple-element.14.got_hbm, f32[8,32,1536]{2,1,0:T(8,128)} %collective-permute-done.perm_hbm, f32[3,32,1536]{2,1,0:T(8,128)} %get-tuple-element.16.send_hbm, ...), custom_call_target="tpu_custom_call" | custom-call | flops 6039797760 | bytes 47185920 | tf_op jit(solution)/shard_map/back/pallas_call | solution.py:593
  131.7 1.8 %fusion = bf16[128,768]{1,0:T(8,128)(2,1)} fusion(f32[4,2,16,768]{3,2,1,0:T(8,128)} %back.1, bf16[128,768]{1,0:T(8,128)(2,1)} %param.10), kind=kLoop, calls=%fused_computation.1 | loop fusion | flops 294912 | bytes 786432 | tf_op jit(solution)/shard_map/convert_element_type | solution.py:615
  (2 shorter events, 0.0 us)
Async XLA Ops:
  0.6 45.5 %copy-start = (s32[16]{0:T(128)S(1)}, s32[16]{0:T(128)}, u32[]{:S(2)}) copy-start(s32[16]{0:T(128)} %len_ref.1) | copy-start | bytes 196
  45.2 36.2 %collective-permute-start = (f32[8,32,1536]{2,1,0:T(8,128)}, f32[8,32,1536]{2,1,0:T(8,128)}, u32[]{:S(2)}, u32[]{:S(2)}) collective-permute-start(f32[8,32,1536]{2,1,0:T(8,128)} %get-tuple-element.15), channel_id=1, source_target_pairs={{0,2},{1,3},{2,0},{3,1},{4,6},{5,7},{6,4},{7,5}} | collective-permute-start | bytes 4718600 | tf_op jit(solution)/shard_map/ppermute | solution.py:641

commit v10 on v9

--- a/solution.py
+++ b/solution.py
@@ -16,10 +16,9 @@
 CQ = 640
 PER_STEP = 2
 SLOTS = 3
-N1 = 5
-N2 = 13
+LOW, SHIFT, PERM = 4, 2, 8
 FULL = 5
-PIECES = (8, 3)
+PIECES = (7, 4)
 
 
 def remote(src, dst, send_sem, recv_sem, device):
@@ -53,6 +52,8 @@
     me = yi * 4 + xi
     sides, side_rows, width = x_hbm.shape
     rows = sides * side_rows
+    n1 = LOW + SHIFT * (xi % 2)
+    n2 = n1 + PERM
     near = xi // 2
     far = 1 - near
     num_q = wq_hbm.shape[1] // CQ
@@ -177,10 +178,10 @@
         return remote(p.at[i, xn], got_hbm.at[i], x_s.at[i], x_r.at[i], xn_dev)
 
     def perm_copy(i):
-        return pltpu.make_async_copy(p.at[i, xn], perm_hbm.at[i - N1], out_sem.at[i])
+        return pltpu.make_async_copy(p.at[i, xn], perm_hbm.at[i - n1], out_sem.at[i])
 
     def send_copy(i):
-        return pltpu.make_async_copy(p.at[i, xn], send_hbm.at[i - N2], out_sem.at[i])
+        return pltpu.make_async_copy(p.at[i, xn], send_hbm.at[i - n2], out_sem.at[i])
 
     def own_copy(i):
         return pltpu.make_async_copy(p.at[i, xi], own_hbm.at[i], own_sem.at[i])
@@ -190,15 +191,15 @@
         d_copy(i, 1).wait_send()
         p[i, xn] = p[i, xn] + r[i, 1]
 
-        @pl.when(i < N1)
+        @pl.when(i < n1)
         def _():
             x_send(i).start()
 
-        @pl.when((i >= N1) & (i < N2))
+        @pl.when((i >= n1) & (i < n2))
         def _():
             perm_copy(i).start()
 
-        @pl.when(i >= N2)
+        @pl.when(i >= n2)
         def _():
             send_copy(i).start()
 
@@ -265,17 +266,17 @@
     def _(i):
         own_copy(i).wait()
 
-    @pl.loop(N1, N2)
+    @pl.loop(n1, n2)
     def _(i):
         perm_copy(i).wait()
 
-    @pl.loop(N2, num_c)
+    @pl.loop(n2, num_c)
     def _(i):
         send_copy(i).wait()
 
     q_out.wait()
 
-    @pl.loop(0, N1)
+    @pl.loop(0, n1)
     def _(i):
         x_send(i).wait()
 
@@ -292,9 +293,9 @@
         name="front",
         out_shape=(
             jax.ShapeDtypeStruct((2, rows // 8, q_cols), BF16),
-            jax.ShapeDtypeStruct((N1, quarter, 2 * C), F32),
-            jax.ShapeDtypeStruct((N2 - N1, quarter, 2 * C), F32),
-            jax.ShapeDtypeStruct((num_c - N2, quarter, 2 * C), F32),
+            jax.ShapeDtypeStruct((LOW + SHIFT, quarter, 2 * C), F32),
+            jax.ShapeDtypeStruct((PERM, quarter, 2 * C), F32),
+            jax.ShapeDtypeStruct((num_c - LOW - PERM, quarter, 2 * C), F32),
             jax.ShapeDtypeStruct((num_c, quarter, 2 * C), F32),
         ),
         in_specs=[any_spec] * 5,
@@ -318,7 +319,7 @@
             pltpu.VMEM((num_c, 2, quarter, 2 * C), F32),
             dma((2,)), dma((num_q,)), dma((SLOTS,)), dma((SLOTS,)), dma((7,)), dma((7,)), dma((3,)), dma((3,)),
             dma((num_q, 2)), dma((num_q, 2)), dma((num_q,)), dma((num_q,)), dma, dma,
-            dma((num_c, 2)), dma((num_c, 2)), dma((N1,)), dma((N1,)), dma((num_c,)), dma((num_c,)), dma,
+            dma((num_c, 2)), dma((num_c, 2)), dma((LOW + SHIFT,)), dma((LOW + SHIFT,)), dma((num_c,)), dma((num_c,)), dma,
         ],
         compiler_params=pltpu.CompilerParams(collective_id=0, has_side_effects=True, vmem_limit_bytes=VMEM_LIMIT),
         cost_estimate=pl.CostEstimate(
@@ -396,6 +397,8 @@
     num_o, num_c = wao_hbm.shape[0] // C, wmo_hbm.shape[0] // C
     num_k = num_o + num_c
     o_cols = wao_hbm.shape[0]
+    n1 = LOW + SHIFT * (xi % 2)
+    n2 = n1 + PERM
     pieces = len(PIECES)
     starts = [FULL + sum(PIECES[:n]) for n in range(pieces + 1)]
 
@@ -406,23 +409,30 @@
     def own_copy(i):
         return pltpu.make_async_copy(own_hbm.at[i], own.at[i], own_sem.at[i])
 
-    def here_copy(i):
-        src = got_hbm.at[i] if i < N1 else perm_hbm.at[i - N1]
+    def here_copy(src, i):
         return pltpu.make_async_copy(src, xr.at[i], x_r.at[i])
 
     def x_send(i):
-        return remote(send_hbm.at[i - N2], xr.at[i], x_s.at[i - N2], x_r.at[i], xn_dev)
+        return remote(send_hbm.at[i - n2], xr.at[i], x_s.at[i - n2], x_r.at[i], xn_dev)
 
     barrier = pltpu.get_barrier_semaphore()
     for dev in (sib_dev, xn_dev, yn_dev):
         pl.semaphore_signal(barrier, inc=1, device_id=dev, device_id_type=MESH)
     o_in = pltpu.make_async_copy(o_hbm.at[yi], act.at[yi, xi, :, 0:o_cols], in_sem)
     o_in.start()
-    for i in range(N2):
+
+    @pl.loop(0, num_c)
+    def _(i):
         own_copy(i).start()
-        here_copy(i).start()
-    for i in range(N2, num_c):
-        own_copy(i).start()
+
+    @pl.loop(0, n1)
+    def _(i):
+        here_copy(got_hbm.at[i], i).start()
+
+    @pl.loop(n1, n2)
+    def _(i):
+        here_copy(perm_hbm.at[i - n1], i).start()
+
     pl.semaphore_wait(barrier, 3)
 
     def o_copy(half, row):
@@ -496,22 +506,17 @@
                 prod = jnp.dot(lhs, w[k, :, b * width:(b + 1) * width], preferred_element_type=F32)
                 z[b, half] = z[b, half] + prod.reshape(z.shape[2:])
 
-    first = (num_c - N2 + 1) // 2
-    for i in range(N2, N2 + first):
+    @pl.loop(n2, num_c)
+    def _(i):
         x_send(i).start()
+
     o_copy(yn, yi).start()
-    unread = list(range(num_k))
-
-    def read_weights(count):
-        for k in unread[:count]:
-            w_copy(k).start()
-        del unread[:count]
-
-    read_weights(2)
+    for k in range(num_k):
+        w_copy(k).start()
     z[...] = jnp.zeros_like(z)
 
     def start_here(i):
-        pltpu.make_async_copy(got_hbm.at[0], xr.at[i], x_r.at[i]).wait()
+        here_copy(got_hbm.at[0], i).wait()
         activate(i)
 
     pl.loop(0, FULL)(start_here)
@@ -519,33 +524,23 @@
     o_copy(yi, yn).wait_recv()
     send_own(1)
     send_own(0)
-    for i in range(N2 + first, num_c):
-        x_send(i).start()
-    read_weights(2)
-    pl.loop(FULL, N2)(start_here)
-    ready = sum(end <= N2 for end in starts[1:])
+    pl.loop(FULL, n2)(start_here)
+    ready = sum(end <= LOW + PERM for end in starts[1:])
     for n in range(ready):
         send_own(2 + n)
-    read_weights(2)
-    for i in range(N2, N2 + first):
+
+    @pl.loop(n2, num_c)
+    def _(i):
         x_send(i).wait_recv()
         activate(i)
-        read_weights(2)
-    pass_on(1)
-    read_weights(2)
-    arrived(1)
-    multiply(0, num_o)
-    read_weights(2)
-
-    for i in range(N2 + first, num_c):
-        x_send(i).wait_recv()
-        activate(i)
-        read_weights(2)
+
     groups = 2 + 2 * pieces
     for e in range(2 + ready, groups):
         send_own(e)
+    pass_on(1)
     pass_on(0)
-    read_weights(num_k)
+    arrived(1)
+    multiply(0, num_o)
     arrived(0)
     multiply(num_o, FULL)
     z_copies = [remote(z.at[yn, half], zr.at[half], z_s.at[half], z_r.at[half], yn_dev) for half in range(2)]
@@ -569,7 +564,7 @@
         to_sib(e, xi).wait_send()
         forward(e, xn).wait_send()
 
-    @pl.loop(N2, num_c)
+    @pl.loop(n2, num_c)
     def _(i):
         x_send(i).wait_send()
 
@@ -603,7 +598,7 @@
             pltpu.VMEM((2, 4, rows // 8, num_k * C), BF16),
             pltpu.VMEM((2, 2, 4, rows // 8, width), F32),
             pltpu.VMEM((2, 4, rows // 8, width), F32),
-            dma, dma((2,)), dma((num_k,)), dma((num_c,)), dma((num_c - N2,)), dma((num_c,)), dma, dma,
+            dma, dma((2,)), dma((num_k,)), dma((num_c,)), dma((num_c - LOW - PERM,)), dma((num_c,)), dma, dma,
             dma((groups,)), dma((groups,)), dma((groups,)), dma((groups,)), dma((groups,)), dma((groups,)),
             dma((2,)), dma((2,)),
         ],

time: 134 us -> 136 us (1.015)
  Pallas kernels: 123 us -> 126 us
    pallas_call x1, Pallas kernels: 50.3 us -> 54.8 us  [back(): pl.pallas_call(back_kernel, name='back', out_shape=jax.ShapeDtypeStruct((...]
    pallas_call x1, Pallas kernels: 44.5 us -> 42.4 us  [front(): pl.pallas_call(functools.partial(front_kernel, d_model), name='front', ou...]
where the time goes in v10:
time: 136 us
  Pallas kernels  126 us (93%)
  other arithmetic  3.33 us (2%)
  local copies, waits for them, and re-layouts  2.77 us (2%)
  waiting for transfers between devices  2.43 us (2%)
    pallas_call x1, Pallas kernels, back(): pl.pallas_call(back_kernel, name='back', out_shape=jax.ShapeDtypeStruct((...  54.8 us
    pallas_call x1, Pallas kernels, front(): pl.pallas_call(functools.partial(front_kernel, d_model), name='front', ou...  42.4 us
    pallas_call x1, Pallas kernels, attend(): pl.pallas_call(attend_kernel, name='attend', grid_spec=pltpu.PrefetchScal...  28.3 us
  transfers between devices with their start and end apart: 1, of which 1 were waited for; matrix products, arithmetic and copies ran while one was open for 3% of the time, Pallas kernels for 21%

profile of v10, /device:TPU:0, one launch (start us, length us, event | category | flops | bytes accessed | tf_op | source)
XLA Modules:
  0.0 135.9 jit_solution(13861141553652428706)
XLA Ops:
  0.6 0.0 copy-start
  0.6 42.4 %front.1 = (bf16[2,16,3200]{2,1,0:T(8,128)(2,1)}, f32[6,32,1536]{2,1,0:T(8,128)}, f32[8,32,1536]{2,1,0:T(8,128)}, f32[4,32,1536]{2,1,0:T(8,128)}, f32[16,32,1536]{2,1,0:T(8,128)}) custom-call(bf16[2,64,768]{2,1,0:T(8,128)(2,1)} %bitcast.13, bf16[768]{0:T(1024)(128)(2,1)} %g_hbm.1, bf16[1536,3200]{1,0:T(8,128)(2,1)} %wq_hbm.1, bf16[1536,12288]{1,0:T(8,128)(2,1)} %wg_hbm.1, ...), custom_call_target="tpu_custom_call" | custom-call | flops 10921967616 | bytes 85327872 | tf_op jit(solution)/shard_map/front/pallas_call | solution.py:291
  43.0 1.1 collective-permute-start
  44.1 0.0 copy-done
  44.2 1.0 fusion.2
  45.1 0.1 concatenate.14
  45.2 0.1 concatenate.15
  45.3 0.1 fusion.1
  45.4 0.8 pad_maximum_fusion.qkv_ref
  46.2 0.7 pad_maximum_fusion.1
  46.8 28.3 %attend.1 = (bf16[16,4096,128]{2,1,0:T(8,128)(2,1)}, bf16[16,4096,128]{2,1,0:T(8,128)(2,1)}, bf16[16,48,128]{2,1,0:T(8,128)(2,1)}) custom-call(s32[16]{0:T(128)} %len_ref.1, bf16[16,50,128]{2,1,0:T(8,128)(2,1)} %pad_maximum_fusion.qkv_ref, f32[16,1,128]{2,1,0:T(1,128)} %bitcast.14, f32[16,1,128]{2,1,0:T(1,128)} %bitcast.15, bf16[16,4096,128]{2,1,0:T(8,128)(2,1)} %k_ref.1, ...), custom_call_target="tpu_custom_call" | custom-call | flops 25769803776 | bytes 67108864 | tf_op jit(solution)/shard_map/attend/pallas_call | solution.py:362
  75.2 1.0 reshape.28
  76.2 0.7 copy.17
  76.9 2.4 %collective-permute-done.perm_hbm = f32[8,32,1536]{2,1,0:T(8,128)} collective-permute-done((f32[8,32,1536]{2,1,0:T(8,128)}, f32[8,32,1536]{2,1,0:T(8,128)}, u32[]{:S(2)}, u32[]{:S(2)}) %collective-permute-start) | collective-permute-done | bytes 1572896 | tf_op jit(solution)/shard_map/ppermute | solution.py:636
  79.3 54.8 %back.1 = f32[4,2,16,768]{3,2,1,0:T(8,128)} custom-call(bf16[2,16,3072]{2,1,0:T(8,128)(2,1)} %bitcast.12, f32[16,32,1536]{2,1,0:T(8,128)} %get-tuple-element.13.own_hbm, f32[6,32,1536]{2,1,0:T(8,128)} %get-tuple-element.14.got_hbm, f32[8,32,1536]{2,1,0:T(8,128)} %collective-permute-done.perm_hbm, f32[4,32,1536]{2,1,0:T(8,128)} %get-tuple-element.16.send_hbm, ...), custom_call_target="tpu_custom_call" | custom-call | flops 6039797760 | bytes 47185920 | tf_op jit(solution)/shard_map/back/pallas_call | solution.py:588
  134.1 1.8 %fusion = bf16[128,768]{1,0:T(8,128)(2,1)} fusion(f32[4,2,16,768]{3,2,1,0:T(8,128)} %back.1, bf16[128,768]{1,0:T(8,128)(2,1)} %param.10), kind=kLoop, calls=%fused_computation.1 | loop fusion | flops 294912 | bytes 786432 | tf_op jit(solution)/shard_map/convert_element_type | solution.py:610
  (2 shorter events, 0.0 us)
Async XLA Ops:
  0.6 43.5 %copy-start = (s32[16]{0:T(128)S(1)}, s32[16]{0:T(128)}, u32[]{:S(2)}) copy-start(s32[16]{0:T(128)} %len_ref.1) | copy-start | bytes 196
  43.0 36.3 %collective-permute-start = (f32[8,32,1536]{2,1,0:T(8,128)}, f32[8,32,1536]{2,1,0:T(8,128)}, u32[]{:S(2)}, u32[]{:S(2)}) collective-permute-start(f32[8,32,1536]{2,1,0:T(8,128)} %get-tuple-element.15), channel_id=1, source_target_pairs={{0,2},{1,3},{2,0},{3,1},{4,6},{5,7},{6,4},{7,5}} | collective-permute-start | bytes 4718600 | tf_op jit(solution)/shard_map/ppermute | solution.py:636

commit v11 on v10

--- a/solution.py
+++ b/solution.py
@@ -16,9 +16,9 @@
 CQ = 640
 PER_STEP = 2
 SLOTS = 3
-LOW, SHIFT, PERM = 4, 2, 8
+LOW, SHIFT, PERM = 5, 1, 8
 FULL = 5
-PIECES = (7, 4)
+PIECES = (8, 3)
 
 
 def remote(src, dst, send_sem, recv_sem, device):
@@ -506,12 +506,14 @@
                 prod = jnp.dot(lhs, w[k, :, b * width:(b + 1) * width], preferred_element_type=F32)
                 z[b, half] = z[b, half] + prod.reshape(z.shape[2:])
 
-    @pl.loop(n2, num_c)
+    middle = num_c - 1
+
+    @pl.loop(n2, middle)
     def _(i):
         x_send(i).start()
 
     o_copy(yn, yi).start()
-    for k in range(num_k):
+    for k in range(num_o):
         w_copy(k).start()
     z[...] = jnp.zeros_like(z)
 
@@ -524,23 +526,28 @@
     o_copy(yi, yn).wait_recv()
     send_own(1)
     send_own(0)
+    x_send(middle).start()
+    for k in range(num_o, num_k):
+        w_copy(k).start()
     pl.loop(FULL, n2)(start_here)
     ready = sum(end <= LOW + PERM for end in starts[1:])
     for n in range(ready):
         send_own(2 + n)
 
-    @pl.loop(n2, num_c)
+    @pl.loop(n2, middle)
     def _(i):
         x_send(i).wait_recv()
         activate(i)
 
+    pass_on(1)
+    arrived(1)
+    multiply(0, num_o)
+    pass_on(0)
+    x_send(middle).wait_recv()
+    activate(middle)
     groups = 2 + 2 * pieces
     for e in range(2 + ready, groups):
         send_own(e)
-    pass_on(1)
-    pass_on(0)
-    arrived(1)
-    multiply(0, num_o)
     arrived(0)
     multiply(num_o, FULL)
     z_copies = [remote(z.at[yn, half], zr.at[half], z_s.at[half], z_r.at[half], yn_dev) for half in range(2)]

time: 136 us -> 134 us (0.985)
  Pallas kernels: 126 us -> 123 us
    pallas_call x1, Pallas kernels: 54.8 us -> 50 us  [back(): pl.pallas_call(back_kernel, name='back', out_shape=jax.ShapeDtypeStruct((...]
    pallas_call x1, Pallas kernels: 42.4 us -> 44.9 us  [front(): pl.pallas_call(functools.partial(front_kernel, d_model), name='front', ou...]
where the time goes in v11:
time: 134 us
  Pallas kernels  123 us (92%)
  other arithmetic  3.35 us (2%)
  waiting for transfers between devices  2.98 us (2%)
  local copies, waits for them, and re-layouts  2.77 us (2%)
    pallas_call x1, Pallas kernels, back(): pl.pallas_call(back_kernel, name='back', out_shape=jax.ShapeDtypeStruct((...  50 us
    pallas_call x1, Pallas kernels, front(): pl.pallas_call(functools.partial(front_kernel, d_model), name='front', ou...  44.9 us
    pallas_call x1, Pallas kernels, attend(): pl.pallas_call(attend_kernel, name='attend', grid_spec=pltpu.PrefetchScal...  28.3 us
    ppermute x1, waiting for transfers between devices, local_layer(): perm = lax.ppermute(perm, 'x', across)  2.98 us
  transfers between devices with their start and end apart: 1, of which 1 were waited for; matrix products, arithmetic and copies ran while one was open for 3% of the time, Pallas kernels for 21%

profile of v11, /device:TPU:0, one launch (start us, length us, event | category | flops | bytes accessed | tf_op | source)
XLA Modules:
  0.0 134.0 jit_solution(13502879099322135353)
XLA Ops:
  0.6 0.0 copy-start
  0.6 44.9 %front.1 = (bf16[2,16,3200]{2,1,0:T(8,128)(2,1)}, f32[6,32,1536]{2,1,0:T(8,128)}, f32[8,32,1536]{2,1,0:T(8,128)}, f32[3,32,1536]{2,1,0:T(8,128)}, f32[16,32,1536]{2,1,0:T(8,128)}) custom-call(bf16[2,64,768]{2,1,0:T(8,128)(2,1)} %bitcast.13, bf16[768]{0:T(1024)(128)(2,1)} %g_hbm.1, bf16[1536,3200]{1,0:T(8,128)(2,1)} %wq_hbm.1, bf16[1536,12288]{1,0:T(8,128)(2,1)} %wg_hbm.1, ...), custom_call_target="tpu_custom_call" | custom-call | flops 10921967616 | bytes 85327872 | tf_op jit(solution)/shard_map/front/pallas_call | solution.py:291
  45.5 1.0 collective-permute-start
  46.5 0.0 copy-done
  46.5 1.0 fusion.2
  47.5 0.1 concatenate.14
  47.5 0.1 concatenate.15
  47.6 0.1 fusion.1
  47.7 0.8 pad_maximum_fusion.qkv_ref
  48.5 0.7 pad_maximum_fusion.1
  49.2 28.3 %attend.1 = (bf16[16,4096,128]{2,1,0:T(8,128)(2,1)}, bf16[16,4096,128]{2,1,0:T(8,128)(2,1)}, bf16[16,48,128]{2,1,0:T(8,128)(2,1)}) custom-call(s32[16]{0:T(128)} %len_ref.1, bf16[16,50,128]{2,1,0:T(8,128)(2,1)} %pad_maximum_fusion.qkv_ref, f32[16,1,128]{2,1,0:T(1,128)} %bitcast.14, f32[16,1,128]{2,1,0:T(1,128)} %bitcast.15, bf16[16,4096,128]{2,1,0:T(8,128)(2,1)} %k_ref.1, ...), custom_call_target="tpu_custom_call" | custom-call | flops 25769803776 | bytes 67108864 | tf_op jit(solution)/shard_map/attend/pallas_call | solution.py:362
  77.5 1.0 reshape.28
  78.5 0.7 copy.17
  79.2 3.0 %collective-permute-done.perm_hbm = f32[8,32,1536]{2,1,0:T(8,128)} collective-permute-done((f32[8,32,1536]{2,1,0:T(8,128)}, f32[8,32,1536]{2,1,0:T(8,128)}, u32[]{:S(2)}, u32[]{:S(2)}) %collective-permute-start) | collective-permute-done | bytes 1572896 | tf_op jit(solution)/shard_map/ppermute | solution.py:643
  82.2 50.0 %back.1 = f32[4,2,16,768]{3,2,1,0:T(8,128)} custom-call(bf16[2,16,3072]{2,1,0:T(8,128)(2,1)} %bitcast.12, f32[16,32,1536]{2,1,0:T(8,128)} %get-tuple-element.13.own_hbm, f32[6,32,1536]{2,1,0:T(8,128)} %get-tuple-element.14.got_hbm, f32[8,32,1536]{2,1,0:T(8,128)} %collective-permute-done.perm_hbm, f32[3,32,1536]{2,1,0:T(8,128)} %get-tuple-element.16.send_hbm, ...), custom_call_target="tpu_custom_call" | custom-call | flops 6039797760 | bytes 47185920 | tf_op jit(solution)/shard_map/back/pallas_call | solution.py:595
  132.3 1.8 %fusion = bf16[128,768]{1,0:T(8,128)(2,1)} fusion(f32[4,2,16,768]{3,2,1,0:T(8,128)} %back.1, bf16[128,768]{1,0:T(8,128)(2,1)} %param.10), kind=kLoop, calls=%fused_computation.1 | loop fusion | flops 294912 | bytes 786432 | tf_op jit(solution)/shard_map/convert_element_type | solution.py:617
  (2 shorter events, 0.0 us)
Async XLA Ops:
  0.6 45.9 %copy-start = (s32[16]{0:T(128)S(1)}, s32[16]{0:T(128)}, u32[]{:S(2)}) copy-start(s32[16]{0:T(128)} %len_ref.1) | copy-start | bytes 196
  45.5 36.7 %collective-permute-start = (f32[8,32,1536]{2,1,0:T(8,128)}, f32[8,32,1536]{2,1,0:T(8,128)}, u32[]{:S(2)}, u32[]{:S(2)}) collective-permute-start(f32[8,32,1536]{2,1,0:T(8,128)} %get-tuple-element.15), channel_id=1, source_target_pairs={{0,2},{1,3},{2,0},{3,1},{4,6},{5,7},{6,4},{7,5}} | collective-permute-start | bytes 4718600 | tf_op jit(solution)/shard_map/ppermute | solution.py:643

commit v12 on v11

--- a/solution.py
+++ b/solution.py
@@ -16,7 +16,7 @@
 CQ = 640
 PER_STEP = 2
 SLOTS = 3
-LOW, SHIFT, PERM = 5, 1, 8
+LOW, SHIFT, PERM = 5, 0, 8
 FULL = 5
 PIECES = (8, 3)
 
@@ -421,10 +421,6 @@
     o_in = pltpu.make_async_copy(o_hbm.at[yi], act.at[yi, xi, :, 0:o_cols], in_sem)
     o_in.start()
 
-    @pl.loop(0, num_c)
-    def _(i):
-        own_copy(i).start()
-
     @pl.loop(0, n1)
     def _(i):
         here_copy(got_hbm.at[i], i).start()
@@ -513,6 +509,11 @@
         x_send(i).start()
 
     o_copy(yn, yi).start()
+
+    @pl.loop(0, num_c)
+    def _(i):
+        own_copy(i).start()
+
     for k in range(num_o):
         w_copy(k).start()
     z[...] = jnp.zeros_like(z)
@@ -525,8 +526,8 @@
     o_in.wait()
     o_copy(yi, yn).wait_recv()
     send_own(1)
+    x_send(middle).start()
     send_own(0)
-    x_send(middle).start()
     for k in range(num_o, num_k):
         w_copy(k).start()
     pl.loop(FULL, n2)(start_here)
@@ -542,12 +543,12 @@
     pass_on(1)
     arrived(1)
     multiply(0, num_o)
-    pass_on(0)
     x_send(middle).wait_recv()
     activate(middle)
     groups = 2 + 2 * pieces
     for e in range(2 + ready, groups):
         send_own(e)
+    pass_on(0)
     arrived(0)
     multiply(num_o, FULL)
     z_copies = [remote(z.at[yn, half], zr.at[half], z_s.at[half], z_r.at[half], yn_dev) for half in range(2)]

time: 134 us -> 134 us (level)
  no operation moved by 1% of the time
where the time goes in v12:
time: 134 us; the launch traced here: 133 us
  Pallas kernels  123 us (92%)
  other arithmetic  3.31 us (2%)
  local copies, waits for them, and re-layouts  2.77 us (2%)
  waiting for transfers between devices  2.55 us (2%)
    pallas_call x1, Pallas kernels, back(): pl.pallas_call(back_kernel, name='back', out_shape=jax.ShapeDtypeStruct((...  50.3 us
    pallas_call x1, Pallas kernels, front(): pl.pallas_call(functools.partial(front_kernel, d_model), name='front', ou...  44.5 us
    pallas_call x1, Pallas kernels, attend(): pl.pallas_call(attend_kernel, name='attend', grid_spec=pltpu.PrefetchScal...  28.3 us
  transfers between devices with their start and end apart: 1, of which 1 were waited for; matrix products, arithmetic and copies ran while one was open for 3% of the time, Pallas kernels for 21%

profile of v12, /device:TPU:0, one launch (start us, length us, event | category | flops | bytes accessed | tf_op | source)
XLA Modules:
  0.0 133.4 jit_solution(14356119543046738617)
XLA Ops:
  0.6 0.0 copy-start
  0.6 44.5 %front.1 = (bf16[2,16,3200]{2,1,0:T(8,128)(2,1)}, f32[5,32,1536]{2,1,0:T(8,128)}, f32[8,32,1536]{2,1,0:T(8,128)}, f32[3,32,1536]{2,1,0:T(8,128)}, f32[16,32,1536]{2,1,0:T(8,128)}) custom-call(bf16[2,64,768]{2,1,0:T(8,128)(2,1)} %bitcast.13, bf16[768]{0:T(1024)(128)(2,1)} %g_hbm.1, bf16[1536,3200]{1,0:T(8,128)(2,1)} %wq_hbm.1, bf16[1536,12288]{1,0:T(8,128)(2,1)} %wg_hbm.1, ...), custom_call_target="tpu_custom_call" | custom-call | flops 10921967616 | bytes 85327872 | tf_op jit(solution)/shard_map/front/pallas_call | solution.py:291
  45.2 1.0 collective-permute-start
  46.1 0.0 copy-done
  46.2 1.0 fusion.2
  47.1 0.1 concatenate.14
  47.2 0.1 concatenate.15
  47.3 0.1 fusion.1
  47.4 0.7 pad_maximum_fusion.qkv_ref
  48.1 0.7 pad_maximum_fusion.1
  48.8 28.3 %attend.1 = (bf16[16,4096,128]{2,1,0:T(8,128)(2,1)}, bf16[16,4096,128]{2,1,0:T(8,128)(2,1)}, bf16[16,48,128]{2,1,0:T(8,128)(2,1)}) custom-call(s32[16]{0:T(128)} %len_ref.1, bf16[16,50,128]{2,1,0:T(8,128)(2,1)} %pad_maximum_fusion.qkv_ref, f32[16,1,128]{2,1,0:T(1,128)} %bitcast.14, f32[16,1,128]{2,1,0:T(1,128)} %bitcast.15, bf16[16,4096,128]{2,1,0:T(8,128)(2,1)} %k_ref.1, ...), custom_call_target="tpu_custom_call" | custom-call | flops 25769803776 | bytes 67108864 | tf_op jit(solution)/shard_map/attend/pallas_call | solution.py:362
  77.1 1.0 reshape.28
  78.1 0.7 copy.17
  78.8 2.6 %collective-permute-done.perm_hbm = f32[8,32,1536]{2,1,0:T(8,128)} collective-permute-done((f32[8,32,1536]{2,1,0:T(8,128)}, f32[8,32,1536]{2,1,0:T(8,128)}, u32[]{:S(2)}, u32[]{:S(2)}) %collective-permute-start) | collective-permute-done | bytes 1572896 | tf_op jit(solution)/shard_map/ppermute | solution.py:644
  81.4 50.3 %back.1 = f32[4,2,16,768]{3,2,1,0:T(8,128)} custom-call(bf16[2,16,3072]{2,1,0:T(8,128)(2,1)} %bitcast.12, f32[16,32,1536]{2,1,0:T(8,128)} %get-tuple-element.13.own_hbm, f32[5,32,1536]{2,1,0:T(8,128)} %get-tuple-element.14.got_hbm, f32[8,32,1536]{2,1,0:T(8,128)} %collective-permute-done.perm_hbm, f32[3,32,1536]{2,1,0:T(8,128)} %get-tuple-element.16.send_hbm, ...), custom_call_target="tpu_custom_call" | custom-call | flops 6039797760 | bytes 47185920 | tf_op jit(solution)/shard_map/back/pallas_call | solution.py:596
  131.7 1.8 %fusion = bf16[128,768]{1,0:T(8,128)(2,1)} fusion(f32[4,2,16,768]{3,2,1,0:T(8,128)} %back.1, bf16[128,768]{1,0:T(8,128)(2,1)} %param.10), kind=kLoop, calls=%fused_computation.1 | loop fusion | flops 294912 | bytes 786432 | tf_op jit(solution)/shard_map/convert_element_type | solution.py:618
  (2 shorter events, 0.0 us)
Async XLA Ops:
  0.6 45.5 %copy-start = (s32[16]{0:T(128)S(1)}, s32[16]{0:T(128)}, u32[]{:S(2)}) copy-start(s32[16]{0:T(128)} %len_ref.1) | copy-start | bytes 196
  45.2 36.2 %collective-permute-start = (f32[8,32,1536]{2,1,0:T(8,128)}, f32[8,32,1536]{2,1,0:T(8,128)}, u32[]{:S(2)}, u32[]{:S(2)}) collective-permute-start(f32[8,32,1536]{2,1,0:T(8,128)} %get-tuple-element.15), channel_id=1, source_target_pairs={{0,2},{1,3},{2,0},{3,1},{4,6},{5,7},{6,4},{7,5}} | collective-permute-start | bytes 4718600 | tf_op jit(solution)/shard_map/ppermute | solution.py:644

commit v13 on v12

--- a/solution.py
+++ b/solution.py
@@ -412,8 +412,8 @@
     def here_copy(src, i):
         return pltpu.make_async_copy(src, xr.at[i], x_r.at[i])
 
-    def x_send(i):
-        return remote(send_hbm.at[i - n2], xr.at[i], x_s.at[i - n2], x_r.at[i], xn_dev)
+    late = num_c - LOW - PERM
+    x_send = remote(send_hbm, xr.at[pl.ds(n2, late)], x_s, x_r.at[n2], xn_dev)
 
     barrier = pltpu.get_barrier_semaphore()
     for dev in (sib_dev, xn_dev, yn_dev):
@@ -436,10 +436,8 @@
 
     def block_of(e, owner):
         if e == 0:
-            return act.at[:, owner, :, pl.ds(o_cols, FULL * C)]
-        if e == 1:
-            return act.at[:, owner, :, pl.ds(0, o_cols)]
-        half, n = divmod(e - 2, pieces)
+            return act.at[:, owner, :, pl.ds(0, o_cols + FULL * C)]
+        half, n = divmod(e - 1, pieces)
         return act.at[half, owner, :, pl.ds(o_cols + starts[n] * C, PIECES[n] * C)]
 
     def to_sib(e, owner):
@@ -502,12 +500,7 @@
                 prod = jnp.dot(lhs, w[k, :, b * width:(b + 1) * width], preferred_element_type=F32)
                 z[b, half] = z[b, half] + prod.reshape(z.shape[2:])
 
-    middle = num_c - 1
-
-    @pl.loop(n2, middle)
-    def _(i):
-        x_send(i).start()
-
+    x_send.start()
     o_copy(yn, yi).start()
 
     @pl.loop(0, num_c)
@@ -525,39 +518,29 @@
     pl.loop(0, FULL)(start_here)
     o_in.wait()
     o_copy(yi, yn).wait_recv()
-    send_own(1)
-    x_send(middle).start()
     send_own(0)
     for k in range(num_o, num_k):
         w_copy(k).start()
     pl.loop(FULL, n2)(start_here)
     ready = sum(end <= LOW + PERM for end in starts[1:])
     for n in range(ready):
-        send_own(2 + n)
-
-    @pl.loop(n2, middle)
-    def _(i):
-        x_send(i).wait_recv()
-        activate(i)
-
-    pass_on(1)
-    arrived(1)
-    multiply(0, num_o)
-    x_send(middle).wait_recv()
-    activate(middle)
-    groups = 2 + 2 * pieces
-    for e in range(2 + ready, groups):
+        send_own(1 + n)
+
+    x_send.wait_recv()
+    pl.loop(n2, num_c)(activate)
+    groups = 1 + 2 * pieces
+    for e in range(1 + ready, groups):
         send_own(e)
     pass_on(0)
     arrived(0)
-    multiply(num_o, FULL)
+    multiply(0, num_o + FULL)
     z_copies = [remote(z.at[yn, half], zr.at[half], z_s.at[half], z_r.at[half], yn_dev) for half in range(2)]
-    pass_on(2)
-    for e in range(2, groups):
+    pass_on(1)
+    for e in range(1, groups):
         if e + 1 < groups:
             pass_on(e + 1)
         arrived(e)
-        half, n = divmod(e - 2, pieces)
+        half, n = divmod(e - 1, pieces)
         if e + 1 < groups:
             multiply_half(half, n)
         else:
@@ -572,9 +555,7 @@
         to_sib(e, xi).wait_send()
         forward(e, xn).wait_send()
 
-    @pl.loop(n2, num_c)
-    def _(i):
-        x_send(i).wait_send()
+    x_send.wait_send()
 
     outs = [pltpu.make_async_copy(zr.at[half], z_out.at[:, half], out_sem.at[half]) for half in range(2)]
     for half in range(2):
@@ -589,7 +570,7 @@
     rows, width = x_loc.shape
     num_o, num_c = wao.shape[0] // C, wmo.shape[0] // C
     num_k = num_o + num_c
-    groups = 2 + 2 * len(PIECES)
+    groups = 1 + 2 * len(PIECES)
     quarter = rows // 4
     dma = pltpu.SemaphoreType.DMA
     any_spec = pl.BlockSpec(memory_space=pl.ANY)
@@ -606,7 +587,7 @@
             pltpu.VMEM((2, 4, rows // 8, num_k * C), BF16),
             pltpu.VMEM((2, 2, 4, rows // 8, width), F32),
             pltpu.VMEM((2, 4, rows // 8, width), F32),
-            dma, dma((2,)), dma((num_k,)), dma((num_c,)), dma((num_c - LOW - PERM,)), dma((num_c,)), dma, dma,
+            dma, dma((2,)), dma((num_k,)), dma((num_c,)), dma, dma((num_c,)), dma, dma,
             dma((groups,)), dma((groups,)), dma((groups,)), dma((groups,)), dma((groups,)), dma((groups,)),
             dma((2,)), dma((2,)),
         ],

time: 134 us -> 135 us (level)
  no operation moved by 1% of the time
where the time goes in v13:
time: 135 us
  Pallas kernels  124 us (92%)
  other arithmetic  3.31 us (2%)
  local copies, waits for them, and re-layouts  2.77 us (2%)
  waiting for transfers between devices  2.55 us (2%)
    pallas_call x1, Pallas kernels, back(): pl.pallas_call(back_kernel, name='back', out_shape=jax.ShapeDtypeStruct((...  51.4 us
    pallas_call x1, Pallas kernels, front(): pl.pallas_call(functools.partial(front_kernel, d_model), name='front', ou...  44.5 us
    pallas_call x1, Pallas kernels, attend(): pl.pallas_call(attend_kernel, name='attend', grid_spec=pltpu.PrefetchScal...  28.3 us
  transfers between devices with their start and end apart: 1, of which 1 were waited for; matrix products, arithmetic and copies ran while one was open for 3% of the time, Pallas kernels for 21%

profile of v13, /device:TPU:0, one launch (start us, length us, event | category | flops | bytes accessed | tf_op | source)
XLA Modules:
  0.0 134.6 jit_solution(266986874638945106)
XLA Ops:
  0.6 0.0 copy-start
  0.6 44.5 %front.1 = (bf16[2,16,3200]{2,1,0:T(8,128)(2,1)}, f32[5,32,1536]{2,1,0:T(8,128)}, f32[8,32,1536]{2,1,0:T(8,128)}, f32[3,32,1536]{2,1,0:T(8,128)}, f32[16,32,1536]{2,1,0:T(8,128)}) custom-call(bf16[2,64,768]{2,1,0:T(8,128)(2,1)} %bitcast.13, bf16[768]{0:T(1024)(128)(2,1)} %g_hbm.1, bf16[1536,3200]{1,0:T(8,128)(2,1)} %wq_hbm.1, bf16[1536,12288]{1,0:T(8,128)(2,1)} %wg_hbm.1, ...), custom_call_target="tpu_custom_call" | custom-call | flops 10921967616 | bytes 85327872 | tf_op jit(solution)/shard_map/front/pallas_call | solution.py:291
  45.2 1.0 collective-permute-start
  46.1 0.0 copy-done
  46.2 1.0 fusion.2
  47.1 0.1 concatenate.14
  47.2 0.1 concatenate.15
  47.3 0.1 fusion.1
  47.4 0.7 pad_maximum_fusion.qkv_ref
  48.1 0.7 pad_maximum_fusion.1
  48.8 28.3 %attend.1 = (bf16[16,4096,128]{2,1,0:T(8,128)(2,1)}, bf16[16,4096,128]{2,1,0:T(8,128)(2,1)}, bf16[16,48,128]{2,1,0:T(8,128)(2,1)}) custom-call(s32[16]{0:T(128)} %len_ref.1, bf16[16,50,128]{2,1,0:T(8,128)(2,1)} %pad_maximum_fusion.qkv_ref, f32[16,1,128]{2,1,0:T(1,128)} %bitcast.14, f32[16,1,128]{2,1,0:T(1,128)} %bitcast.15, bf16[16,4096,128]{2,1,0:T(8,128)(2,1)} %k_ref.1, ...), custom_call_target="tpu_custom_call" | custom-call | flops 25769803776 | bytes 67108864 | tf_op jit(solution)/shard_map/attend/pallas_call | solution.py:362
  77.1 1.0 reshape.28
  78.1 0.7 copy.17
  78.8 2.6 %collective-permute-done.perm_hbm = f32[8,32,1536]{2,1,0:T(8,128)} collective-permute-done((f32[8,32,1536]{2,1,0:T(8,128)}, f32[8,32,1536]{2,1,0:T(8,128)}, u32[]{:S(2)}, u32[]{:S(2)}) %collective-permute-start) | collective-permute-done | bytes 1572896 | tf_op jit(solution)/shard_map/ppermute | solution.py:625
  81.4 51.4 %back.1 = f32[4,2,16,768]{3,2,1,0:T(8,128)} custom-call(bf16[2,16,3072]{2,1,0:T(8,128)(2,1)} %bitcast.12, f32[16,32,1536]{2,1,0:T(8,128)} %get-tuple-element.13.own_hbm, f32[5,32,1536]{2,1,0:T(8,128)} %get-tuple-element.14.got_hbm, f32[8,32,1536]{2,1,0:T(8,128)} %collective-permute-done.perm_hbm, f32[3,32,1536]{2,1,0:T(8,128)} %get-tuple-element.16.send_hbm, ...), custom_call_target="tpu_custom_call" | custom-call | flops 6039797760 | bytes 47185920 | tf_op jit(solution)/shard_map/back/pallas_call | solution.py:577
  132.8 1.8 %fusion = bf16[128,768]{1,0:T(8,128)(2,1)} fusion(f32[4,2,16,768]{3,2,1,0:T(8,128)} %back.1, bf16[128,768]{1,0:T(8,128)(2,1)} %param.10), kind=kLoop, calls=%fused_computation.1 | loop fusion | flops 294912 | bytes 786432 | tf_op jit(solution)/shard_map/convert_element_type | solution.py:599
  (2 shorter events, 0.0 us)
Async XLA Ops:
  0.6 45.5 %copy-start = (s32[16]{0:T(128)S(1)}, s32[16]{0:T(128)}, u32[]{:S(2)}) copy-start(s32[16]{0:T(128)} %len_ref.1) | copy-start | bytes 196
  45.2 36.2 %collective-permute-start = (f32[8,32,1536]{2,1,0:T(8,128)}, f32[8,32,1536]{2,1,0:T(8,128)}, u32[]{:S(2)}, u32[]{:S(2)}) collective-permute-start(f32[8,32,1536]{2,1,0:T(8,128)} %get-tuple-element.15), channel_id=1, source_target_pairs={{0,2},{1,3},{2,0},{3,1},{4,6},{5,7},{6,4},{7,5}} | collective-permute-start | bytes 4718600 | tf_op jit(solution)/shard_map/ppermute | solution.py:625

commit v14 on v6

--- a/solution.py
+++ b/solution.py
@@ -18,7 +18,7 @@
 SLOTS = 3
 N1 = 5
 N2 = 13
-PIECES = (3, 3, 2, 2, 1)
+PIECES = (8, 3)
 
 
 def remote(src, dst, send_sem, recv_sem, device):

time: 133 us -> 135 us (1.015)
    pallas_call x1, Pallas kernels: 49.4 us -> 50.8 us  [back(): pl.pallas_call(back_kernel, name='back', out_shape=jax.ShapeDtypeStruct((...]
where the time goes in v14:
time: 135 us
  Pallas kernels  124 us (92%)
  other arithmetic  3.31 us (2%)
  local copies, waits for them, and re-layouts  2.77 us (2%)
  waiting for transfers between devices  2.45 us (2%)
    pallas_call x1, Pallas kernels, back(): pl.pallas_call(back_kernel, name='back', out_shape=jax.ShapeDtypeStruct((...  50.8 us
    pallas_call x1, Pallas kernels, front(): pl.pallas_call(functools.partial(front_kernel, d_model), name='front', ou...  45.3 us
    pallas_call x1, Pallas kernels, attend(): pl.pallas_call(attend_kernel, name='attend', grid_spec=pltpu.PrefetchScal...  28.3 us
  transfers between devices with their start and end apart: 1, of which 1 were waited for; matrix products, arithmetic and copies ran while one was open for 3% of the time, Pallas kernels for 21%

profile of v14, /device:TPU:0, one launch (start us, length us, event | category | flops | bytes accessed | tf_op | source)
XLA Modules:
  0.0 134.6 jit_solution(16941749636385601500)
XLA Ops:
  0.6 0.0 copy-start
  0.6 45.3 %front.1 = (bf16[2,16,3200]{2,1,0:T(8,128)(2,1)}, bf16[2,16,3840]{2,1,0:T(8,128)(2,1)}, f32[8,32,1536]{2,1,0:T(8,128)}, f32[3,32,1536]{2,1,0:T(8,128)}, f32[11,32,1536]{2,1,0:T(8,128)}) custom-call(bf16[2,64,768]{2,1,0:T(8,128)(2,1)} %bitcast.13, bf16[768]{0:T(1024)(128)(2,1)} %g_hbm.1, bf16[1536,3200]{1,0:T(8,128)(2,1)} %wq_hbm.1, ...), custom_call_target="tpu_custom_call" | custom-call | flops 10921967616 | bytes 85327872 | tf_op jit(solution)/shard_map/front/pallas_call | solution.py:298
  45.9 1.0 collective-permute-start
  46.9 0.0 copy-done
  46.9 1.0 fusion.2
  47.9 0.1 concatenate.14
  48.0 0.1 concatenate.15
  48.0 0.1 fusion.1
  48.1 0.7 pad_maximum_fusion.qkv_ref
  48.9 0.7 pad_maximum_fusion.1
  49.6 28.3 %attend.1 = (bf16[16,4096,128]{2,1,0:T(8,128)(2,1)}, bf16[16,4096,128]{2,1,0:T(8,128)(2,1)}, bf16[16,48,128]{2,1,0:T(8,128)(2,1)}) custom-call(s32[16]{0:T(128)} %len_ref.1, bf16[16,50,128]{2,1,0:T(8,128)(2,1)} %pad_maximum_fusion.qkv_ref, f32[16,1,128]{2,1,0:T(1,128)} %bitcast.14, f32[16,1,128]{2,1,0:T(1,128)} %bitcast.15, bf16[16,4096,128]{2,1,0:T(8,128)(2,1)} %k_ref.1, ...), custom_call_target="tpu_custom_call" | custom-call | flops 25769803776 | bytes 67108864 | tf_op jit(solution)/shard_map/attend/pallas_call | solution.py:371
  77.9 1.0 reshape.28
  78.9 0.7 copy.17
  79.6 2.4 %collective-permute-done.perm_hbm = f32[8,32,1536]{2,1,0:T(8,128)} collective-permute-done((f32[8,32,1536]{2,1,0:T(8,128)}, f32[8,32,1536]{2,1,0:T(8,128)}, u32[]{:S(2)}, u32[]{:S(2)}) %collective-permute-start) | collective-permute-done | bytes 1572896 | tf_op jit(solution)/shard_map/ppermute | solution.py:633
  82.0 50.8 %back.1 = f32[4,2,16,768]{3,2,1,0:T(8,128)} custom-call(bf16[2,16,3072]{2,1,0:T(8,128)(2,1)} %bitcast.12, bf16[2,16,3840]{2,1,0:T(8,128)(2,1)} %get-tuple-element.13.a1_hbm, f32[11,32,1536]{2,1,0:T(8,128)} %get-tuple-element.14.own_hbm, f32[8,32,1536]{2,1,0:T(8,128)} %collective-permute-done.perm_hbm, f32[3,32,1536]{2,1,0:T(8,128)} %get-tuple-element.16.send_hbm, ...), custom_call_target="tpu_custom_call" | custom-call | flops 6039797760 | bytes 47185920 | tf_op jit(solution)/shard_map/back/pallas_call | solution.py:585
  132.9 1.8 %fusion = bf16[128,768]{1,0:T(8,128)(2,1)} fusion(f32[4,2,16,768]{3,2,1,0:T(8,128)} %back.1, bf16[128,768]{1,0:T(8,128)(2,1)} %param.10), kind=kLoop, calls=%fused_computation.1 | loop fusion | flops 294912 | bytes 786432 | tf_op jit(solution)/shard_map/convert_element_type | solution.py:607
  (2 shorter events, 0.0 us)
Async XLA Ops:
  0.6 46.3 %copy-start = (s32[16]{0:T(128)S(1)}, s32[16]{0:T(128)}, u32[]{:S(2)}) copy-start(s32[16]{0:T(128)} %len_ref.1) | copy-start | bytes 196
  45.9 36.1 %collective-permute-start = (f32[8,32,1536]{2,1,0:T(8,128)}, f32[8,32,1536]{2,1,0:T(8,128)}, u32[]{:S(2)}, u32[]{:S(2)}) collective-permute-start(f32[8,32,1536]{2,1,0:T(8,128)} %get-tuple-element.15), channel_id=1, source_target_pairs={{0,2},{1,3},{2,0},{3,1},{4,6},{5,7},{6,4},{7,5}} | collective-permute-start | bytes 4718600 | tf_op jit(solution)/shard_map/ppermute | solution.py:633
